TPU v7x, 32 devices: a whole 2x2x4 slice. The times are simulated.
32 devices in a mesh: blk: 4 (over z), acc: 4 (over x, core), tail: 2 (over y).
Axes of the slice: x: 2, y: 2, z: 4, core: 2. Of those that a mesh axis runs over, the one named last changes fastest.
Arguments:
- reciprocal_spectra: float32 [4, 2, 64, 4096], P(None, None, 'acc'), may hold values from -6 to 6
- divisor: float32 [8, 131072], P(('blk', 'tail'), 'acc'), may hold values from -1 to 1
Outputs:
- middle_product: float32 [8, 131072], P(('blk', 'tail'), 'acc')
All inputs are finite; a program needn't handle non-finite values.
Results may differ from a plain program's by a relative error of at most 0.0003.
Values sent between devices are 32-bit elements; how exact they have to be, the bound alone decides.
No kernel may reach another device: no remote copies, remote signals or barrier semaphores. Data moves between devices by JAX's collectives and lax.ppermute only.
A program may use at most 64 MiB of HBM per device.

v0:
```python
import math

import jax
import jax.numpy as jnp
import numpy as np
from jax import lax
from jax.experimental import pallas as pl
from jax.experimental.pallas import tpu as pltpu
from jax.sharding import PartitionSpec as P


LANES = 128
EXTRA = 8
GRANT = 16 * 1024 * 1024
STRIDE = 2


class Plan:
    def __init__(self, freq_rows, plane, quarters, groups, rounds):
        self.rounds = rounds
        self.quarters = quarters
        self.groups = groups
        self.freq_rows = freq_rows
        self.radix = freq_rows * quarters
        self.length = self.radix * plane
        self.side = math.isqrt(self.length)
        self.half = self.side // 2
        self.m_los = self.side // self.radix
        self.m_his = self.radix // self.m_los
        self.rows = self.m_los * freq_rows
        self.n1s = self.side // 2
        self.chunk = self.n1s // quarters
        self.cols = self.side // LANES
        self.half_cols = self.half // LANES
        self.slice_rows = self.rows // groups
        self.per = groups // self.m_los
        self.packed = 2 * self.half_cols * self.slice_rows + EXTRA


def tables(plan):
    row = (np.arange(plan.m_los)[:, None] * plan.radix + np.arange(plan.freq_rows)[None, :]).reshape(-1)
    part = np.arange(plan.quarters) * plan.freq_rows
    n1 = np.arange(plan.n1s)
    n2 = np.arange(plan.side)
    f2 = (np.arange(plan.m_his)[:, None] + plan.m_los * np.arange(plan.radix // 2)[None, :]).reshape(-1)

    def wave(first, second, modulus):
        angle = (first[:, None] * second[None, :] % modulus) * (-2.0 * math.pi / modulus)
        return np.stack([np.cos(angle), np.sin(angle)])

    first_rows = wave(row, n1, plan.side)
    first_part = wave(part, n1, plan.side)
    twist_rows = wave(row, n2, plan.length)
    twist_part = wave(part, n2, plan.length)
    cosine, sine = wave(n2, f2, plan.side)
    second = np.concatenate([cosine, -sine], axis=1)
    second_high = second.astype(jnp.bfloat16)
    second_low = (second - second_high.astype(np.float64)).astype(jnp.bfloat16)
    single = lambda value: value.astype(np.float32)
    return (
        single(first_rows),
        single(first_part.transpose(1, 0, 2)),
        single(twist_rows),
        single(twist_part.transpose(1, 0, 2)),
        np.stack([second_high, second_low]),
    )


def far(value):
    return pltpu.with_memory_space_constraint(value, pltpu.HBM)


def split(value):
    high = value.astype(jnp.bfloat16)
    low = (value - high.astype(jnp.float32)).astype(jnp.bfloat16)
    return high, low


def product(first, second, transposed=False):
    dims = (((1,), (1 if transposed else 0,)), ((), ()))
    dot = lambda a, b: lax.dot_general(a, b, dims, preferred_element_type=jnp.float32)
    return dot(first[0], second[0]) + (dot(first[1], second[0]) + dot(first[0], second[1]))


def call(kernel, out_shape, memory, scratch=(), flops=1_000_000, moved=1_000_000):
    where = {"smem": pltpu.SMEM, "vmem": pltpu.VMEM, "hbm": pltpu.HBM}
    vmem = pl.BlockSpec(memory_space=pltpu.VMEM)
    return pl.pallas_call(
        kernel,
        out_shape=out_shape,
        in_specs=[pl.BlockSpec(memory_space=where[kind]) for kind in memory],
        out_specs=jax.tree.map(lambda _: vmem, out_shape),
        scratch_shapes=scratch,
        cost_estimate=pl.CostEstimate(flops=flops, bytes_accessed=moved, transcendentals=0),
        compiler_params=pltpu.CompilerParams(vmem_limit_bytes=GRANT),
    )


def fetch(plan, spectra, held, sems, m_lo):
    copies = []
    for m_hi in range(plan.m_his):
        start = pl.multiple_of((m_hi * plan.m_los + m_lo) * plan.radix // LANES * LANES, LANES)
        copies.append(pltpu.make_async_copy(spectra.at[:, :, pl.ds(start, LANES)], held.at[m_hi], sems.at[m_hi]))
        copies[-1].start()
    return copies


def gathered(plan, held, index, column, within, count):
    piece_lanes = plan.radix // 2
    each = LANES // piece_lanes
    lane = lax.broadcasted_iota(jnp.int32, (count, LANES), 1)
    value = jnp.zeros((count, LANES), jnp.float32)
    for piece in range(each):
        tile = held[column * each + piece, index, :count]
        turned = pltpu.roll(tile, (piece * piece_lanes - within + LANES) % LANES, 1)
        value = jnp.where((lane >= piece * piece_lanes) & (lane < (piece + 1) * piece_lanes), turned, value)
    return value


def held_scratch(plan):
    return [
        pltpu.VMEM((plan.m_his, 2 * plan.rounds, plan.freq_rows, LANES), jnp.float32),
        pltpu.SemaphoreType.DMA((plan.m_his,)),
    ]


def opposite(plan):
    def kernel(at, spectra, out, held, sems):
        m_lo = plan.m_los - 1 - at[1]
        for copy in fetch(plan, spectra, held, sems, m_lo):
            copy.wait()
        within = m_lo * plan.radix % LANES + plan.radix // 2
        for index in range(2 * plan.rounds):
            for column in range(plan.half_cols):
                out[index, :, column * LANES : (column + 1) * LANES] = gathered(
                    plan, held, index, column, within, plan.freq_rows
                )

    shape = jax.ShapeDtypeStruct((2 * plan.rounds, plan.freq_rows, plan.half), jnp.float32)
    return call(kernel, shape, ["smem", "hbm"], held_scratch(plan))


def prepare(plan):
    def kernel(at, *refs):
        first, twist, second, near = refs[6:10]
        first_rows, first_part, twist_rows, twist_part = refs[10:14]
        sems = refs[14]
        place = at[0]
        targets = (first_rows, first_part, twist_rows, twist_part, second, near)
        copies = [
            pltpu.make_async_copy(source, target, sems.at[index])
            for index, (source, target) in enumerate(zip(refs[:6], targets))
        ]
        for copy in copies:
            copy.start()
        copies[0].wait()
        copies[1].wait()
        part_cos = first_part[pl.ds(place, 1), 0, :]
        part_sin = first_part[pl.ds(place, 1), 1, :]
        rows = plan.rows
        first[0, :rows], first[1, :rows] = split(first_rows[0] * part_cos - first_rows[1] * part_sin)
        first[0, rows:], first[1, rows:] = split(first_rows[0] * part_sin + first_rows[1] * part_cos)
        copies[2].wait()
        copies[3].wait()
        part_cos = twist_part[pl.ds(place, 1), 0, :]
        part_sin = twist_part[pl.ds(place, 1), 1, :]
        twist[0] = twist_rows[0] * part_cos - twist_rows[1] * part_sin
        twist[1] = twist_rows[0] * part_sin + twist_rows[1] * part_cos
        copies[4].wait()
        copies[5].wait()

    shape = jax.ShapeDtypeStruct
    out_shape = (
        shape((2, 2 * plan.rows, plan.n1s), jnp.bfloat16),
        shape((2, plan.rows, plan.side), jnp.float32),
        shape((2, plan.side, 2 * plan.half), jnp.bfloat16),
        shape((plan.chunk * plan.cols, LANES), jnp.float32),
    )
    scratch = [
        pltpu.VMEM((2, plan.rows, plan.n1s), jnp.float32),
        pltpu.VMEM((plan.quarters, 2, plan.n1s), jnp.float32),
        pltpu.VMEM((2, plan.rows, plan.side), jnp.float32),
        pltpu.VMEM((plan.quarters, 2, plan.side), jnp.float32),
        pltpu.SemaphoreType.DMA((6,)),
    ]
    return call(kernel, out_shape, ["smem"] + ["hbm"] * 6, scratch)


def resident(plan):
    def kernel(at, first, spectra, last, own, own_real, own_imag, held, sems):
        m_lo = at[1]
        copies = fetch(plan, spectra, held, sems, m_lo)
        last[0], last[1] = split((first[0].astype(jnp.float32) + first[1].astype(jnp.float32)).T)
        for copy in copies:
            copy.wait()
        within = m_lo * plan.radix % LANES
        kept = at[3].astype(jnp.float32) / plan.length
        for index in range(2 * plan.rounds):
            step, imaginary = divmod(index, 2)
            for column in range(plan.half_cols):
                own[index, column] = gathered(plan, held, index, column, within, plan.freq_rows)
                upper = gathered(plan, held, index, column, within + plan.radix // 2, 1) * kept
                for turn in range(EXTRA // plan.half_cols):
                    row = turn * plan.half_cols + column
                    if imaginary:
                        own_imag[step, row : row + 1] = upper if turn % 2 else -upper
                    else:
                        own_real[step, row : row + 1] = upper

    shape = jax.ShapeDtypeStruct
    out_shape = (
        shape((2, plan.n1s, 2 * plan.rows), jnp.bfloat16),
        shape((2 * plan.rounds, plan.half_cols, plan.freq_rows, LANES), jnp.float32),
        shape((plan.rounds, EXTRA, LANES), jnp.float32),
        shape((plan.rounds, EXTRA, LANES), jnp.float32),
    )
    return call(kernel, out_shape, ["smem", "vmem", "hbm"], held_scratch(plan))


def blend(plan):
    def kernel(own, arrived, out):
        count = 2 * plan.rounds * plan.freq_rows
        row = lax.broadcasted_iota(jnp.int32, (count, count), 0)
        column = lax.broadcasted_iota(jnp.int32, (count, count), 1)
        within = row % plan.freq_rows
        turn = (row + column == 2 * (row - within) + plan.freq_rows) & (within != 0)
        turn = jnp.where(turn, 1.0, 0.0).astype(jnp.bfloat16)
        row = lax.broadcasted_iota(jnp.int32, (plan.half, plan.half), 0)
        column = lax.broadcasted_iota(jnp.int32, (plan.half, plan.half), 1)
        flip = jnp.where(row + column == plan.half - 1, 1.0, 0.0).astype(jnp.bfloat16)
        total = None
        for value in split(arrived[...].reshape(count, plan.half)):
            turned = jnp.dot(turn, value, preferred_element_type=jnp.float32).astype(jnp.bfloat16)
            turned = jnp.dot(turned, flip, preferred_element_type=jnp.float32)
            total = turned if total is None else total + turned
        scale = 1.0 / plan.length
        for index in range(2 * plan.rounds):
            sign = -1.0 if index % 2 else 1.0
            for column in range(plan.half_cols):
                there = total[
                    index * plan.freq_rows : (index + 1) * plan.freq_rows, column * LANES : (column + 1) * LANES
                ]
                out[index, column] = (own[index, column] + sign * there) * scale

    shape = jax.ShapeDtypeStruct((2 * plan.rounds, plan.half_cols, plan.freq_rows, LANES), jnp.float32)
    return call(kernel, shape, ["vmem"] * 2)


def alternating(plan, count):
    lane = lax.broadcasted_iota(jnp.int32, (count, plan.side), 1)
    return jnp.where(lane % 2 == 0, 1.0, -1.0)


def packed_rows(plan, part, column):
    start = (part * plan.half_cols + column) * plan.slice_rows
    return slice(start, start + plan.slice_rows)


def forward(plan):
    def kernel(at, *refs):
        limbs = refs[: plan.quarters]
        first, twist, second, out, matrix, turned = refs[plan.quarters :]
        place = at[0]
        for index in range(plan.quarters):
            start = pl.multiple_of((place ^ index) * plan.chunk, 8)
            for column in range(plan.cols):
                matrix[pl.ds(start, plan.chunk), column * LANES : (column + 1) * LANES] = limbs[index][
                    pl.ds(column, plan.chunk, stride=plan.cols), :
                ]
        value = product((first[0], first[1]), split(matrix[...]))
        rows, whole, few = plan.rows, 2 * plan.rows, plan.m_los
        real, imag = value[:rows], value[rows:]
        turned[:rows] = real * twist[0] - imag * twist[1]
        turned[rows:whole] = real * twist[1] + imag * twist[0]
        sign = alternating(plan, 1)
        for part in range(2):
            for m_lo in range(few):
                row, start = part * rows + m_lo * plan.freq_rows, whole + part * few + m_lo
                turned[start : start + 1] = turned[row : row + 1] * sign
        value = product(split(turned[...]), (second[0], second[1]))
        by_cos, by_sin = value[:, : plan.half], value[:, plan.half :]
        main = (by_cos[:rows] + by_sin[rows:whole], by_cos[rows:whole] - by_sin[:rows])
        extra = (by_cos[whole : whole + few] + by_sin[whole + few :], by_cos[whole + few :] - by_sin[whole : whole + few])
        base = plan.packed - EXTRA
        for group in range(plan.groups):
            for part in range(2):
                for column in range(plan.half_cols):
                    lanes = slice(column * LANES, (column + 1) * LANES)
                    out[group, packed_rows(plan, part, column)] = main[part][
                        group * plan.slice_rows : (group + 1) * plan.slice_rows, lanes
                    ]
                    m_lo = group // plan.per
                    for turn in range(EXTRA // (2 * plan.half_cols)):
                        row = base + (turn * 2 + part) * plan.half_cols + column
                        out[group, row : row + 1] = extra[part][m_lo : m_lo + 1, lanes]

    shape = jax.ShapeDtypeStruct((plan.groups, plan.packed, LANES), jnp.float32)
    scratch = [
        pltpu.VMEM((plan.n1s, plan.side), jnp.float32),
        pltpu.VMEM((2 * plan.rows + 2 * plan.m_los, plan.side), jnp.float32),
    ]
    return call(kernel, shape, ["smem"] + ["vmem"] * (plan.quarters + 3), scratch)


def combine(plan):
    def kernel(at, spectra, own, own_real, own_imag, out):
        row = lax.broadcasted_iota(jnp.int32, (plan.slice_rows, LANES), 0) + at[2]
        sign = jnp.where(row % 2 == 0, 1.0, -1.0)
        row = lax.broadcasted_iota(jnp.int32, (EXTRA, LANES), 0) * 0 + at[0] * plan.freq_rows
        extra_sign = jnp.where(row % 2 == 0, 1.0, -1.0)
        base = plan.packed - EXTRA

        def one_block(block, carry):
            sums = [jnp.zeros((plan.slice_rows, LANES), jnp.float32) for _ in range(2 * plan.half_cols)]
            extra = jnp.zeros((EXTRA, LANES), jnp.float32)
            for step in range(plan.rounds):
                here = lax.rem(block + (plan.rounds * STRIDE * plan.groups - step * STRIDE), plan.groups)
                before = lax.rem(here + (plan.groups - 1), plan.groups)
                for column in range(plan.half_cols):
                    real, imag = (
                        spectra[here, packed_rows(plan, part, column)]
                        + sign * spectra[before, packed_rows(plan, part, column)]
                        for part in range(2)
                    )
                    own_r, own_i = own[2 * step, column], own[2 * step + 1, column]
                    sums[column] = sums[column] + own_r * real - own_i * imag
                    sums[plan.half_cols + column] = sums[plan.half_cols + column] + own_r * imag + own_i * real
                both = spectra[here, base:] + extra_sign * spectra[before, base:]
                extra = extra + own_real[step] * both + own_imag[step] * pltpu.roll(both, plan.half_cols, 0)
            for part in range(2):
                for column in range(plan.half_cols):
                    out[block, packed_rows(plan, part, column)] = sums[part * plan.half_cols + column]
            out[block, base:] = extra
            return carry

        lax.fori_loop(0, plan.groups, one_block, 0)

    shape = jax.ShapeDtypeStruct((plan.groups, plan.packed, LANES), jnp.float32)
    return call(kernel, shape, ["smem"] + ["vmem"] * 4)


def backward(plan):
    def kernel(at, spectra, last, twist, second, out, stack, spread, matrix):
        place = at[0]
        rows, whole, few = plan.rows, 2 * plan.rows, plan.m_los
        base = plan.packed - EXTRA
        for part in range(2):
            for column in range(plan.half_cols):
                lanes = slice(column * LANES, (column + 1) * LANES)
                for group in range(plan.groups):
                    start = part * rows + group * plan.slice_rows
                    stack[start : start + plan.slice_rows, lanes] = spectra[group, packed_rows(plan, part, column)]
                for m_lo in range(few):
                    row = base + part * plan.half_cols + column
                    start = whole + part * few + m_lo
                    stack[start : start + 1, lanes] = spectra[m_lo * plan.per, row : row + 1]
        value = split(stack[...])
        by_cos = product(value, (second[0, :, : plan.half], second[1, :, : plan.half]), True)
        by_sin = product(value, (second[0, :, plan.half :], second[1, :, plan.half :]), True)
        spread[:rows] = by_cos[:rows] - by_sin[rows:whole]
        spread[rows:] = by_cos[rows:whole] + by_sin[:rows]
        sign = alternating(plan, few)
        extra = (
            (by_cos[whole : whole + few] - by_sin[whole + few :]) * sign,
            (by_cos[whole + few :] + by_sin[whole : whole + few]) * sign,
        )
        for part in range(2):
            for m_lo in range(few):
                row = part * rows + m_lo * plan.freq_rows
                spread[row : row + 1] = spread[row : row + 1] + extra[part][m_lo : m_lo + 1]
        real, imag = spread[:rows], spread[rows:]
        turned = jnp.concatenate([real * twist[0] + imag * twist[1], imag * twist[0] - real * twist[1]], axis=0)
        matrix[...] = product((last[0], last[1]), split(turned))
        for index in range(plan.quarters):
            start = pl.multiple_of((place ^ index) * plan.chunk, 8)
            for column in range(plan.cols):
                out[index, pl.ds(column, plan.chunk, stride=plan.cols), :] = matrix[
                    pl.ds(start, plan.chunk), column * LANES : (column + 1) * LANES
                ]

    shape = jax.ShapeDtypeStruct((plan.quarters, plan.chunk * plan.cols, LANES), jnp.float32)
    scratch = [
        pltpu.VMEM((2 * plan.rows + 2 * plan.m_los, plan.half), jnp.float32),
        pltpu.VMEM((2 * plan.rows, plan.side), jnp.float32),
        pltpu.VMEM((plan.n1s, plan.side), jnp.float32),
    ]
    return call(kernel, shape, ["smem"] + ["vmem"] * 4, scratch)


def swapped(value, bit):
    count = lax.axis_size("acc")
    return lax.ppermute(value, "acc", [(source, source ^ bit) for source in range(count)])


def per_device(reciprocal_spectra, divisor):
    rounds, _, freq_rows, plane = reciprocal_spectra.shape
    quarters = lax.axis_size("acc")
    groups = lax.axis_size("blk") * lax.axis_size("tail")
    plan = Plan(freq_rows, plane, quarters, groups, rounds)
    place = lax.axis_index("acc")
    group = lax.axis_index(("blk", "tail"))
    first_row = group % plan.per * plan.slice_rows
    has_first = jnp.where(first_row == 0, 1, 0)
    at = jnp.stack([place, group // plan.per, first_row + place * freq_rows, has_first]).astype(jnp.int32)
    constants = [jnp.asarray(table) for table in tables(plan)]

    limbs = divisor.reshape(plan.chunk * plan.cols, LANES)
    pieces = {0: limbs}
    bit = quarters // 2
    while bit:
        pieces.update({index | bit: swapped(piece, bit) for index, piece in list(pieces.items())})
        bit //= 2
    spectra = far(reciprocal_spectra.reshape(2 * rounds, freq_rows, plane))
    first, twist, second, near = prepare(plan)(at, *map(far, constants + [limbs]))
    pieces[0] = near
    facing = swapped(opposite(plan)(at, spectra), quarters - 1)
    last, own, own_real, own_imag = resident(plan)(at, first, spectra)

    own_spectrum = forward(plan)(at, *[pieces[index] for index in range(quarters)], first, twist, second)
    own = blend(plan)(own, facing)
    if plan.per > 1:
        own = lax.dynamic_slice_in_dim(own, first_row, plan.slice_rows, 2)
    every = lax.all_to_all(own_spectrum, ("blk", "tail"), 0, 0, tiled=True)
    sums = combine(plan)(at, every, own, own_real, own_imag)
    back = lax.all_to_all(sums, ("blk", "tail"), 0, 0, tiled=True)
    slots = backward(plan)(at, back, last, twist, second)

    held = {index: slots[index] for index in range(quarters)}
    bit = 1
    while bit < quarters:
        sent = sorted(index for index in held if index & bit)
        arrived = swapped(jnp.stack([held[index] for index in sent]), bit)
        held = {index ^ bit: held[index ^ bit] + arrived[where] for where, index in enumerate(sent)}
        bit *= 2
    return held[0].reshape(divisor.shape)


def solution(mesh):
    in_specs = (P(None, None, "acc", None), P(("blk", "tail"), "acc"))
    out_specs = P(("blk", "tail"), "acc")
    return jax.shard_map(per_device, mesh=mesh, in_specs=in_specs, out_specs=out_specs, check_vma=False)
```

profile of v0, /device:TPU:0, one launch (start us, length us, event | category | flops | bytes accessed | tf_op | source)
XLA Modules:
  0.0 52.3 jit_solution(13227873957785307982)
XLA Ops:
  0.0 3.0 %collective-permute-start.1 = (f32[256,128]{1,0:T(8,128)}, f32[256,128]{1,0:T(8,128)S(1)}, u32[]{:S(2)}, u32[]{:S(2)}) collective-permute-start(f32[256,128]{1,0:T(8,128)} %bitcast.8), channel_id=1, source_target_pairs={{0,4},{2,6},{4,0},{6,2},{1,5},{3,7},{5,1},{7,3},{8,12},{10,14},{12... | collective-permute-start | bytes 393224 | tf_op jit(solution)/shard_map/ppermute | solution.py:392
  3.0 0.0 collective-permute-start
  3.0 3.7 %collective-permute-done.1.refs_2_ = f32[256,128]{1,0:T(8,128)S(1)} collective-permute-done((f32[256,128]{1,0:T(8,128)}, f32[256,128]{1,0:T(8,128)S(1)}, u32[]{:S(2)}, u32[]{:S(2)}) %collective-permute-start.1) | collective-permute-done | bytes 131104 | tf_op jit(solution)/shard_map/ppermute | solution.py:392
  6.7 0.0 collective-permute-start.2
  6.7 0.1 pad_add_fusion.at
  6.8 2.1 %shard_map.73 = (bf16[2,256,256]{2,1,0:T(8,128)(2,1)S(1)}, f32[2,128,512]{2,1,0:T(8,128)S(1)}, bf16[2,512,512]{2,1,0:T(8,128)(2,1)S(1)}, f32[256,128]{1,0:T(8,128)S(1)}) custom-call(s32[4]{0:T(128)S(1)} %pad_add_fusion.at, f32[2,128,256]{2,1,0:T(8,128)} %constant.49.clone.refs_0_, f32[4,2,256]{2,1,0:T(2,128)} %constant.50.clone.refs_1_, ...), custom_call_target="tpu_custom_call" | custom-call | flops 1000000 | bytes 1000000 | tf_op jit(solution)/shard_map/pallas_call | solution.py:414
  8.9 0.0 collective-permute-done.refs_1_
  8.9 0.0 collective-permute-done.2.refs_3_
  8.9 2.3 %shard_map.74 = f32[8,72,128]{2,1,0:T(8,128)} custom-call(s32[4]{0:T(128)S(1)} %pad_add_fusion.at, f32[256,128]{1,0:T(8,128)S(1)} %get-tuple-element.13.refs_0_, f32[256,128]{1,0:T(8,128)S(1)} %collective-permute-done.refs_1_, f32[256,128]{1,0:T(8,128)S(1)} %collective-permute-done.1.refs_2_, f32[256,128]{1,0:T(8,128)S(1)} %collective-permute-done.2.refs_3_, ...), custom_call_target="tpu_custom_call" | custom-call | flops 1000000 | bytes 1000000 | tf_op jit(solution)/shard_map/pallas_call | solution.py:419
  11.1 6.1 %all-to-all-start = ((f32[8,72,128]{2,1,0:T(8,128)}), f32[8,72,128]{2,1,0:T(8,128)S(1)}, u32[]{:S(2)}, u32[]{:S(2)}) async-start(f32[8,72,128]{2,1,0:T(8,128)} %shard_map.74), calls=%async_computation | async-start | bytes 589824 | tf_op jit(solution)/shard_map/all_to_all | solution.py:423
  17.2 1.9 %shard_map.76 = f32[8,16,256]{2,1,0:T(8,128)S(1)} custom-call(s32[4]{0:T(128)S(1)} %pad_add_fusion.at, f32[8,16,4096]{2,1,0:T(8,128)} %bitcast.6), custom_call_target="tpu_custom_call" | custom-call | flops 1000000 | bytes 1000000 | tf_op jit(solution)/shard_map/pallas_call | solution.py:416
  19.1 1.4 %collective-permute-start.3 = (f32[8,16,256]{2,1,0:T(8,128)S(1)}, f32[8,16,256]{2,1,0:T(8,128)S(1)}, u32[]{:S(2)}, u32[]{:S(2)}) collective-permute-start(f32[8,16,256]{2,1,0:T(8,128)S(1)} %shard_map.76), channel_id=1, source_target_pairs={{0,6},{2,4},{4,2},{6,0},{1,7},{3,5},{5,3},{7,1},{8,14},{10,12},{12... | collective-permute-start | bytes 393224 | tf_op jit(solution)/shard_map/ppermute | solution.py:392
  20.5 2.0 %shard_map.75 = (bf16[2,256,256]{2,1,0:T(8,128)(2,1)S(1)}, f32[8,2,16,128]{3,2,1,0:T(8,128)S(1)}, f32[4,8,128]{2,1,0:T(8,128)S(1)}, f32[4,8,128]{2,1,0:T(8,128)S(1)}) custom-call(s32[4]{0:T(128)S(1)} %pad_add_fusion.at, bf16[2,256,256]{2,1,0:T(8,128)(2,1)S(1)} %get-tuple-element.14.refs_4_.first, f32[8,16,4096]{2,1,0:T(8,128)} %bitcast.7), custom_call_target="tpu_custom_call" | custom-call | flops 1000000 | bytes 1000000 | tf_op jit(solution)/shard_map/pallas_call | solution.py:417
  22.5 2.1 %collective-permute-done.3.arrived = f32[8,16,256]{2,1,0:T(8,128)S(1)} collective-permute-done((f32[8,16,256]{2,1,0:T(8,128)S(1)}, f32[8,16,256]{2,1,0:T(8,128)S(1)}, u32[]{:S(2)}, u32[]{:S(2)}) %collective-permute-start.3) | collective-permute-done | bytes 131104 | tf_op jit(solution)/shard_map/ppermute | solution.py:392
  24.6 0.3 shard_map.77.own
  24.9 2.6 %all-to-all-done.spectra = f32[8,72,128]{2,1,0:T(8,128)S(1)} async-done(((f32[8,72,128]{2,1,0:T(8,128)}), f32[8,72,128]{2,1,0:T(8,128)S(1)}, u32[]{:S(2)}, u32[]{:S(2)}) %all-to-all-start) | async-done | bytes 294944 | tf_op jit(solution)/shard_map/all_to_all | solution.py:423
  27.5 0.9 %shard_map.78 = f32[8,72,128]{2,1,0:T(8,128)S(1)} custom-call(s32[4]{0:T(128)S(1)} %pad_add_fusion.at, f32[8,72,128]{2,1,0:T(8,128)S(1)} %all-to-all-done.spectra, f32[8,2,16,128]{3,2,1,0:T(8,128)S(1)} %shard_map.77.own, f32[4,8,128]{2,1,0:T(8,128)S(1)} %get-tuple-element.18.own_real, f32[4,8,128]{2,1,0:T(8,128)S(1)} %get-tuple-element.19.own_imag), custom_call_target="tpu_custom_call" | custom-call | flops 1000000 | bytes 1000000 | tf_op jit(solution)/shard_map/pallas_call | solution.py:424
  28.4 14.3 %all_to_all.10.spectra = f32[8,72,128]{2,1,0:T(8,128)S(1)} all-to-all(f32[8,72,128]{2,1,0:T(8,128)S(1)} %shard_map.78), channel_id=1, replica_groups=mesh['blk'=4,'acc'=4,'tail'=2] {'blk','tail'}, dimensions={0} | all-to-all | bytes 589824 | tf_op jit(solution)/shard_map/all_to_all | solution.py:425
  42.7 1.7 %shard_map.79 = f32[4,256,128]{2,1,0:T(8,128)S(1)} custom-call(s32[4]{0:T(128)S(1)} %pad_add_fusion.at, f32[8,72,128]{2,1,0:T(8,128)S(1)} %all_to_all.10.spectra, bf16[2,256,256]{2,1,0:T(8,128)(2,1)S(1)} %get-tuple-element.20.last, f32[2,128,512]{2,1,0:T(8,128)S(1)} %get-tuple-element.15.refs_5_.twist, bf16[2,512,512]{2,1,0:T(8,128)(2,1)S(1)} %get-tuple-element.16.refs_6_.second), custom_call_target="tpu_custom_call" | custom-call | flops 1000000 | bytes 1000000 | tf_op jit(solution)/shard_map/pallas_call | solution.py:426
  44.4 0.1 collective-permute-start.4
  44.5 1.5 %collective-permute-done.4 = f32[2,256,128]{2,1,0:T(8,128)S(1)} collective-permute-done((f32[2,256,128]{2,1,0:T(8,128)S(1)}, f32[2,256,128]{2,1,0:T(8,128)S(1)}, u32[]{:S(2)}, u32[]{:S(2)}) %collective-permute-start.4) | collective-permute-done | bytes 262176 | tf_op jit(solution)/shard_map/ppermute | solution.py:392
  46.0 1.6 %collective-permute-start.5 = (f32[1,256,128]{2,1,0:T(8,128)S(1)}, f32[1,256,128]{2,1,0:T(8,128)S(1)}, u32[]{:S(2)}, u32[]{:S(2)}) collective-permute-start(f32[1,256,128]{2,1,0:T(8,128)S(1)} %slice_add_fusion), channel_id=1, source_target_pairs={{0,4},{2,6},{4,0},{6,2},{1,5},{3,7},{5,1},{7,3},{8,12},{10,14},{12... | collective-permute-start | bytes 393224 | tf_op jit(solution)/shard_map/ppermute | solution.py:392
  47.6 4.0 %collective-permute-done.5 = f32[1,256,128]{2,1,0:T(8,128)S(1)} collective-permute-done((f32[1,256,128]{2,1,0:T(8,128)S(1)}, f32[1,256,128]{2,1,0:T(8,128)S(1)}, u32[]{:S(2)}, u32[]{:S(2)}) %collective-permute-start.5) | collective-permute-done | bytes 131104 | tf_op jit(solution)/shard_map/ppermute | solution.py:392
  51.6 0.7 %fusion = f32[1,256,128]{2,1,0:T(8,128)} fusion(f32[1,256,128]{2,1,0:T(8,128)S(1)} %collective-permute-done.5, f32[2,256,128]{2,1,0:T(8,128)S(1)} %collective-permute-done.4, f32[4,256,128]{2,1,0:T(8,128)S(1)} %shard_map.79), kind=kLoop, calls=%fused_computation.3 | loop fusion | flops 65536 | bytes 524288 | tf_op jit(solution)/shard_map/add | solution.py:433
  (3 shorter events, 0.1 us)
Async XLA Ops:
  0.0 6.7 %collective-permute-start.1 = (f32[256,128]{1,0:T(8,128)}, f32[256,128]{1,0:T(8,128)S(1)}, u32[]{:S(2)}, u32[]{:S(2)}) collective-permute-start(f32[256,128]{1,0:T(8,128)} %bitcast.8), channel_id=1, source_target_pairs={{0,4},{2,6},{4,0},{6,2},{1,5},{3,7},{5,1},{7,3},{8,12},{10,14},{12... | collective-permute-start | bytes 393224 | tf_op jit(solution)/shard_map/ppermute | solution.py:392
  3.0 5.9 %collective-permute-start = (f32[256,128]{1,0:T(8,128)}, f32[256,128]{1,0:T(8,128)S(1)}, u32[]{:S(2)}, u32[]{:S(2)}) collective-permute-start(f32[256,128]{1,0:T(8,128)} %bitcast.9), channel_id=1, source_target_pairs={{0,2},{2,0},{4,6},{6,4},{1,3},{3,1},{5,7},{7,5},{8,10},{10,8},{12,... | collective-permute-start | bytes 393224 | tf_op jit(solution)/shard_map/ppermute | solution.py:392
  6.7 2.2 %collective-permute-start.2 = (f32[256,128]{1,0:T(8,128)S(1)}, f32[256,128]{1,0:T(8,128)S(1)}, u32[]{:S(2)}, u32[]{:S(2)}) collective-permute-start(f32[256,128]{1,0:T(8,128)S(1)} %collective-permute-done.1.refs_2_), channel_id=1, source_target_pairs={{0,2},{2,0},{4,6},{6,4},{1,3},{3,1},{5,7},{7,5},{8,10},{10,8},{12,... | collective-permute-start | bytes 393224 | tf_op jit(solution)/shard_map/ppermute | solution.py:392
  11.1 16.3 %all-to-all-start = ((f32[8,72,128]{2,1,0:T(8,128)}), f32[8,72,128]{2,1,0:T(8,128)S(1)}, u32[]{:S(2)}, u32[]{:S(2)}) async-start(f32[8,72,128]{2,1,0:T(8,128)} %shard_map.74), calls=%async_computation | async-start | bytes 589824 | tf_op jit(solution)/shard_map/all_to_all | solution.py:423
  19.1 5.5 %collective-permute-start.3 = (f32[8,16,256]{2,1,0:T(8,128)S(1)}, f32[8,16,256]{2,1,0:T(8,128)S(1)}, u32[]{:S(2)}, u32[]{:S(2)}) collective-permute-start(f32[8,16,256]{2,1,0:T(8,128)S(1)} %shard_map.76), channel_id=1, source_target_pairs={{0,6},{2,4},{4,2},{6,0},{1,7},{3,5},{5,3},{7,1},{8,14},{10,12},{12... | collective-permute-start | bytes 393224 | tf_op jit(solution)/shard_map/ppermute | solution.py:392
  44.4 1.6 %collective-permute-start.4 = (f32[2,256,128]{2,1,0:T(8,128)S(1)}, f32[2,256,128]{2,1,0:T(8,128)S(1)}, u32[]{:S(2)}, u32[]{:S(2)}) collective-permute-start(f32[2,256,128]{2,1,0:T(8,128)S(1)} %pad_maximum_fusion), channel_id=1, source_target_pairs={{0,2},{2,0},{4,6},{6,4},{1,3},{3,1},{5,7},{7,5},{8,10},{10,8},{12,... | collective-permute-start | bytes 786440 | tf_op jit(solution)/shard_map/ppermute | solution.py:392
  46.0 5.6 %collective-permute-start.5 = (f32[1,256,128]{2,1,0:T(8,128)S(1)}, f32[1,256,128]{2,1,0:T(8,128)S(1)}, u32[]{:S(2)}, u32[]{:S(2)}) collective-permute-start(f32[1,256,128]{2,1,0:T(8,128)S(1)} %slice_add_fusion), channel_id=1, source_target_pairs={{0,4},{2,6},{4,0},{6,2},{1,5},{3,7},{5,1},{7,3},{8,12},{10,14},{12... | collective-permute-start | bytes 393224 | tf_op jit(solution)/shard_map/ppermute | solution.py:392
where the time goes:
time: 52.7 us; the launch traced here: 52.3 us
  blocking collectives  14.3 us (27%)
  waiting for transfers between devices  13.9 us (26%)
  starting transfers between devices  12.1 us (23%)
  Pallas kernels  11.1 us (21%)
  other arithmetic  0.79 us (1%)
    all_to_all x1, blocking collectives, per_device(): back = lax.all_to_all(sums, ('blk', 'tail'), 0, 0, tiled=True)  14.3 us
    ppermute x6, waiting for transfers between devices, swapped(): lax.ppermute(value, 'acc', [(source, source ^ bit) for source in range(co...  11.4 us
    all_to_all x1, starting transfers between devices, per_device(): every = lax.all_to_all(own_spectrum, ('blk', 'tail'), 0, 0, tiled=True)  6.09 us
    ppermute x6, starting transfers between devices, swapped(): lax.ppermute(value, 'acc', [(source, source ^ bit) for source in range(co...  5.98 us
    all_to_all x1, waiting for transfers between devices, per_device(): every = lax.all_to_all(own_spectrum, ('blk', 'tail'), 0, 0, tiled=True)  2.56 us
    pallas_call x1, Pallas kernels, per_device(): forward(plan)  2.26 us
    pallas_call x1, Pallas kernels, per_device(): prepare(plan)(at, *map(far, constants + [limbs]))  2.1 us
    pallas_call x1, Pallas kernels, per_device(): last, own, own_real, own_imag = resident(plan)(at, first, spectra)  1.98 us
  transfers between devices with their start and end apart: 7, of which 5 were waited for; matrix products, arithmetic and copies ran while one was open for 0% of the time, Pallas kernels for 12%

commit v1 on v0

--- a/solution.py
+++ b/solution.py
@@ -66,6 +66,15 @@
     )
 
 
+def spot(plan):
+    place = lax.axis_index("acc")
+    group = lax.axis_index("blk") * lax.axis_size("tail") + lax.axis_index("tail")
+    if plan.per == 1:
+        return place, group, 0, True
+    first_row = lax.rem(group, plan.per) * plan.slice_rows
+    return place, lax.div(group, plan.per), first_row, first_row == 0
+
+
 def far(value):
     return pltpu.with_memory_space_constraint(value, pltpu.HBM)
 
@@ -83,7 +92,7 @@
 
 
 def call(kernel, out_shape, memory, scratch=(), flops=1_000_000, moved=1_000_000):
-    where = {"smem": pltpu.SMEM, "vmem": pltpu.VMEM, "hbm": pltpu.HBM}
+    where = {"vmem": pltpu.VMEM, "hbm": pltpu.HBM}
     vmem = pl.BlockSpec(memory_space=pltpu.VMEM)
     return pl.pallas_call(
         kernel,
@@ -101,7 +110,6 @@
     for m_hi in range(plan.m_his):
         start = pl.multiple_of((m_hi * plan.m_los + m_lo) * plan.radix // LANES * LANES, LANES)
         copies.append(pltpu.make_async_copy(spectra.at[:, :, pl.ds(start, LANES)], held.at[m_hi], sems.at[m_hi]))
-        copies[-1].start()
     return copies
 
 
@@ -117,18 +125,13 @@
     return value
 
 
-def held_scratch(plan):
-    return [
-        pltpu.VMEM((plan.m_his, 2 * plan.rounds, plan.freq_rows, LANES), jnp.float32),
-        pltpu.SemaphoreType.DMA((plan.m_his,)),
-    ]
+def held_shape(plan):
+    return jax.ShapeDtypeStruct((plan.m_his, 2 * plan.rounds, plan.freq_rows, LANES), jnp.float32)
 
 
 def opposite(plan):
-    def kernel(at, spectra, out, held, sems):
-        m_lo = plan.m_los - 1 - at[1]
-        for copy in fetch(plan, spectra, held, sems, m_lo):
-            copy.wait()
+    def kernel(held, out):
+        m_lo = plan.m_los - 1 - spot(plan)[1]
         within = m_lo * plan.radix % LANES + plan.radix // 2
         for index in range(2 * plan.rounds):
             for column in range(plan.half_cols):
@@ -137,20 +140,22 @@
                 )
 
     shape = jax.ShapeDtypeStruct((2 * plan.rounds, plan.freq_rows, plan.half), jnp.float32)
-    return call(kernel, shape, ["smem", "hbm"], held_scratch(plan))
+    return call(kernel, shape, ["vmem"])
 
 
 def prepare(plan):
-    def kernel(at, *refs):
-        first, twist, second, near = refs[6:10]
-        first_rows, first_part, twist_rows, twist_part = refs[10:14]
-        sems = refs[14]
-        place = at[0]
+    def kernel(*refs):
+        first, twist, second, near, held, facing = refs[7:13]
+        first_rows, first_part, twist_rows, twist_part = refs[13:17]
+        sems, held_sems, facing_sems = refs[17:]
+        place, m_lo, _, _ = spot(plan)
         targets = (first_rows, first_part, twist_rows, twist_part, second, near)
         copies = [
             pltpu.make_async_copy(source, target, sems.at[index])
             for index, (source, target) in enumerate(zip(refs[:6], targets))
         ]
+        copies += fetch(plan, refs[6], facing, facing_sems, plan.m_los - 1 - m_lo)
+        copies += fetch(plan, refs[6], held, held_sems, m_lo)
         for copy in copies:
             copy.start()
         copies[0].wait()
@@ -166,8 +171,8 @@
         part_sin = twist_part[pl.ds(place, 1), 1, :]
         twist[0] = twist_rows[0] * part_cos - twist_rows[1] * part_sin
         twist[1] = twist_rows[0] * part_sin + twist_rows[1] * part_cos
-        copies[4].wait()
-        copies[5].wait()
+        for copy in copies[4:]:
+            copy.wait()
 
     shape = jax.ShapeDtypeStruct
     out_shape = (
@@ -175,6 +180,8 @@
         shape((2, plan.rows, plan.side), jnp.float32),
         shape((2, plan.side, 2 * plan.half), jnp.bfloat16),
         shape((plan.chunk * plan.cols, LANES), jnp.float32),
+        held_shape(plan),
+        held_shape(plan),
     )
     scratch = [
         pltpu.VMEM((2, plan.rows, plan.n1s), jnp.float32),
@@ -182,19 +189,18 @@
         pltpu.VMEM((2, plan.rows, plan.side), jnp.float32),
         pltpu.VMEM((plan.quarters, 2, plan.side), jnp.float32),
         pltpu.SemaphoreType.DMA((6,)),
+        pltpu.SemaphoreType.DMA((plan.m_his,)),
+        pltpu.SemaphoreType.DMA((plan.m_his,)),
     ]
-    return call(kernel, out_shape, ["smem"] + ["hbm"] * 6, scratch)
+    return call(kernel, out_shape, ["hbm"] * 7, scratch)
 
 
 def resident(plan):
-    def kernel(at, first, spectra, last, own, own_real, own_imag, held, sems):
-        m_lo = at[1]
-        copies = fetch(plan, spectra, held, sems, m_lo)
+    def kernel(first, held, last, own, own_real, own_imag):
+        _, m_lo, _, unpaired = spot(plan)
         last[0], last[1] = split((first[0].astype(jnp.float32) + first[1].astype(jnp.float32)).T)
-        for copy in copies:
-            copy.wait()
         within = m_lo * plan.radix % LANES
-        kept = at[3].astype(jnp.float32) / plan.length
+        kept = jnp.where(unpaired, 1.0 / plan.length, 0.0)
         for index in range(2 * plan.rounds):
             step, imaginary = divmod(index, 2)
             for column in range(plan.half_cols):
@@ -214,7 +220,7 @@
         shape((plan.rounds, EXTRA, LANES), jnp.float32),
         shape((plan.rounds, EXTRA, LANES), jnp.float32),
     )
-    return call(kernel, out_shape, ["smem", "vmem", "hbm"], held_scratch(plan))
+    return call(kernel, out_shape, ["vmem"] * 2)
 
 
 def blend(plan):
@@ -257,10 +263,10 @@
 
 
 def forward(plan):
-    def kernel(at, *refs):
+    def kernel(*refs):
         limbs = refs[: plan.quarters]
         first, twist, second, out, matrix, turned = refs[plan.quarters :]
-        place = at[0]
+        place = spot(plan)[0]
         for index in range(plan.quarters):
             start = pl.multiple_of((place ^ index) * plan.chunk, 8)
             for column in range(plan.cols):
@@ -299,14 +305,16 @@
         pltpu.VMEM((plan.n1s, plan.side), jnp.float32),
         pltpu.VMEM((2 * plan.rows + 2 * plan.m_los, plan.side), jnp.float32),
     ]
-    return call(kernel, shape, ["smem"] + ["vmem"] * (plan.quarters + 3), scratch)
+    return call(kernel, shape, ["vmem"] * (plan.quarters + 3), scratch)
 
 
 def combine(plan):
-    def kernel(at, spectra, own, own_real, own_imag, out):
-        row = lax.broadcasted_iota(jnp.int32, (plan.slice_rows, LANES), 0) + at[2]
+    def kernel(spectra, own, own_real, own_imag, out):
+        place, _, first_row, _ = spot(plan)
+        first_freq = place * plan.freq_rows
+        row = lax.broadcasted_iota(jnp.int32, (plan.slice_rows, LANES), 0) + first_row + first_freq
         sign = jnp.where(row % 2 == 0, 1.0, -1.0)
-        row = lax.broadcasted_iota(jnp.int32, (EXTRA, LANES), 0) * 0 + at[0] * plan.freq_rows
+        row = lax.broadcasted_iota(jnp.int32, (EXTRA, LANES), 0) * 0 + first_freq
         extra_sign = jnp.where(row % 2 == 0, 1.0, -1.0)
         base = plan.packed - EXTRA
 
@@ -336,12 +344,12 @@
         lax.fori_loop(0, plan.groups, one_block, 0)
 
     shape = jax.ShapeDtypeStruct((plan.groups, plan.packed, LANES), jnp.float32)
-    return call(kernel, shape, ["smem"] + ["vmem"] * 4)
+    return call(kernel, shape, ["vmem"] * 4)
 
 
 def backward(plan):
-    def kernel(at, spectra, last, twist, second, out, stack, spread, matrix):
-        place = at[0]
+    def kernel(spectra, last, twist, second, out, stack, spread, matrix):
+        place = spot(plan)[0]
         rows, whole, few = plan.rows, 2 * plan.rows, plan.m_los
         base = plan.packed - EXTRA
         for part in range(2):
@@ -384,7 +392,7 @@
         pltpu.VMEM((2 * plan.rows, plan.side), jnp.float32),
         pltpu.VMEM((plan.n1s, plan.side), jnp.float32),
     ]
-    return call(kernel, shape, ["smem"] + ["vmem"] * 4, scratch)
+    return call(kernel, shape, ["vmem"] * 4, scratch)
 
 
 def swapped(value, bit):
@@ -397,11 +405,6 @@
     quarters = lax.axis_size("acc")
     groups = lax.axis_size("blk") * lax.axis_size("tail")
     plan = Plan(freq_rows, plane, quarters, groups, rounds)
-    place = lax.axis_index("acc")
-    group = lax.axis_index(("blk", "tail"))
-    first_row = group % plan.per * plan.slice_rows
-    has_first = jnp.where(first_row == 0, 1, 0)
-    at = jnp.stack([place, group // plan.per, first_row + place * freq_rows, has_first]).astype(jnp.int32)
     constants = [jnp.asarray(table) for table in tables(plan)]
 
     limbs = divisor.reshape(plan.chunk * plan.cols, LANES)
@@ -410,20 +413,21 @@
     while bit:
         pieces.update({index | bit: swapped(piece, bit) for index, piece in list(pieces.items())})
         bit //= 2
-    spectra = far(reciprocal_spectra.reshape(2 * rounds, freq_rows, plane))
-    first, twist, second, near = prepare(plan)(at, *map(far, constants + [limbs]))
+    spectra = reciprocal_spectra.reshape(2 * rounds, freq_rows, plane)
+    first, twist, second, near, held, facing = prepare(plan)(*map(far, constants + [limbs, spectra]))
     pieces[0] = near
-    facing = swapped(opposite(plan)(at, spectra), quarters - 1)
-    last, own, own_real, own_imag = resident(plan)(at, first, spectra)
-
-    own_spectrum = forward(plan)(at, *[pieces[index] for index in range(quarters)], first, twist, second)
+    facing = swapped(opposite(plan)(facing), quarters - 1)
+    last, own, own_real, own_imag = resident(plan)(first, held)
+
+    own_spectrum = forward(plan)(*[pieces[index] for index in range(quarters)], first, twist, second)
     own = blend(plan)(own, facing)
     if plan.per > 1:
+        first_row = lax.axis_index(("blk", "tail")) % plan.per * plan.slice_rows
         own = lax.dynamic_slice_in_dim(own, first_row, plan.slice_rows, 2)
     every = lax.all_to_all(own_spectrum, ("blk", "tail"), 0, 0, tiled=True)
-    sums = combine(plan)(at, every, own, own_real, own_imag)
+    sums = combine(plan)(every, own, own_real, own_imag)
     back = lax.all_to_all(sums, ("blk", "tail"), 0, 0, tiled=True)
-    slots = backward(plan)(at, back, last, twist, second)
+    slots = backward(plan)(back, last, twist, second)
 
     held = {index: slots[index] for index in range(quarters)}
     bit = 1

time: 52.7 us -> 50.5 us (0.958)
  Pallas kernels: 11.1 us -> 6.16 us
  waiting for transfers between devices: 13.9 us -> 17.2 us
    pallas_call x5, Pallas kernels: 8.57 us -> 4.12 us  [the longest x1 2.03 us: per_device(): prepare(plan)(*map(far, constants + [limbs, spectra]))]
    all_to_all x1, waiting for transfers between devices: 2.56 us -> 4.25 us  [per_device(): every = lax.all_to_all(own_spectrum, ('blk', 'tail'), 0, 0, tiled=True)]
    ppermute x6, waiting for transfers between devices: 11.4 us -> 13 us  [swapped(): lax.ppermute(value, 'acc', [(source, source ^ bit) for source in range(co...]
    pallas_call x1, Pallas kernels: 2.26 us -> 1.73 us  [per_device(): forward(plan)]
  transfers between devices with their start and end apart: 7 -> 7, of which waited for: 5 -> 5; matrix products, arithmetic and copies ran while one was open for 0% -> 0% of each run, Pallas kernels for 12% -> 6%
where the time goes in v1:
time: 50.5 us; the launch traced here: 50.3 us
  waiting for transfers between devices  17.2 us (34%)
  blocking collectives  14 us (28%)
  starting transfers between devices  12.1 us (24%)
  Pallas kernels  6.16 us (12%)
  other arithmetic  0.72 us (1%)
    all_to_all x1, blocking collectives, per_device(): back = lax.all_to_all(sums, ('blk', 'tail'), 0, 0, tiled=True)  14 us
    ppermute x6, waiting for transfers between devices, swapped(): lax.ppermute(value, 'acc', [(source, source ^ bit) for source in range(co...  13 us
    all_to_all x1, starting transfers between devices, per_device(): every = lax.all_to_all(own_spectrum, ('blk', 'tail'), 0, 0, tiled=True)  6.08 us
    ppermute x6, starting transfers between devices, swapped(): lax.ppermute(value, 'acc', [(source, source ^ bit) for source in range(co...  5.98 us
    all_to_all x1, waiting for transfers between devices, per_device(): every = lax.all_to_all(own_spectrum, ('blk', 'tail'), 0, 0, tiled=True)  4.25 us
    pallas_call x1, Pallas kernels, per_device(): prepare(plan)(*map(far, constants + [limbs, spectra]))  2.03 us
    pallas_call x1, Pallas kernels, per_device(): forward(plan)  1.73 us
    pallas_call x1, Pallas kernels, per_device(): slots = backward(plan)(back, last, twist, second)  1.14 us
  transfers between devices with their start and end apart: 7, of which 5 were waited for; matrix products, arithmetic and copies ran while one was open for 0% of the time, Pallas kernels for 6%

profile of v1, /device:TPU:0, one launch (start us, length us, event | category | flops | bytes accessed | tf_op | source)
XLA Modules:
  0.0 50.3 jit_solution(3256967964388819012)
XLA Ops:
  0.0 3.0 %collective-permute-start.1 = (f32[256,128]{1,0:T(8,128)}, f32[256,128]{1,0:T(8,128)S(1)}, u32[]{:S(2)}, u32[]{:S(2)}) collective-permute-start(f32[256,128]{1,0:T(8,128)} %bitcast.4), channel_id=1, source_target_pairs={{0,4},{2,6},{4,0},{6,2},{1,5},{3,7},{5,1},{7,3},{8,12},{10,14},{12... | collective-permute-start | bytes 393224 | tf_op jit(solution)/shard_map/ppermute | solution.py:400
  3.0 0.0 collective-permute-start
  3.0 3.7 %collective-permute-done.1.refs_2_ = f32[256,128]{1,0:T(8,128)S(1)} collective-permute-done((f32[256,128]{1,0:T(8,128)}, f32[256,128]{1,0:T(8,128)S(1)}, u32[]{:S(2)}, u32[]{:S(2)}) %collective-permute-start.1) | collective-permute-done | bytes 131104 | tf_op jit(solution)/shard_map/ppermute | solution.py:400
  6.7 0.0 collective-permute-start.2
  6.7 2.0 %shard_map.73 = (bf16[2,256,256]{2,1,0:T(8,128)(2,1)S(1)}, f32[2,128,512]{2,1,0:T(8,128)S(1)}, bf16[2,512,512]{2,1,0:T(8,128)(2,1)S(1)}, f32[256,128]{1,0:T(8,12...) custom-call(f32[2,128,256]{2,1,0:T(8,128)} %constant.10.clone.refs_0_, ...), custom_call_target="tpu_custom_call" | custom-call | flops 1000000 | bytes 1000000 | tf_op jit(solution)/shard_map/pallas_call | solution.py:417
  8.7 0.0 collective-permute-done.refs_1_
  8.7 0.0 collective-permute-done.2.refs_3_
  8.7 1.7 %shard_map.74 = f32[8,72,128]{2,1,0:T(8,128)} custom-call(f32[256,128]{1,0:T(8,128)S(1)} %get-tuple-element.15.refs_0_, f32[256,128]{1,0:T(8,128)S(1)} %collective-permute-done.refs_1_, f32[256,128]{1,0:T(8,128)S(1)} %collective-permute-done.1.refs_2_, f32[256,128]{1,0:T(8,128)S(1)} %collective-permute-done.2.refs_3_, ...), custom_call_target="tpu_custom_call" | custom-call | flops 1000000 | bytes 1000000 | tf_op jit(solution)/shard_map/pallas_call | solution.py:422
  10.5 6.1 %all-to-all-start = ((f32[8,72,128]{2,1,0:T(8,128)}), f32[8,72,128]{2,1,0:T(8,128)S(1)}, u32[]{:S(2)}, u32[]{:S(2)}) async-start(f32[8,72,128]{2,1,0:T(8,128)} %shard_map.74), calls=%async_computation | async-start | bytes 589824 | tf_op jit(solution)/shard_map/all_to_all | solution.py:427
  16.6 0.2 shard_map.76
  16.8 1.4 %collective-permute-start.3 = (f32[8,16,256]{2,1,0:T(8,128)S(1)}, f32[8,16,256]{2,1,0:T(8,128)S(1)}, u32[]{:S(2)}, u32[]{:S(2)}) collective-permute-start(f32[8,16,256]{2,1,0:T(8,128)S(1)} %shard_map.76), channel_id=1, source_target_pairs={{0,6},{2,4},{4,2},{6,0},{1,7},{3,5},{5,3},{7,1},{8,14},{10,12},{12... | collective-permute-start | bytes 393224 | tf_op jit(solution)/shard_map/ppermute | solution.py:400
  18.2 0.4 shard_map.75
  18.5 3.7 %collective-permute-done.3.arrived = f32[8,16,256]{2,1,0:T(8,128)S(1)} collective-permute-done((f32[8,16,256]{2,1,0:T(8,128)S(1)}, f32[8,16,256]{2,1,0:T(8,128)S(1)}, u32[]{:S(2)}, u32[]{:S(2)}) %collective-permute-start.3) | collective-permute-done | bytes 131104 | tf_op jit(solution)/shard_map/ppermute | solution.py:400
  22.2 0.3 shard_map.77.own
  22.5 4.3 %all-to-all-done.spectra = f32[8,72,128]{2,1,0:T(8,128)S(1)} async-done(((f32[8,72,128]{2,1,0:T(8,128)}), f32[8,72,128]{2,1,0:T(8,128)S(1)}, u32[]{:S(2)}, u32[]{:S(2)}) %all-to-all-start) | async-done | bytes 294944 | tf_op jit(solution)/shard_map/all_to_all | solution.py:427
  26.8 0.4 shard_map.78
  27.2 14.0 %all_to_all.10.spectra = f32[8,72,128]{2,1,0:T(8,128)S(1)} all-to-all(f32[8,72,128]{2,1,0:T(8,128)S(1)} %shard_map.78), channel_id=1, replica_groups=mesh['blk'=4,'acc'=4,'tail'=2] {'blk','tail'}, dimensions={0} | all-to-all | bytes 589824 | tf_op jit(solution)/shard_map/all_to_all | solution.py:429
  41.2 1.1 %shard_map.79 = f32[4,256,128]{2,1,0:T(8,128)S(1)} custom-call(f32[8,72,128]{2,1,0:T(8,128)S(1)} %all_to_all.10.spectra, bf16[2,256,256]{2,1,0:T(8,128)(2,1)S(1)} %get-tuple-element.24.last, f32[2,128,512]{2,1,0:T(8,128)S(1)} %get-tuple-element.17.refs_5_.twist, bf16[2,512,512]{2,1,0:T(8,128)(2,1)S(1)} %get-tuple-element.18.refs_6_.second), custom_call_target="tpu_custom_call" | custom-call | flops 1000000 | bytes 1000000 | tf_op jit(solution)/shard_map/pallas_call | solution.py:430
  42.4 0.1 collective-permute-start.4
  42.4 1.5 %collective-permute-done.4 = f32[2,256,128]{2,1,0:T(8,128)S(1)} collective-permute-done((f32[2,256,128]{2,1,0:T(8,128)S(1)}, f32[2,256,128]{2,1,0:T(8,128)S(1)}, u32[]{:S(2)}, u32[]{:S(2)}) %collective-permute-start.4) | collective-permute-done | bytes 262176 | tf_op jit(solution)/shard_map/ppermute | solution.py:400
  44.0 1.6 %collective-permute-start.5 = (f32[1,256,128]{2,1,0:T(8,128)S(1)}, f32[1,256,128]{2,1,0:T(8,128)S(1)}, u32[]{:S(2)}, u32[]{:S(2)}) collective-permute-start(f32[1,256,128]{2,1,0:T(8,128)S(1)} %slice_add_fusion), channel_id=1, source_target_pairs={{0,4},{2,6},{4,0},{6,2},{1,5},{3,7},{5,1},{7,3},{8,12},{10,14},{12... | collective-permute-start | bytes 393224 | tf_op jit(solution)/shard_map/ppermute | solution.py:400
  45.5 4.0 %collective-permute-done.5 = f32[1,256,128]{2,1,0:T(8,128)S(1)} collective-permute-done((f32[1,256,128]{2,1,0:T(8,128)S(1)}, f32[1,256,128]{2,1,0:T(8,128)S(1)}, u32[]{:S(2)}, u32[]{:S(2)}) %collective-permute-start.5) | collective-permute-done | bytes 131104 | tf_op jit(solution)/shard_map/ppermute | solution.py:400
  49.6 0.7 %fusion = f32[1,256,128]{2,1,0:T(8,128)} fusion(f32[1,256,128]{2,1,0:T(8,128)S(1)} %collective-permute-done.5, f32[2,256,128]{2,1,0:T(8,128)S(1)} %collective-permute-done.4, f32[4,256,128]{2,1,0:T(8,128)S(1)} %shard_map.79), kind=kLoop, calls=%fused_computation.3 | loop fusion | flops 65536 | bytes 524288 | tf_op jit(solution)/shard_map/add | solution.py:437
  (3 shorter events, 0.1 us)
Async XLA Ops:
  0.0 6.7 %collective-permute-start.1 = (f32[256,128]{1,0:T(8,128)}, f32[256,128]{1,0:T(8,128)S(1)}, u32[]{:S(2)}, u32[]{:S(2)}) collective-permute-start(f32[256,128]{1,0:T(8,128)} %bitcast.4), channel_id=1, source_target_pairs={{0,4},{2,6},{4,0},{6,2},{1,5},{3,7},{5,1},{7,3},{8,12},{10,14},{12... | collective-permute-start | bytes 393224 | tf_op jit(solution)/shard_map/ppermute | solution.py:400
  3.0 5.8 %collective-permute-start = (f32[256,128]{1,0:T(8,128)}, f32[256,128]{1,0:T(8,128)S(1)}, u32[]{:S(2)}, u32[]{:S(2)}) collective-permute-start(f32[256,128]{1,0:T(8,128)} %bitcast.5), channel_id=1, source_target_pairs={{0,2},{2,0},{4,6},{6,4},{1,3},{3,1},{5,7},{7,5},{8,10},{10,8},{12,... | collective-permute-start | bytes 393224 | tf_op jit(solution)/shard_map/ppermute | solution.py:400
  6.7 2.1 %collective-permute-start.2 = (f32[256,128]{1,0:T(8,128)S(1)}, f32[256,128]{1,0:T(8,128)S(1)}, u32[]{:S(2)}, u32[]{:S(2)}) collective-permute-start(f32[256,128]{1,0:T(8,128)S(1)} %collective-permute-done.1.refs_2_), channel_id=1, source_target_pairs={{0,2},{2,0},{4,6},{6,4},{1,3},{3,1},{5,7},{7,5},{8,10},{10,8},{12,... | collective-permute-start | bytes 393224 | tf_op jit(solution)/shard_map/ppermute | solution.py:400
  10.5 16.3 %all-to-all-start = ((f32[8,72,128]{2,1,0:T(8,128)}), f32[8,72,128]{2,1,0:T(8,128)S(1)}, u32[]{:S(2)}, u32[]{:S(2)}) async-start(f32[8,72,128]{2,1,0:T(8,128)} %shard_map.74), calls=%async_computation | async-start | bytes 589824 | tf_op jit(solution)/shard_map/all_to_all | solution.py:427
  16.8 5.5 %collective-permute-start.3 = (f32[8,16,256]{2,1,0:T(8,128)S(1)}, f32[8,16,256]{2,1,0:T(8,128)S(1)}, u32[]{:S(2)}, u32[]{:S(2)}) collective-permute-start(f32[8,16,256]{2,1,0:T(8,128)S(1)} %shard_map.76), channel_id=1, source_target_pairs={{0,6},{2,4},{4,2},{6,0},{1,7},{3,5},{5,3},{7,1},{8,14},{10,12},{12... | collective-permute-start | bytes 393224 | tf_op jit(solution)/shard_map/ppermute | solution.py:400
  42.4 1.6 %collective-permute-start.4 = (f32[2,256,128]{2,1,0:T(8,128)S(1)}, f32[2,256,128]{2,1,0:T(8,128)S(1)}, u32[]{:S(2)}, u32[]{:S(2)}) collective-permute-start(f32[2,256,128]{2,1,0:T(8,128)S(1)} %pad_maximum_fusion), channel_id=1, source_target_pairs={{0,2},{2,0},{4,6},{6,4},{1,3},{3,1},{5,7},{7,5},{8,10},{10,8},{12,... | collective-permute-start | bytes 786440 | tf_op jit(solution)/shard_map/ppermute | solution.py:400
  44.0 5.6 %collective-permute-start.5 = (f32[1,256,128]{2,1,0:T(8,128)S(1)}, f32[1,256,128]{2,1,0:T(8,128)S(1)}, u32[]{:S(2)}, u32[]{:S(2)}) collective-permute-start(f32[1,256,128]{2,1,0:T(8,128)S(1)} %slice_add_fusion), channel_id=1, source_target_pairs={{0,4},{2,6},{4,0},{6,2},{1,5},{3,7},{5,1},{7,3},{8,12},{10,14},{12... | collective-permute-start | bytes 393224 | tf_op jit(solution)/shard_map/ppermute | solution.py:400

commit v2 on v1

--- a/solution.py
+++ b/solution.py
@@ -10,7 +10,7 @@
 
 
 LANES = 128
-EXTRA = 8
+TILE = 8
 GRANT = 16 * 1024 * 1024
 STRIDE = 2
 
@@ -34,7 +34,7 @@
         self.half_cols = self.half // LANES
         self.slice_rows = self.rows // groups
         self.per = groups // self.m_los
-        self.packed = 2 * self.half_cols * self.slice_rows + EXTRA
+        self.packed = 2 * self.half_cols * self.slice_rows
 
 
 def tables(plan):
@@ -70,9 +70,12 @@
     place = lax.axis_index("acc")
     group = lax.axis_index("blk") * lax.axis_size("tail") + lax.axis_index("tail")
     if plan.per == 1:
-        return place, group, 0, True
-    first_row = lax.rem(group, plan.per) * plan.slice_rows
-    return place, lax.div(group, plan.per), first_row, first_row == 0
+        return place, group, 0
+    return place, lax.div(group, plan.per), lax.rem(group, plan.per) * plan.slice_rows
+
+
+def rim_m_lo(plan, place, m_lo):
+    return jnp.where(place == 0, lax.rem(plan.m_los - m_lo, plan.m_los), plan.m_los - 1 - m_lo)
 
 
 def far(value):
@@ -105,11 +108,12 @@
     )
 
 
-def fetch(plan, spectra, held, sems, m_lo):
+def fetch(plan, spectra, held, sems, m_lo, rows):
     copies = []
     for m_hi in range(plan.m_his):
         start = pl.multiple_of((m_hi * plan.m_los + m_lo) * plan.radix // LANES * LANES, LANES)
-        copies.append(pltpu.make_async_copy(spectra.at[:, :, pl.ds(start, LANES)], held.at[m_hi], sems.at[m_hi]))
+        source = spectra.at[:, pl.ds(0, rows), pl.ds(start, LANES)]
+        copies.append(pltpu.make_async_copy(source, held.at[m_hi], sems.at[m_hi]))
     return copies
 
 
@@ -125,37 +129,59 @@
     return value
 
 
-def held_shape(plan):
-    return jax.ShapeDtypeStruct((plan.m_his, 2 * plan.rounds, plan.freq_rows, LANES), jnp.float32)
+def held_shape(plan, rows):
+    return jax.ShapeDtypeStruct((plan.m_his, 2 * plan.rounds, rows, LANES), jnp.float32)
+
+
+def bundle(plan):
+    def kernel(near, held, out, rim):
+        place, m_lo, _ = spot(plan)
+        within = rim_m_lo(plan, place, m_lo) * plan.radix % LANES + plan.radix // 2
+        base = plan.chunk * plan.cols
+        out[:base] = near[...]
+        for index in range(2 * plan.rounds):
+            for column in range(plan.half_cols):
+                row = index * plan.half_cols + column
+                value = gathered(plan, held, index, column, within, 1)
+                out[base + row : base + row + 1] = value
+                rim[index : index + 1, column * LANES : (column + 1) * LANES] = value
+
+    shape = jax.ShapeDtypeStruct
+    rows = plan.chunk * plan.cols + 2 * plan.rounds * plan.half_cols
+    out_shape = (shape((rows, LANES), jnp.float32), shape((2 * plan.rounds, plan.half), jnp.float32))
+    return call(kernel, out_shape, ["vmem"] * 2)
 
 
 def opposite(plan):
-    def kernel(held, out):
+    def kernel(held, other, out):
         m_lo = plan.m_los - 1 - spot(plan)[1]
         within = m_lo * plan.radix % LANES + plan.radix // 2
+        base = plan.chunk * plan.cols
         for index in range(2 * plan.rounds):
             for column in range(plan.half_cols):
-                out[index, :, column * LANES : (column + 1) * LANES] = gathered(
-                    plan, held, index, column, within, plan.freq_rows
-                )
+                lanes = slice(column * LANES, (column + 1) * LANES)
+                out[index, :, lanes] = gathered(plan, held, index, column, within, plan.freq_rows)
+                row = base + index * plan.half_cols + column
+                out[index, :1, lanes] = other[row : row + 1]
 
     shape = jax.ShapeDtypeStruct((2 * plan.rounds, plan.freq_rows, plan.half), jnp.float32)
-    return call(kernel, shape, ["vmem"])
+    return call(kernel, shape, ["vmem"] * 2)
 
 
 def prepare(plan):
     def kernel(*refs):
-        first, twist, second, near, held, facing = refs[7:13]
-        first_rows, first_part, twist_rows, twist_part = refs[13:17]
-        sems, held_sems, facing_sems = refs[17:]
-        place, m_lo, _, _ = spot(plan)
+        first, twist, second, near, held, facing, rim = refs[7:14]
+        first_rows, first_part, twist_rows, twist_part = refs[14:18]
+        sems, held_sems, facing_sems, rim_sems = refs[18:]
+        place, m_lo, _ = spot(plan)
         targets = (first_rows, first_part, twist_rows, twist_part, second, near)
         copies = [
             pltpu.make_async_copy(source, target, sems.at[index])
             for index, (source, target) in enumerate(zip(refs[:6], targets))
         ]
-        copies += fetch(plan, refs[6], facing, facing_sems, plan.m_los - 1 - m_lo)
-        copies += fetch(plan, refs[6], held, held_sems, m_lo)
+        copies += fetch(plan, refs[6], facing, facing_sems, plan.m_los - 1 - m_lo, plan.freq_rows)
+        copies += fetch(plan, refs[6], held, held_sems, m_lo, plan.freq_rows)
+        copies += fetch(plan, refs[6], rim, rim_sems, rim_m_lo(plan, place, m_lo), TILE)
         for copy in copies:
             copy.start()
         copies[0].wait()
@@ -180,8 +206,9 @@
         shape((2, plan.rows, plan.side), jnp.float32),
         shape((2, plan.side, 2 * plan.half), jnp.bfloat16),
         shape((plan.chunk * plan.cols, LANES), jnp.float32),
-        held_shape(plan),
-        held_shape(plan),
+        held_shape(plan, plan.freq_rows),
+        held_shape(plan, plan.freq_rows),
+        held_shape(plan, TILE),
     )
     scratch = [
         pltpu.VMEM((2, plan.rows, plan.n1s), jnp.float32),
@@ -191,40 +218,32 @@
         pltpu.SemaphoreType.DMA((6,)),
         pltpu.SemaphoreType.DMA((plan.m_his,)),
         pltpu.SemaphoreType.DMA((plan.m_his,)),
+        pltpu.SemaphoreType.DMA((plan.m_his,)),
     ]
     return call(kernel, out_shape, ["hbm"] * 7, scratch)
 
 
 def resident(plan):
-    def kernel(first, held, last, own, own_real, own_imag):
-        _, m_lo, _, unpaired = spot(plan)
+    def kernel(first, held, last, own):
+        _, m_lo, _ = spot(plan)
         last[0], last[1] = split((first[0].astype(jnp.float32) + first[1].astype(jnp.float32)).T)
         within = m_lo * plan.radix % LANES
-        kept = jnp.where(unpaired, 1.0 / plan.length, 0.0)
         for index in range(2 * plan.rounds):
-            step, imaginary = divmod(index, 2)
             for column in range(plan.half_cols):
                 own[index, column] = gathered(plan, held, index, column, within, plan.freq_rows)
-                upper = gathered(plan, held, index, column, within + plan.radix // 2, 1) * kept
-                for turn in range(EXTRA // plan.half_cols):
-                    row = turn * plan.half_cols + column
-                    if imaginary:
-                        own_imag[step, row : row + 1] = upper if turn % 2 else -upper
-                    else:
-                        own_real[step, row : row + 1] = upper
 
     shape = jax.ShapeDtypeStruct
     out_shape = (
         shape((2, plan.n1s, 2 * plan.rows), jnp.bfloat16),
         shape((2 * plan.rounds, plan.half_cols, plan.freq_rows, LANES), jnp.float32),
-        shape((plan.rounds, EXTRA, LANES), jnp.float32),
-        shape((plan.rounds, EXTRA, LANES), jnp.float32),
     )
     return call(kernel, out_shape, ["vmem"] * 2)
 
 
-def blend(plan):
-    def kernel(own, arrived, out):
+def blend(plan, rides):
+    def kernel(own, arrived, rim, out):
+        place, m_lo, _ = spot(plan)
+        special = (place == 0) & (m_lo == 0)
         count = 2 * plan.rounds * plan.freq_rows
         row = lax.broadcasted_iota(jnp.int32, (count, count), 0)
         column = lax.broadcasted_iota(jnp.int32, (count, count), 1)
@@ -234,22 +253,43 @@
         row = lax.broadcasted_iota(jnp.int32, (plan.half, plan.half), 0)
         column = lax.broadcasted_iota(jnp.int32, (plan.half, plan.half), 1)
         flip = jnp.where(row + column == plan.half - 1, 1.0, 0.0).astype(jnp.bfloat16)
-        total = None
-        for value in split(arrived[...].reshape(count, plan.half)):
-            turned = jnp.dot(turn, value, preferred_element_type=jnp.float32).astype(jnp.bfloat16)
-            turned = jnp.dot(turned, flip, preferred_element_type=jnp.float32)
-            total = turned if total is None else total + turned
+        dot = lambda a, b: jnp.dot(a, b, preferred_element_type=jnp.float32)
+        high, low = split(arrived[...].reshape(count, plan.half))
+        total = dot(dot(turn, high).astype(jnp.bfloat16), flip) + dot(dot(turn, low).astype(jnp.bfloat16), flip)
+        paired = rim[...]
+        if rides:
+            top = jnp.concatenate([arrived[index, :1] for index in range(2 * plan.rounds)], axis=0)
+            paired = jnp.where(lax.rem(place, 2) == 1, top, paired)
+        high, low = split(paired)
+        edge = dot(high, flip) + dot(low, flip)
+        lane = lax.broadcasted_iota(jnp.int32, edge.shape, 1)
+        later = pltpu.roll(edge, plan.radix // 2, 1)
+        later = jnp.where(lane < plan.radix // 2, pltpu.roll(later, 1, 1), later)
+        edge = jnp.where(special, later, edge)
+        top = lax.broadcasted_iota(jnp.int32, (plan.freq_rows, LANES), 0) == 0
+        corner = top & (lax.broadcasted_iota(jnp.int32, (plan.freq_rows, LANES), 1) == 0)
+        corner = corner & special
         scale = 1.0 / plan.length
-        for index in range(2 * plan.rounds):
-            sign = -1.0 if index % 2 else 1.0
+        for step in range(plan.rounds):
             for column in range(plan.half_cols):
-                there = total[
-                    index * plan.freq_rows : (index + 1) * plan.freq_rows, column * LANES : (column + 1) * LANES
-                ]
-                out[index, column] = (own[index, column] + sign * there) * scale
-
-    shape = jax.ShapeDtypeStruct((2 * plan.rounds, plan.half_cols, plan.freq_rows, LANES), jnp.float32)
-    return call(kernel, shape, ["vmem"] * 2)
+                lanes = slice(column * LANES, (column + 1) * LANES)
+                whole = []
+                for part in range(2):
+                    index = 2 * step + part
+                    there = total[index * plan.freq_rows : (index + 1) * plan.freq_rows, lanes]
+                    there = jnp.where(top, edge[index : index + 1, lanes], there)
+                    here = own[index, column]
+                    if column == 0:
+                        there = jnp.where(corner, here if part else 0.0, there)
+                    whole.append((here - there if part else here + there) * scale)
+                out[3 * step, column] = whole[0]
+                out[3 * step + 1, column] = whole[1]
+                if column == 0:
+                    whole[0] = jnp.where(corner, rim[2 * step : 2 * step + 1, lanes] * scale, whole[0])
+                out[3 * step + 2, column] = whole[0]
+
+    shape = jax.ShapeDtypeStruct((3 * plan.rounds, plan.half_cols, plan.freq_rows, LANES), jnp.float32)
+    return call(kernel, shape, ["vmem"] * 3)
 
 
 def alternating(plan, count):
@@ -274,53 +314,42 @@
                     pl.ds(column, plan.chunk, stride=plan.cols), :
                 ]
         value = product((first[0], first[1]), split(matrix[...]))
-        rows, whole, few = plan.rows, 2 * plan.rows, plan.m_los
+        rows = plan.rows
         real, imag = value[:rows], value[rows:]
         turned[:rows] = real * twist[0] - imag * twist[1]
-        turned[rows:whole] = real * twist[1] + imag * twist[0]
-        sign = alternating(plan, 1)
-        for part in range(2):
-            for m_lo in range(few):
-                row, start = part * rows + m_lo * plan.freq_rows, whole + part * few + m_lo
-                turned[start : start + 1] = turned[row : row + 1] * sign
+        turned[rows:] = real * twist[1] + imag * twist[0]
+        middle = jnp.sum(turned[:1] * alternating(plan, 1), axis=1, keepdims=True)
+        middle = jnp.where(place == 0, middle, 0.0)
         value = product(split(turned[...]), (second[0], second[1]))
         by_cos, by_sin = value[:, : plan.half], value[:, plan.half :]
-        main = (by_cos[:rows] + by_sin[rows:whole], by_cos[rows:whole] - by_sin[:rows])
-        extra = (by_cos[whole : whole + few] + by_sin[whole + few :], by_cos[whole + few :] - by_sin[whole : whole + few])
-        base = plan.packed - EXTRA
+        main = (by_cos[:rows] + by_sin[rows:], by_cos[rows:] - by_sin[:rows])
+        corner = lax.broadcasted_iota(jnp.int32, (plan.slice_rows, LANES), 0) == 0
+        corner = corner & (lax.broadcasted_iota(jnp.int32, (plan.slice_rows, LANES), 1) == 0)
         for group in range(plan.groups):
             for part in range(2):
                 for column in range(plan.half_cols):
                     lanes = slice(column * LANES, (column + 1) * LANES)
-                    out[group, packed_rows(plan, part, column)] = main[part][
-                        group * plan.slice_rows : (group + 1) * plan.slice_rows, lanes
-                    ]
-                    m_lo = group // plan.per
-                    for turn in range(EXTRA // (2 * plan.half_cols)):
-                        row = base + (turn * 2 + part) * plan.half_cols + column
-                        out[group, row : row + 1] = extra[part][m_lo : m_lo + 1, lanes]
+                    tile = main[part][group * plan.slice_rows : (group + 1) * plan.slice_rows, lanes]
+                    if (group, part, column) == (0, 1, 0):
+                        tile = tile + jnp.where(corner, middle, 0.0)
+                    out[group, packed_rows(plan, part, column)] = tile
 
     shape = jax.ShapeDtypeStruct((plan.groups, plan.packed, LANES), jnp.float32)
     scratch = [
         pltpu.VMEM((plan.n1s, plan.side), jnp.float32),
-        pltpu.VMEM((2 * plan.rows + 2 * plan.m_los, plan.side), jnp.float32),
+        pltpu.VMEM((2 * plan.rows, plan.side), jnp.float32),
     ]
     return call(kernel, shape, ["vmem"] * (plan.quarters + 3), scratch)
 
 
 def combine(plan):
-    def kernel(spectra, own, own_real, own_imag, out):
-        place, _, first_row, _ = spot(plan)
-        first_freq = place * plan.freq_rows
-        row = lax.broadcasted_iota(jnp.int32, (plan.slice_rows, LANES), 0) + first_row + first_freq
+    def kernel(spectra, own, out):
+        place, _, first_row = spot(plan)
+        row = lax.broadcasted_iota(jnp.int32, (plan.slice_rows, LANES), 0) + first_row + place * plan.freq_rows
         sign = jnp.where(row % 2 == 0, 1.0, -1.0)
-        row = lax.broadcasted_iota(jnp.int32, (EXTRA, LANES), 0) * 0 + first_freq
-        extra_sign = jnp.where(row % 2 == 0, 1.0, -1.0)
-        base = plan.packed - EXTRA
 
         def one_block(block, carry):
             sums = [jnp.zeros((plan.slice_rows, LANES), jnp.float32) for _ in range(2 * plan.half_cols)]
-            extra = jnp.zeros((EXTRA, LANES), jnp.float32)
             for step in range(plan.rounds):
                 here = lax.rem(block + (plan.rounds * STRIDE * plan.groups - step * STRIDE), plan.groups)
                 before = lax.rem(here + (plan.groups - 1), plan.groups)
@@ -330,52 +359,37 @@
                         + sign * spectra[before, packed_rows(plan, part, column)]
                         for part in range(2)
                     )
-                    own_r, own_i = own[2 * step, column], own[2 * step + 1, column]
+                    own_r, own_i, own_c = (own[3 * step + part, column] for part in range(3))
                     sums[column] = sums[column] + own_r * real - own_i * imag
-                    sums[plan.half_cols + column] = sums[plan.half_cols + column] + own_r * imag + own_i * real
-                both = spectra[here, base:] + extra_sign * spectra[before, base:]
-                extra = extra + own_real[step] * both + own_imag[step] * pltpu.roll(both, plan.half_cols, 0)
+                    sums[plan.half_cols + column] = sums[plan.half_cols + column] + own_c * imag + own_i * real
             for part in range(2):
                 for column in range(plan.half_cols):
                     out[block, packed_rows(plan, part, column)] = sums[part * plan.half_cols + column]
-            out[block, base:] = extra
             return carry
 
         lax.fori_loop(0, plan.groups, one_block, 0)
 
     shape = jax.ShapeDtypeStruct((plan.groups, plan.packed, LANES), jnp.float32)
-    return call(kernel, shape, ["vmem"] * 4)
+    return call(kernel, shape, ["vmem"] * 2)
 
 
 def backward(plan):
     def kernel(spectra, last, twist, second, out, stack, spread, matrix):
         place = spot(plan)[0]
-        rows, whole, few = plan.rows, 2 * plan.rows, plan.m_los
-        base = plan.packed - EXTRA
+        rows = plan.rows
         for part in range(2):
             for column in range(plan.half_cols):
                 lanes = slice(column * LANES, (column + 1) * LANES)
                 for group in range(plan.groups):
                     start = part * rows + group * plan.slice_rows
                     stack[start : start + plan.slice_rows, lanes] = spectra[group, packed_rows(plan, part, column)]
-                for m_lo in range(few):
-                    row = base + part * plan.half_cols + column
-                    start = whole + part * few + m_lo
-                    stack[start : start + 1, lanes] = spectra[m_lo * plan.per, row : row + 1]
         value = split(stack[...])
         by_cos = product(value, (second[0, :, : plan.half], second[1, :, : plan.half]), True)
         by_sin = product(value, (second[0, :, plan.half :], second[1, :, plan.half :]), True)
-        spread[:rows] = by_cos[:rows] - by_sin[rows:whole]
-        spread[rows:] = by_cos[rows:whole] + by_sin[:rows]
-        sign = alternating(plan, few)
-        extra = (
-            (by_cos[whole : whole + few] - by_sin[whole + few :]) * sign,
-            (by_cos[whole + few :] + by_sin[whole : whole + few]) * sign,
-        )
-        for part in range(2):
-            for m_lo in range(few):
-                row = part * rows + m_lo * plan.freq_rows
-                spread[row : row + 1] = spread[row : row + 1] + extra[part][m_lo : m_lo + 1]
+        spread[:rows] = by_cos[:rows] - by_sin[rows:]
+        spread[rows:] = by_cos[rows:] + by_sin[:rows]
+        middle = jnp.where(place == 0, stack[rows : rows + 1, :1], 0.0)
+        spread[:1] = spread[:1] + middle * alternating(plan, 1)
         real, imag = spread[:rows], spread[rows:]
         turned = jnp.concatenate([real * twist[0] + imag * twist[1], imag * twist[0] - real * twist[1]], axis=0)
         matrix[...] = product((last[0], last[1]), split(turned))
@@ -388,7 +402,7 @@
 
     shape = jax.ShapeDtypeStruct((plan.quarters, plan.chunk * plan.cols, LANES), jnp.float32)
     scratch = [
-        pltpu.VMEM((2 * plan.rows + 2 * plan.m_los, plan.half), jnp.float32),
+        pltpu.VMEM((2 * plan.rows, plan.half), jnp.float32),
         pltpu.VMEM((2 * plan.rows, plan.side), jnp.float32),
         pltpu.VMEM((plan.n1s, plan.side), jnp.float32),
     ]
@@ -408,24 +422,29 @@
     constants = [jnp.asarray(table) for table in tables(plan)]
 
     limbs = divisor.reshape(plan.chunk * plan.cols, LANES)
+    spectra = reciprocal_spectra.reshape(2 * rounds, freq_rows, plane)
+    first, twist, second, near, held, facing, rim = prepare(plan)(*map(far, constants + [limbs, spectra]))
+    bundled, rim = bundle(plan)(near, rim)
     pieces = {0: limbs}
     bit = quarters // 2
     while bit:
-        pieces.update({index | bit: swapped(piece, bit) for index, piece in list(pieces.items())})
+        for index, piece in list(pieces.items()):
+            pieces[index | bit] = swapped(bundled if bit == 1 and index == 0 else piece, bit)
         bit //= 2
-    spectra = reciprocal_spectra.reshape(2 * rounds, freq_rows, plane)
-    first, twist, second, near, held, facing = prepare(plan)(*map(far, constants + [limbs, spectra]))
     pieces[0] = near
-    facing = swapped(opposite(plan)(facing), quarters - 1)
-    last, own, own_real, own_imag = resident(plan)(first, held)
+    facing = swapped(opposite(plan)(facing, pieces[1]), quarters - 1)
+    rides = quarters <= 4
+    if not rides:
+        rim = lax.ppermute(rim, "acc", [(source, -source % quarters) for source in range(quarters)])
+    last, own = resident(plan)(first, held)
 
     own_spectrum = forward(plan)(*[pieces[index] for index in range(quarters)], first, twist, second)
-    own = blend(plan)(own, facing)
+    own = blend(plan, rides)(own, facing, rim)
     if plan.per > 1:
         first_row = lax.axis_index(("blk", "tail")) % plan.per * plan.slice_rows
         own = lax.dynamic_slice_in_dim(own, first_row, plan.slice_rows, 2)
     every = lax.all_to_all(own_spectrum, ("blk", "tail"), 0, 0, tiled=True)
-    sums = combine(plan)(every, own, own_real, own_imag)
+    sums = combine(plan)(every, own)
     back = lax.all_to_all(sums, ("blk", "tail"), 0, 0, tiled=True)
     slots = backward(plan)(back, last, twist, second)
 

time: 50.5 us -> 47.3 us (0.937)
  blocking collectives: 14 us -> 12.2 us
  waiting for transfers between devices: 17.2 us -> 15.8 us
  starting transfers between devices: 12.1 us -> 11.5 us
    all_to_all x1, blocking collectives: 14 us -> 12.2 us  [per_device(): back = lax.all_to_all(sums, ('blk', 'tail'), 0, 0, tiled=True)]
    all_to_all x1, waiting for transfers between devices: 4.25 us -> 2.82 us  [per_device(): every = lax.all_to_all(own_spectrum, ('blk', 'tail'), 0, 0, tiled=True)]
    ppermute x6, starting transfers between devices: 5.98 us -> 5.4 us  [swapped(): lax.ppermute(value, 'acc', [(source, source ^ bit) for source in range(co...]
    pallas_call x4 -> x5, Pallas kernels: 1.25 us -> 1.33 us  [the longest x1 0.37 us: per_device(): own = blend(plan, rides)(own, facing, rim)]
  transfers between devices with their start and end apart: 7 -> 7, of which waited for: 5 -> 7; matrix products, arithmetic and copies ran while one was open for 0% -> 0% of each run, Pallas kernels for 6% -> 7%
where the time goes in v2:
time: 47.3 us; the launch traced here: 47 us
  waiting for transfers between devices  15.8 us (33%)
  blocking collectives  12.2 us (26%)
  starting transfers between devices  11.5 us (24%)
  Pallas kernels  6.65 us (14%)
  other arithmetic  0.72 us (2%)
    ppermute x6, waiting for transfers between devices, swapped(): lax.ppermute(value, 'acc', [(source, source ^ bit) for source in range(co...  12.9 us
    all_to_all x1, blocking collectives, per_device(): back = lax.all_to_all(sums, ('blk', 'tail'), 0, 0, tiled=True)  12.2 us
    all_to_all x1, starting transfers between devices, per_device(): every = lax.all_to_all(own_spectrum, ('blk', 'tail'), 0, 0, tiled=True)  6.09 us
    ppermute x6, starting transfers between devices, swapped(): lax.ppermute(value, 'acc', [(source, source ^ bit) for source in range(co...  5.4 us
    all_to_all x1, waiting for transfers between devices, per_device(): every = lax.all_to_all(own_spectrum, ('blk', 'tail'), 0, 0, tiled=True)  2.82 us
    pallas_call x1, Pallas kernels, per_device(): prepare(plan)(*map(far, constants + [limbs, spectra]))  2.2 us
    pallas_call x1, Pallas kernels, per_device(): forward(plan)  2.03 us
    pallas_call x1, Pallas kernels, per_device(): slots = backward(plan)(back, last, twist, second)  1.09 us
  transfers between devices with their start and end apart: 7, of which 7 were waited for; matrix products, arithmetic and copies ran while one was open for 0% of the time, Pallas kernels for 7%

profile of v2, /device:TPU:0, one launch (start us, length us, event | category | flops | bytes accessed | tf_op | source)
XLA Modules:
  0.0 47.0 jit_solution(2262261162201243077)
XLA Ops:
  0.0 3.0 %collective-permute-start.1 = (f32[256,128]{1,0:T(8,128)}, f32[256,128]{1,0:T(8,128)S(1)}, u32[]{:S(2)}, u32[]{:S(2)}) collective-permute-start(f32[256,128]{1,0:T(8,128)} %bitcast.4), channel_id=1, source_target_pairs={{0,4},{2,6},{4,0},{6,2},{1,5},{3,7},{5,1},{7,3},{8,12},{10,14},{12... | collective-permute-start | bytes 393224 | tf_op jit(solution)/shard_map/ppermute | solution.py:414
  3.0 2.2 %shard_map.73 = (bf16[2,256,256]{2,1,0:T(8,128)(2,1)S(1)}, f32[2,128,512]{2,1,0:T(8,128)S(1)}, bf16[2,512,512]{2,1,0:T(8,128)(2,1)S(1)}, f32[256,128]{1,0:T(8,12...) custom-call(f32[2,128,256]{2,1,0:T(8,128)} %constant.10.clone.refs_0_, ...), custom_call_target="tpu_custom_call" | custom-call | flops 1000000 | bytes 1000000 | tf_op jit(solution)/shard_map/pallas_call | solution.py:426
  5.2 0.2 shard_map.74
  5.3 0.1 collective-permute-start
  5.4 1.2 %collective-permute-done.1.refs_2_ = f32[256,128]{1,0:T(8,128)S(1)} collective-permute-done((f32[256,128]{1,0:T(8,128)}, f32[256,128]{1,0:T(8,128)S(1)}, u32[]{:S(2)}, u32[]{:S(2)}) %collective-permute-start.1) | collective-permute-done | bytes 131104 | tf_op jit(solution)/shard_map/ppermute | solution.py:414
  6.7 0.0 collective-permute-start.2
  6.7 0.1 collective-permute-done.refs_1_.other
  6.8 1.3 %collective-permute-done.2.refs_3_ = f32[256,128]{1,0:T(8,128)S(1)} collective-permute-done((f32[256,128]{1,0:T(8,128)S(1)}, f32[256,128]{1,0:T(8,128)S(1)}, u32[]{:S(2)}, u32[]{:S(2)}) %collective-permute-start.2) | collective-permute-done | bytes 131104 | tf_op jit(solution)/shard_map/ppermute | solution.py:414
  8.0 2.0 %shard_map.75 = f32[8,64,128]{2,1,0:T(8,128)} custom-call(f32[256,128]{1,0:T(8,128)S(1)} %get-tuple-element.16.near.refs_0_, f32[272,128]{1,0:T(8,128)S(1)} %collective-permute-done.refs_1_.other, f32[256,128]{1,0:T(8,128)S(1)} %collective-permute-done.1.refs_2_, f32[256,128]{1,0:T(8,128)S(1)} %collective-permute-done.2.refs_3_, ...), custom_call_target="tpu_custom_call" | custom-call | flops 1000000 | bytes 1000000 | tf_op jit(solution)/shard_map/pallas_call | solution.py:441
  10.0 6.1 %all-to-all-start = ((f32[8,64,128]{2,1,0:T(8,128)}), f32[8,64,128]{2,1,0:T(8,128)S(1)}, u32[]{:S(2)}, u32[]{:S(2)}) async-start(f32[8,64,128]{2,1,0:T(8,128)} %shard_map.75), calls=%async_computation | async-start | bytes 524288 | tf_op jit(solution)/shard_map/all_to_all | solution.py:446
  16.1 0.2 shard_map.77
  16.4 1.0 %collective-permute-start.3 = (f32[8,16,256]{2,1,0:T(8,128)S(1)}, f32[8,16,256]{2,1,0:T(8,128)S(1)}, u32[]{:S(2)}, u32[]{:S(2)}) collective-permute-start(f32[8,16,256]{2,1,0:T(8,128)S(1)} %shard_map.77), channel_id=1, source_target_pairs={{0,6},{2,4},{4,2},{6,0},{1,7},{3,5},{5,3},{7,1},{8,14},{10,12},{12... | collective-permute-start | bytes 393224 | tf_op jit(solution)/shard_map/ppermute | solution.py:414
  17.4 0.3 shard_map.76
  17.7 4.5 %collective-permute-done.3.arrived = f32[8,16,256]{2,1,0:T(8,128)S(1)} collective-permute-done((f32[8,16,256]{2,1,0:T(8,128)S(1)}, f32[8,16,256]{2,1,0:T(8,128)S(1)}, u32[]{:S(2)}, u32[]{:S(2)}) %collective-permute-start.3) | collective-permute-done | bytes 131104 | tf_op jit(solution)/shard_map/ppermute | solution.py:414
  22.2 0.4 shard_map.78.own
  22.5 2.8 %all-to-all-done.spectra = f32[8,64,128]{2,1,0:T(8,128)S(1)} async-done(((f32[8,64,128]{2,1,0:T(8,128)}), f32[8,64,128]{2,1,0:T(8,128)S(1)}, u32[]{:S(2)}, u32[]{:S(2)}) %all-to-all-start) | async-done | bytes 262176 | tf_op jit(solution)/shard_map/all_to_all | solution.py:446
  25.4 0.3 shard_map.79
  25.7 12.2 %all_to_all.10.spectra = f32[8,64,128]{2,1,0:T(8,128)S(1)} all-to-all(f32[8,64,128]{2,1,0:T(8,128)S(1)} %shard_map.79), channel_id=1, replica_groups=mesh['blk'=4,'acc'=4,'tail'=2] {'blk','tail'}, dimensions={0} | all-to-all | bytes 524288 | tf_op jit(solution)/shard_map/all_to_all | solution.py:448
  37.9 1.1 %shard_map.80 = f32[4,256,128]{2,1,0:T(8,128)S(1)} custom-call(f32[8,64,128]{2,1,0:T(8,128)S(1)} %all_to_all.10.spectra, bf16[2,256,256]{2,1,0:T(8,128)(2,1)S(1)} %get-tuple-element.26.last, f32[2,128,512]{2,1,0:T(8,128)S(1)} %get-tuple-element.20.refs_5_.twist, bf16[2,512,512]{2,1,0:T(8,128)(2,1)S(1)} %get-tuple-element.21.refs_6_.second), custom_call_target="tpu_custom_call" | custom-call | flops 1000000 | bytes 1000000 | tf_op jit(solution)/shard_map/pallas_call | solution.py:449
  39.1 0.1 collective-permute-start.4
  39.2 1.5 %collective-permute-done.4 = f32[2,256,128]{2,1,0:T(8,128)S(1)} collective-permute-done((f32[2,256,128]{2,1,0:T(8,128)S(1)}, f32[2,256,128]{2,1,0:T(8,128)S(1)}, u32[]{:S(2)}, u32[]{:S(2)}) %collective-permute-start.4) | collective-permute-done | bytes 262176 | tf_op jit(solution)/shard_map/ppermute | solution.py:414
  40.7 1.3 %collective-permute-start.5 = (f32[1,256,128]{2,1,0:T(8,128)S(1)}, f32[1,256,128]{2,1,0:T(8,128)S(1)}, u32[]{:S(2)}, u32[]{:S(2)}) collective-permute-start(f32[1,256,128]{2,1,0:T(8,128)S(1)} %slice_add_fusion), channel_id=1, source_target_pairs={{0,4},{2,6},{4,0},{6,2},{1,5},{3,7},{5,1},{7,3},{8,12},{10,14},{12... | collective-permute-start | bytes 393224 | tf_op jit(solution)/shard_map/ppermute | solution.py:414
  42.0 4.3 %collective-permute-done.5 = f32[1,256,128]{2,1,0:T(8,128)S(1)} collective-permute-done((f32[1,256,128]{2,1,0:T(8,128)S(1)}, f32[1,256,128]{2,1,0:T(8,128)S(1)}, u32[]{:S(2)}, u32[]{:S(2)}) %collective-permute-start.5) | collective-permute-done | bytes 131104 | tf_op jit(solution)/shard_map/ppermute | solution.py:414
  46.3 0.7 %fusion = f32[1,256,128]{2,1,0:T(8,128)} fusion(f32[1,256,128]{2,1,0:T(8,128)S(1)} %collective-permute-done.5, f32[2,256,128]{2,1,0:T(8,128)S(1)} %collective-permute-done.4, f32[4,256,128]{2,1,0:T(8,128)S(1)} %shard_map.80), kind=kLoop, calls=%fused_computation.3 | loop fusion | flops 65536 | bytes 524288 | tf_op jit(solution)/shard_map/add | solution.py:456
  (3 shorter events, 0.1 us)
Async XLA Ops:
  0.0 6.7 %collective-permute-start.1 = (f32[256,128]{1,0:T(8,128)}, f32[256,128]{1,0:T(8,128)S(1)}, u32[]{:S(2)}, u32[]{:S(2)}) collective-permute-start(f32[256,128]{1,0:T(8,128)} %bitcast.4), channel_id=1, source_target_pairs={{0,4},{2,6},{4,0},{6,2},{1,5},{3,7},{5,1},{7,3},{8,12},{10,14},{12... | collective-permute-start | bytes 393224 | tf_op jit(solution)/shard_map/ppermute | solution.py:414
  5.3 1.4 %collective-permute-start = (f32[272,128]{1,0:T(8,128)S(1)}, f32[272,128]{1,0:T(8,128)S(1)}, u32[]{:S(2)}, u32[]{:S(2)}) collective-permute-start(f32[272,128]{1,0:T(8,128)S(1)} %get-tuple-element.18), channel_id=1, source_target_pairs={{0,2},{2,0},{4,6},{6,4},{1,3},{3,1},{5,7},{7,5},{8,10},{10,8},{12,... | collective-permute-start | bytes 417800 | tf_op jit(solution)/shard_map/ppermute | solution.py:414
  6.7 1.3 %collective-permute-start.2 = (f32[256,128]{1,0:T(8,128)S(1)}, f32[256,128]{1,0:T(8,128)S(1)}, u32[]{:S(2)}, u32[]{:S(2)}) collective-permute-start(f32[256,128]{1,0:T(8,128)S(1)} %collective-permute-done.1.refs_2_), channel_id=1, source_target_pairs={{0,2},{2,0},{4,6},{6,4},{1,3},{3,1},{5,7},{7,5},{8,10},{10,8},{12,... | collective-permute-start | bytes 393224 | tf_op jit(solution)/shard_map/ppermute | solution.py:414
  10.0 15.3 %all-to-all-start = ((f32[8,64,128]{2,1,0:T(8,128)}), f32[8,64,128]{2,1,0:T(8,128)S(1)}, u32[]{:S(2)}, u32[]{:S(2)}) async-start(f32[8,64,128]{2,1,0:T(8,128)} %shard_map.75), calls=%async_computation | async-start | bytes 524288 | tf_op jit(solution)/shard_map/all_to_all | solution.py:446
  16.4 5.8 %collective-permute-start.3 = (f32[8,16,256]{2,1,0:T(8,128)S(1)}, f32[8,16,256]{2,1,0:T(8,128)S(1)}, u32[]{:S(2)}, u32[]{:S(2)}) collective-permute-start(f32[8,16,256]{2,1,0:T(8,128)S(1)} %shard_map.77), channel_id=1, source_target_pairs={{0,6},{2,4},{4,2},{6,0},{1,7},{3,5},{5,3},{7,1},{8,14},{10,12},{12... | collective-permute-start | bytes 393224 | tf_op jit(solution)/shard_map/ppermute | solution.py:414
  39.1 1.6 %collective-permute-start.4 = (f32[2,256,128]{2,1,0:T(8,128)S(1)}, f32[2,256,128]{2,1,0:T(8,128)S(1)}, u32[]{:S(2)}, u32[]{:S(2)}) collective-permute-start(f32[2,256,128]{2,1,0:T(8,128)S(1)} %pad_maximum_fusion), channel_id=1, source_target_pairs={{0,2},{2,0},{4,6},{6,4},{1,3},{3,1},{5,7},{7,5},{8,10},{10,8},{12,... | collective-permute-start | bytes 786440 | tf_op jit(solution)/shard_map/ppermute | solution.py:414
  40.7 5.6 %collective-permute-start.5 = (f32[1,256,128]{2,1,0:T(8,128)S(1)}, f32[1,256,128]{2,1,0:T(8,128)S(1)}, u32[]{:S(2)}, u32[]{:S(2)}) collective-permute-start(f32[1,256,128]{2,1,0:T(8,128)S(1)} %slice_add_fusion), channel_id=1, source_target_pairs={{0,4},{2,6},{4,0},{6,2},{1,5},{3,7},{5,1},{7,3},{8,12},{10,14},{12... | collective-permute-start | bytes 393224 | tf_op jit(solution)/shard_map/ppermute | solution.py:414

commit v3 on v2

--- a/solution.py
+++ b/solution.py
@@ -11,6 +11,7 @@
 
 LANES = 128
 TILE = 8
+PIECES = 2
 GRANT = 16 * 1024 * 1024
 STRIDE = 2
 
@@ -94,14 +95,14 @@
     return dot(first[0], second[0]) + (dot(first[1], second[0]) + dot(first[0], second[1]))
 
 
-def call(kernel, out_shape, memory, scratch=(), flops=1_000_000, moved=1_000_000):
+def call(kernel, out_shape, memory, scratch=(), result="vmem", flops=1_000_000, moved=1_000_000):
     where = {"vmem": pltpu.VMEM, "hbm": pltpu.HBM}
-    vmem = pl.BlockSpec(memory_space=pltpu.VMEM)
+    out_spec = pl.BlockSpec(memory_space=where[result])
     return pl.pallas_call(
         kernel,
         out_shape=out_shape,
         in_specs=[pl.BlockSpec(memory_space=where[kind]) for kind in memory],
-        out_specs=jax.tree.map(lambda _: vmem, out_shape),
+        out_specs=jax.tree.map(lambda _: out_spec, out_shape),
         scratch_shapes=scratch,
         cost_estimate=pl.CostEstimate(flops=flops, bytes_accessed=moved, transcendentals=0),
         compiler_params=pltpu.CompilerParams(vmem_limit_bytes=GRANT),
@@ -152,20 +153,40 @@
     return call(kernel, out_shape, ["vmem"] * 2)
 
 
+def flipped(plan, value):
+    row = lax.broadcasted_iota(jnp.int32, (plan.half, plan.half), 0)
+    column = lax.broadcasted_iota(jnp.int32, (plan.half, plan.half), 1)
+    flip = jnp.where(row + column == plan.half - 1, 1.0, 0.0).astype(jnp.bfloat16)
+    high, low = value
+    dot = lambda a: jnp.dot(a, flip, preferred_element_type=jnp.float32)
+    return dot(high) + dot(low)
+
+
 def opposite(plan):
-    def kernel(held, other, out):
+    def kernel(held, other, out, stack):
         m_lo = plan.m_los - 1 - spot(plan)[1]
         within = m_lo * plan.radix % LANES + plan.radix // 2
         base = plan.chunk * plan.cols
+        rows = plan.freq_rows
         for index in range(2 * plan.rounds):
             for column in range(plan.half_cols):
                 lanes = slice(column * LANES, (column + 1) * LANES)
-                out[index, :, lanes] = gathered(plan, held, index, column, within, plan.freq_rows)
+                stack[index * rows : (index + 1) * rows, lanes] = gathered(plan, held, index, column, within, rows)
                 row = base + index * plan.half_cols + column
-                out[index, :1, lanes] = other[row : row + 1]
+                stack[index * rows : index * rows + 1, lanes] = other[row : row + 1]
+        count = 2 * plan.rounds * rows
+        row = lax.broadcasted_iota(jnp.int32, (count, count), 0)
+        column = lax.broadcasted_iota(jnp.int32, (count, count), 1)
+        inside = row % rows
+        target = jnp.where(inside == 0, row, 2 * (row - inside) + rows - row)
+        turn = jnp.where(column == target, 1.0, 0.0).astype(jnp.bfloat16)
+        dot = lambda a: jnp.dot(turn, a, preferred_element_type=jnp.float32).astype(jnp.bfloat16)
+        high, low = split(stack[...])
+        out[...] = flipped(plan, (dot(high), dot(low))).reshape(out.shape)
 
     shape = jax.ShapeDtypeStruct((2 * plan.rounds, plan.freq_rows, plan.half), jnp.float32)
-    return call(kernel, shape, ["vmem"] * 2)
+    scratch = [pltpu.VMEM((2 * plan.rounds * plan.freq_rows, plan.half), jnp.float32)]
+    return call(kernel, shape, ["vmem"] * 2, scratch)
 
 
 def prepare(plan):
@@ -224,51 +245,37 @@
 
 
 def resident(plan):
-    def kernel(first, held, last, own):
-        _, m_lo, _ = spot(plan)
+    def kernel(first, held, rim, last, own, edge):
+        place, m_lo, _ = spot(plan)
         last[0], last[1] = split((first[0].astype(jnp.float32) + first[1].astype(jnp.float32)).T)
         within = m_lo * plan.radix % LANES
         for index in range(2 * plan.rounds):
             for column in range(plan.half_cols):
                 own[index, column] = gathered(plan, held, index, column, within, plan.freq_rows)
+        value = flipped(plan, split(rim[...]))
+        lane = lax.broadcasted_iota(jnp.int32, value.shape, 1)
+        later = pltpu.roll(value, plan.radix // 2, 1)
+        later = jnp.where(lane < plan.radix // 2, pltpu.roll(later, 1, 1), later)
+        edge[...] = jnp.where((place == 0) & (m_lo == 0), later, value)
 
     shape = jax.ShapeDtypeStruct
     out_shape = (
         shape((2, plan.n1s, 2 * plan.rows), jnp.bfloat16),
         shape((2 * plan.rounds, plan.half_cols, plan.freq_rows, LANES), jnp.float32),
+        shape((2 * plan.rounds, plan.half), jnp.float32),
     )
-    return call(kernel, out_shape, ["vmem"] * 2)
+    return call(kernel, out_shape, ["vmem"] * 3)
 
 
 def blend(plan, rides):
-    def kernel(own, arrived, rim, out):
+    def kernel(own, arrived, edge, rim, out):
         place, m_lo, _ = spot(plan)
-        special = (place == 0) & (m_lo == 0)
-        count = 2 * plan.rounds * plan.freq_rows
-        row = lax.broadcasted_iota(jnp.int32, (count, count), 0)
-        column = lax.broadcasted_iota(jnp.int32, (count, count), 1)
-        within = row % plan.freq_rows
-        turn = (row + column == 2 * (row - within) + plan.freq_rows) & (within != 0)
-        turn = jnp.where(turn, 1.0, 0.0).astype(jnp.bfloat16)
-        row = lax.broadcasted_iota(jnp.int32, (plan.half, plan.half), 0)
-        column = lax.broadcasted_iota(jnp.int32, (plan.half, plan.half), 1)
-        flip = jnp.where(row + column == plan.half - 1, 1.0, 0.0).astype(jnp.bfloat16)
-        dot = lambda a, b: jnp.dot(a, b, preferred_element_type=jnp.float32)
-        high, low = split(arrived[...].reshape(count, plan.half))
-        total = dot(dot(turn, high).astype(jnp.bfloat16), flip) + dot(dot(turn, low).astype(jnp.bfloat16), flip)
-        paired = rim[...]
+        corner = lax.broadcasted_iota(jnp.int32, (plan.freq_rows, LANES), 0)
+        top = corner == 0
+        corner = top & (lax.broadcasted_iota(jnp.int32, (plan.freq_rows, LANES), 1) == 0)
+        corner = corner & ((place == 0) & (m_lo == 0))
         if rides:
-            top = jnp.concatenate([arrived[index, :1] for index in range(2 * plan.rounds)], axis=0)
-            paired = jnp.where(lax.rem(place, 2) == 1, top, paired)
-        high, low = split(paired)
-        edge = dot(high, flip) + dot(low, flip)
-        lane = lax.broadcasted_iota(jnp.int32, edge.shape, 1)
-        later = pltpu.roll(edge, plan.radix // 2, 1)
-        later = jnp.where(lane < plan.radix // 2, pltpu.roll(later, 1, 1), later)
-        edge = jnp.where(special, later, edge)
-        top = lax.broadcasted_iota(jnp.int32, (plan.freq_rows, LANES), 0) == 0
-        corner = top & (lax.broadcasted_iota(jnp.int32, (plan.freq_rows, LANES), 1) == 0)
-        corner = corner & special
+            top = top & (lax.rem(place, 2) == 0)
         scale = 1.0 / plan.length
         for step in range(plan.rounds):
             for column in range(plan.half_cols):
@@ -276,8 +283,7 @@
                 whole = []
                 for part in range(2):
                     index = 2 * step + part
-                    there = total[index * plan.freq_rows : (index + 1) * plan.freq_rows, lanes]
-                    there = jnp.where(top, edge[index : index + 1, lanes], there)
+                    there = jnp.where(top, edge[index : index + 1, lanes], arrived[index, :, lanes])
                     here = own[index, column]
                     if column == 0:
                         there = jnp.where(corner, here if part else 0.0, there)
@@ -289,7 +295,7 @@
                 out[3 * step + 2, column] = whole[0]
 
     shape = jax.ShapeDtypeStruct((3 * plan.rounds, plan.half_cols, plan.freq_rows, LANES), jnp.float32)
-    return call(kernel, shape, ["vmem"] * 3)
+    return call(kernel, shape, ["vmem"] * 4)
 
 
 def alternating(plan, count):
@@ -305,7 +311,7 @@
 def forward(plan):
     def kernel(*refs):
         limbs = refs[: plan.quarters]
-        first, twist, second, out, matrix, turned = refs[plan.quarters :]
+        first, twist, second, out, matrix, turned, packed, sems = refs[plan.quarters :]
         place = spot(plan)[0]
         for index in range(plan.quarters):
             start = pl.multiple_of((place ^ index) * plan.chunk, 8)
@@ -320,26 +326,40 @@
         turned[rows:] = real * twist[1] + imag * twist[0]
         middle = jnp.sum(turned[:1] * alternating(plan, 1), axis=1, keepdims=True)
         middle = jnp.where(place == 0, middle, 0.0)
-        value = product(split(turned[...]), (second[0], second[1]))
-        by_cos, by_sin = value[:, : plan.half], value[:, plan.half :]
-        main = (by_cos[:rows] + by_sin[rows:], by_cos[rows:] - by_sin[:rows])
         corner = lax.broadcasted_iota(jnp.int32, (plan.slice_rows, LANES), 0) == 0
         corner = corner & (lax.broadcasted_iota(jnp.int32, (plan.slice_rows, LANES), 1) == 0)
-        for group in range(plan.groups):
-            for part in range(2):
-                for column in range(plan.half_cols):
-                    lanes = slice(column * LANES, (column + 1) * LANES)
-                    tile = main[part][group * plan.slice_rows : (group + 1) * plan.slice_rows, lanes]
-                    if (group, part, column) == (0, 1, 0):
-                        tile = tile + jnp.where(corner, middle, 0.0)
-                    out[group, packed_rows(plan, part, column)] = tile
+        table = (second[0], second[1])
+        count, groups = rows // PIECES, plan.groups // PIECES
+        copies = []
+        for piece in range(PIECES):
+            start = piece * count
+            both = jnp.concatenate([turned[start : start + count], turned[rows + start : rows + start + count]], axis=0)
+            value = product(split(both), table)
+            by_cos, by_sin = value[:, : plan.half], value[:, plan.half :]
+            main = (by_cos[:count] + by_sin[count:], by_cos[count:] - by_sin[:count])
+            for index in range(groups):
+                group = piece * groups + index
+                for part in range(2):
+                    for column in range(plan.half_cols):
+                        lanes = slice(column * LANES, (column + 1) * LANES)
+                        tile = main[part][index * plan.slice_rows : (index + 1) * plan.slice_rows, lanes]
+                        if (group, part, column) == (0, 1, 0):
+                            tile = tile + jnp.where(corner, middle, 0.0)
+                        packed[group, packed_rows(plan, part, column)] = tile
+            where = pl.ds(piece * groups, groups)
+            copies.append(pltpu.make_async_copy(packed.at[where], out.at[where], sems.at[piece]))
+            copies[-1].start()
+        for copy in copies:
+            copy.wait()
 
     shape = jax.ShapeDtypeStruct((plan.groups, plan.packed, LANES), jnp.float32)
     scratch = [
         pltpu.VMEM((plan.n1s, plan.side), jnp.float32),
         pltpu.VMEM((2 * plan.rows, plan.side), jnp.float32),
+        pltpu.VMEM((plan.groups, plan.packed, LANES), jnp.float32),
+        pltpu.SemaphoreType.DMA((PIECES,)),
     ]
-    return call(kernel, shape, ["vmem"] * (plan.quarters + 3), scratch)
+    return call(kernel, shape, ["vmem"] * (plan.quarters + 3), scratch, "hbm")
 
 
 def combine(plan):
@@ -432,14 +452,15 @@
             pieces[index | bit] = swapped(bundled if bit == 1 and index == 0 else piece, bit)
         bit //= 2
     pieces[0] = near
-    facing = swapped(opposite(plan)(facing, pieces[1]), quarters - 1)
+    facing = opposite(plan)(facing, pieces[1])
+    facing = swapped(facing, quarters - 1)
     rides = quarters <= 4
     if not rides:
         rim = lax.ppermute(rim, "acc", [(source, -source % quarters) for source in range(quarters)])
-    last, own = resident(plan)(first, held)
+    last, own, edge = resident(plan)(first, held, rim)
 
     own_spectrum = forward(plan)(*[pieces[index] for index in range(quarters)], first, twist, second)
-    own = blend(plan, rides)(own, facing, rim)
+    own = blend(plan, rides)(own, facing, edge, rim)
     if plan.per > 1:
         first_row = lax.axis_index(("blk", "tail")) % plan.per * plan.slice_rows
         own = lax.dynamic_slice_in_dim(own, first_row, plan.slice_rows, 2)

time: 47.3 us -> 46.9 us (level)
  no operation moved by 1% of the time
where the time goes in v3:
time: 46.9 us; the launch traced here: 46.6 us
  waiting for transfers between devices  15.8 us (34%)
  blocking collectives  12.2 us (26%)
  starting transfers between devices  11.6 us (25%)
  Pallas kernels  6.28 us (13%)
  other arithmetic  0.72 us (2%)
    ppermute x6, waiting for transfers between devices, swapped(): lax.ppermute(value, 'acc', [(source, source ^ bit) for source in range(co...  12.9 us
    all_to_all x1, blocking collectives, per_device(): back = lax.all_to_all(sums, ('blk', 'tail'), 0, 0, tiled=True)  12.2 us
    all_to_all x1, starting transfers between devices, per_device(): every = lax.all_to_all(own_spectrum, ('blk', 'tail'), 0, 0, tiled=True)  6.1 us
    ppermute x6, starting transfers between devices, swapped(): lax.ppermute(value, 'acc', [(source, source ^ bit) for source in range(co...  5.46 us
    all_to_all x1, waiting for transfers between devices, per_device(): every = lax.all_to_all(own_spectrum, ('blk', 'tail'), 0, 0, tiled=True)  2.87 us
    pallas_call x1, Pallas kernels, per_device(): prepare(plan)(*map(far, constants + [limbs, spectra]))  2.2 us
    pallas_call x1, Pallas kernels, per_device(): forward(plan)  1.69 us
    pallas_call x1, Pallas kernels, per_device(): slots = backward(plan)(back, last, twist, second)  1.09 us
  transfers between devices with their start and end apart: 7, of which 7 were waited for; matrix products, arithmetic and copies ran while one was open for 0% of the time, Pallas kernels for 7%

profile of v3, /device:TPU:0, one launch (start us, length us, event | category | flops | bytes accessed | tf_op | source)
XLA Modules:
  0.0 46.6 jit_solution(17281919225035312256)
XLA Ops:
  0.0 3.0 %collective-permute-start.1 = (f32[256,128]{1,0:T(8,128)}, f32[256,128]{1,0:T(8,128)S(1)}, u32[]{:S(2)}, u32[]{:S(2)}) collective-permute-start(f32[256,128]{1,0:T(8,128)} %bitcast.4), channel_id=1, source_target_pairs={{0,4},{2,6},{4,0},{6,2},{1,5},{3,7},{5,1},{7,3},{8,12},{10,14},{12... | collective-permute-start | bytes 393224 | tf_op jit(solution)/shard_map/ppermute | solution.py:434
  3.0 2.2 %shard_map.73 = (bf16[2,256,256]{2,1,0:T(8,128)(2,1)S(1)}, f32[2,128,512]{2,1,0:T(8,128)S(1)}, bf16[2,512,512]{2,1,0:T(8,128)(2,1)S(1)}, f32[256,128]{1,0:T(8,12...) custom-call(f32[2,128,256]{2,1,0:T(8,128)} %constant.10.clone.refs_0_, ...), custom_call_target="tpu_custom_call" | custom-call | flops 1000000 | bytes 1000000 | tf_op jit(solution)/shard_map/pallas_call | solution.py:446
  5.2 0.2 shard_map.74
  5.3 0.1 collective-permute-start
  5.4 1.2 %collective-permute-done.1.refs_2_ = f32[256,128]{1,0:T(8,128)S(1)} collective-permute-done((f32[256,128]{1,0:T(8,128)}, f32[256,128]{1,0:T(8,128)S(1)}, u32[]{:S(2)}, u32[]{:S(2)}) %collective-permute-start.1) | collective-permute-done | bytes 131104 | tf_op jit(solution)/shard_map/ppermute | solution.py:434
  6.7 0.0 collective-permute-start.2
  6.7 0.1 collective-permute-done.refs_1_.other
  6.8 1.3 %collective-permute-done.2.refs_3_ = f32[256,128]{1,0:T(8,128)S(1)} collective-permute-done((f32[256,128]{1,0:T(8,128)S(1)}, f32[256,128]{1,0:T(8,128)S(1)}, u32[]{:S(2)}, u32[]{:S(2)}) %collective-permute-start.2) | collective-permute-done | bytes 131104 | tf_op jit(solution)/shard_map/ppermute | solution.py:434
  8.0 1.7 %shard_map.75 = f32[8,64,128]{2,1,0:T(8,128)} custom-call(f32[256,128]{1,0:T(8,128)S(1)} %get-tuple-element.17.near.refs_0_, f32[272,128]{1,0:T(8,128)S(1)} %collective-permute-done.refs_1_.other, f32[256,128]{1,0:T(8,128)S(1)} %collective-permute-done.1.refs_2_, f32[256,128]{1,0:T(8,128)S(1)} %collective-permute-done.2.refs_3_, ...), custom_call_target="tpu_custom_call" | custom-call | flops 1000000 | bytes 1000000 | tf_op jit(solution)/shard_map/pallas_call | solution.py:462
  9.7 6.1 %all-to-all-start = ((f32[8,64,128]{2,1,0:T(8,128)}), f32[8,64,128]{2,1,0:T(8,128)S(1)}, u32[]{:S(2)}, u32[]{:S(2)}) async-start(f32[8,64,128]{2,1,0:T(8,128)} %shard_map.75), calls=%async_computation | async-start | bytes 524288 | tf_op jit(solution)/shard_map/all_to_all | solution.py:467
  15.8 0.5 %shard_map.77 = f32[8,16,256]{2,1,0:T(8,128)S(1)} custom-call(f32[8,8,16,128]{3,2,1,0:T(8,128)S(1)} %get-tuple-element.26.held, f32[272,128]{1,0:T(8,128)S(1)} %collective-permute-done.refs_1_.other), custom_call_target="tpu_custom_call" | custom-call | flops 1000000 | bytes 1000000 | tf_op jit(solution)/shard_map/pallas_call | solution.py:455
  16.3 1.0 %collective-permute-start.3 = (f32[8,16,256]{2,1,0:T(8,128)S(1)}, f32[8,16,256]{2,1,0:T(8,128)S(1)}, u32[]{:S(2)}, u32[]{:S(2)}) collective-permute-start(f32[8,16,256]{2,1,0:T(8,128)S(1)} %shard_map.77), channel_id=1, source_target_pairs={{0,6},{2,4},{4,2},{6,0},{1,7},{3,5},{5,3},{7,1},{8,14},{10,12},{12... | collective-permute-start | bytes 393224 | tf_op jit(solution)/shard_map/ppermute | solution.py:434
  17.4 0.3 shard_map.76
  17.7 4.5 %collective-permute-done.3.arrived = f32[8,16,256]{2,1,0:T(8,128)S(1)} collective-permute-done((f32[8,16,256]{2,1,0:T(8,128)S(1)}, f32[8,16,256]{2,1,0:T(8,128)S(1)}, u32[]{:S(2)}, u32[]{:S(2)}) %collective-permute-start.3) | collective-permute-done | bytes 131104 | tf_op jit(solution)/shard_map/ppermute | solution.py:434
  22.2 2.9 %all-to-all-done.spectra = f32[8,64,128]{2,1,0:T(8,128)S(1)} async-done(((f32[8,64,128]{2,1,0:T(8,128)}), f32[8,64,128]{2,1,0:T(8,128)S(1)}, u32[]{:S(2)}, u32[]{:S(2)}) %all-to-all-start) | async-done | bytes 262176 | tf_op jit(solution)/shard_map/all_to_all | solution.py:467
  25.0 0.3 shard_map.79
  25.4 12.2 %all_to_all.10.spectra = f32[8,64,128]{2,1,0:T(8,128)S(1)} all-to-all(f32[8,64,128]{2,1,0:T(8,128)S(1)} %shard_map.79), channel_id=1, replica_groups=mesh['blk'=4,'acc'=4,'tail'=2] {'blk','tail'}, dimensions={0} | all-to-all | bytes 524288 | tf_op jit(solution)/shard_map/all_to_all | solution.py:469
  37.6 1.1 %shard_map.80 = f32[4,256,128]{2,1,0:T(8,128)S(1)} custom-call(f32[8,64,128]{2,1,0:T(8,128)S(1)} %all_to_all.10.spectra, bf16[2,256,256]{2,1,0:T(8,128)(2,1)S(1)} %get-tuple-element.28.last, f32[2,128,512]{2,1,0:T(8,128)S(1)} %get-tuple-element.21.refs_5_.twist, bf16[2,512,512]{2,1,0:T(8,128)(2,1)S(1)} %get-tuple-element.22.refs_6_.second), custom_call_target="tpu_custom_call" | custom-call | flops 1000000 | bytes 1000000 | tf_op jit(solution)/shard_map/pallas_call | solution.py:470
  38.7 0.1 collective-permute-start.4
  38.8 1.5 %collective-permute-done.4 = f32[2,256,128]{2,1,0:T(8,128)S(1)} collective-permute-done((f32[2,256,128]{2,1,0:T(8,128)S(1)}, f32[2,256,128]{2,1,0:T(8,128)S(1)}, u32[]{:S(2)}, u32[]{:S(2)}) %collective-permute-start.4) | collective-permute-done | bytes 262176 | tf_op jit(solution)/shard_map/ppermute | solution.py:434
  40.3 1.3 %collective-permute-start.5 = (f32[1,256,128]{2,1,0:T(8,128)S(1)}, f32[1,256,128]{2,1,0:T(8,128)S(1)}, u32[]{:S(2)}, u32[]{:S(2)}) collective-permute-start(f32[1,256,128]{2,1,0:T(8,128)S(1)} %slice_add_fusion), channel_id=1, source_target_pairs={{0,4},{2,6},{4,0},{6,2},{1,5},{3,7},{5,1},{7,3},{8,12},{10,14},{12... | collective-permute-start | bytes 393224 | tf_op jit(solution)/shard_map/ppermute | solution.py:434
  41.6 4.3 %collective-permute-done.5 = f32[1,256,128]{2,1,0:T(8,128)S(1)} collective-permute-done((f32[1,256,128]{2,1,0:T(8,128)S(1)}, f32[1,256,128]{2,1,0:T(8,128)S(1)}, u32[]{:S(2)}, u32[]{:S(2)}) %collective-permute-start.5) | collective-permute-done | bytes 131104 | tf_op jit(solution)/shard_map/ppermute | solution.py:434
  45.9 0.7 %fusion = f32[1,256,128]{2,1,0:T(8,128)} fusion(f32[1,256,128]{2,1,0:T(8,128)S(1)} %collective-permute-done.5, f32[2,256,128]{2,1,0:T(8,128)S(1)} %collective-permute-done.4, f32[4,256,128]{2,1,0:T(8,128)S(1)} %shard_map.80), kind=kLoop, calls=%fused_computation.3 | loop fusion | flops 65536 | bytes 524288 | tf_op jit(solution)/shard_map/add | solution.py:477
  (4 shorter events, 0.1 us)
Async XLA Ops:
  0.0 6.7 %collective-permute-start.1 = (f32[256,128]{1,0:T(8,128)}, f32[256,128]{1,0:T(8,128)S(1)}, u32[]{:S(2)}, u32[]{:S(2)}) collective-permute-start(f32[256,128]{1,0:T(8,128)} %bitcast.4), channel_id=1, source_target_pairs={{0,4},{2,6},{4,0},{6,2},{1,5},{3,7},{5,1},{7,3},{8,12},{10,14},{12... | collective-permute-start | bytes 393224 | tf_op jit(solution)/shard_map/ppermute | solution.py:434
  5.3 1.4 %collective-permute-start = (f32[272,128]{1,0:T(8,128)S(1)}, f32[272,128]{1,0:T(8,128)S(1)}, u32[]{:S(2)}, u32[]{:S(2)}) collective-permute-start(f32[272,128]{1,0:T(8,128)S(1)} %get-tuple-element.19), channel_id=1, source_target_pairs={{0,2},{2,0},{4,6},{6,4},{1,3},{3,1},{5,7},{7,5},{8,10},{10,8},{12,... | collective-permute-start | bytes 417800 | tf_op jit(solution)/shard_map/ppermute | solution.py:434
  6.7 1.3 %collective-permute-start.2 = (f32[256,128]{1,0:T(8,128)S(1)}, f32[256,128]{1,0:T(8,128)S(1)}, u32[]{:S(2)}, u32[]{:S(2)}) collective-permute-start(f32[256,128]{1,0:T(8,128)S(1)} %collective-permute-done.1.refs_2_), channel_id=1, source_target_pairs={{0,2},{2,0},{4,6},{6,4},{1,3},{3,1},{5,7},{7,5},{8,10},{10,8},{12,... | collective-permute-start | bytes 393224 | tf_op jit(solution)/shard_map/ppermute | solution.py:434
  9.7 15.3 %all-to-all-start = ((f32[8,64,128]{2,1,0:T(8,128)}), f32[8,64,128]{2,1,0:T(8,128)S(1)}, u32[]{:S(2)}, u32[]{:S(2)}) async-start(f32[8,64,128]{2,1,0:T(8,128)} %shard_map.75), calls=%async_computation | async-start | bytes 524288 | tf_op jit(solution)/shard_map/all_to_all | solution.py:467
  16.3 5.8 %collective-permute-start.3 = (f32[8,16,256]{2,1,0:T(8,128)S(1)}, f32[8,16,256]{2,1,0:T(8,128)S(1)}, u32[]{:S(2)}, u32[]{:S(2)}) collective-permute-start(f32[8,16,256]{2,1,0:T(8,128)S(1)} %shard_map.77), channel_id=1, source_target_pairs={{0,6},{2,4},{4,2},{6,0},{1,7},{3,5},{5,3},{7,1},{8,14},{10,12},{12... | collective-permute-start | bytes 393224 | tf_op jit(solution)/shard_map/ppermute | solution.py:434
  38.7 1.6 %collective-permute-start.4 = (f32[2,256,128]{2,1,0:T(8,128)S(1)}, f32[2,256,128]{2,1,0:T(8,128)S(1)}, u32[]{:S(2)}, u32[]{:S(2)}) collective-permute-start(f32[2,256,128]{2,1,0:T(8,128)S(1)} %pad_maximum_fusion), channel_id=1, source_target_pairs={{0,2},{2,0},{4,6},{6,4},{1,3},{3,1},{5,7},{7,5},{8,10},{10,8},{12,... | collective-permute-start | bytes 786440 | tf_op jit(solution)/shard_map/ppermute | solution.py:434
  40.3 5.6 %collective-permute-start.5 = (f32[1,256,128]{2,1,0:T(8,128)S(1)}, f32[1,256,128]{2,1,0:T(8,128)S(1)}, u32[]{:S(2)}, u32[]{:S(2)}) collective-permute-start(f32[1,256,128]{2,1,0:T(8,128)S(1)} %slice_add_fusion), channel_id=1, source_target_pairs={{0,4},{2,6},{4,0},{6,2},{1,5},{3,7},{5,1},{7,3},{8,12},{10,14},{12... | collective-permute-start | bytes 393224 | tf_op jit(solution)/shard_map/ppermute | solution.py:434

commit v4 on v3

--- a/solution.py
+++ b/solution.py
@@ -191,9 +191,9 @@
 
 def prepare(plan):
     def kernel(*refs):
-        first, twist, second, near, held, facing, rim = refs[7:14]
-        first_rows, first_part, twist_rows, twist_part = refs[14:18]
-        sems, held_sems, facing_sems, rim_sems = refs[18:]
+        first, twist, second, near, facing, rim = refs[7:13]
+        first_rows, first_part, twist_rows, twist_part = refs[13:17]
+        sems, facing_sems, rim_sems = refs[17:]
         place, m_lo, _ = spot(plan)
         targets = (first_rows, first_part, twist_rows, twist_part, second, near)
         copies = [
@@ -201,7 +201,6 @@
             for index, (source, target) in enumerate(zip(refs[:6], targets))
         ]
         copies += fetch(plan, refs[6], facing, facing_sems, plan.m_los - 1 - m_lo, plan.freq_rows)
-        copies += fetch(plan, refs[6], held, held_sems, m_lo, plan.freq_rows)
         copies += fetch(plan, refs[6], rim, rim_sems, rim_m_lo(plan, place, m_lo), TILE)
         for copy in copies:
             copy.start()
@@ -228,7 +227,6 @@
         shape((2, plan.side, 2 * plan.half), jnp.bfloat16),
         shape((plan.chunk * plan.cols, LANES), jnp.float32),
         held_shape(plan, plan.freq_rows),
-        held_shape(plan, plan.freq_rows),
         held_shape(plan, TILE),
     )
     scratch = [
@@ -239,24 +237,28 @@
         pltpu.SemaphoreType.DMA((6,)),
         pltpu.SemaphoreType.DMA((plan.m_his,)),
         pltpu.SemaphoreType.DMA((plan.m_his,)),
-        pltpu.SemaphoreType.DMA((plan.m_his,)),
     ]
     return call(kernel, out_shape, ["hbm"] * 7, scratch)
 
 
 def resident(plan):
-    def kernel(first, held, rim, last, own, edge):
+    def kernel(first, spectra, rim, last, own, edge, held, sems):
         place, m_lo, _ = spot(plan)
+        copies = fetch(plan, spectra, held, sems, m_lo, plan.freq_rows)
+        for copy in copies:
+            copy.start()
         last[0], last[1] = split((first[0].astype(jnp.float32) + first[1].astype(jnp.float32)).T)
-        within = m_lo * plan.radix % LANES
-        for index in range(2 * plan.rounds):
-            for column in range(plan.half_cols):
-                own[index, column] = gathered(plan, held, index, column, within, plan.freq_rows)
         value = flipped(plan, split(rim[...]))
         lane = lax.broadcasted_iota(jnp.int32, value.shape, 1)
         later = pltpu.roll(value, plan.radix // 2, 1)
         later = jnp.where(lane < plan.radix // 2, pltpu.roll(later, 1, 1), later)
         edge[...] = jnp.where((place == 0) & (m_lo == 0), later, value)
+        for copy in copies:
+            copy.wait()
+        within = m_lo * plan.radix % LANES
+        for index in range(2 * plan.rounds):
+            for column in range(plan.half_cols):
+                own[index, column] = gathered(plan, held, index, column, within, plan.freq_rows)
 
     shape = jax.ShapeDtypeStruct
     out_shape = (
@@ -264,7 +266,9 @@
         shape((2 * plan.rounds, plan.half_cols, plan.freq_rows, LANES), jnp.float32),
         shape((2 * plan.rounds, plan.half), jnp.float32),
     )
-    return call(kernel, out_shape, ["vmem"] * 3)
+    held = held_shape(plan, plan.freq_rows)
+    scratch = [pltpu.VMEM(held.shape, held.dtype), pltpu.SemaphoreType.DMA((plan.m_his,))]
+    return call(kernel, out_shape, ["vmem", "hbm", "vmem"], scratch)
 
 
 def blend(plan, rides):
@@ -393,8 +397,19 @@
     return call(kernel, shape, ["vmem"] * 2)
 
 
+def into_slots(plan, place, odd, last, turned, out, matrix):
+    where = [pl.ds(pl.multiple_of((place ^ (2 * slot + odd)) * plan.chunk, 16), plan.chunk) for slot in range(plan.quarters // 2)]
+    rows = [jnp.concatenate([last[part, at, :] for at in where], axis=0) for part in range(2)]
+    matrix[...] = product(rows, turned)
+    for slot in range(plan.quarters // 2):
+        for column in range(plan.cols):
+            out[slot, pl.ds(column, plan.chunk, stride=plan.cols), :] = matrix[
+                slot * plan.chunk : (slot + 1) * plan.chunk, column * LANES : (column + 1) * LANES
+            ]
+
+
 def backward(plan):
-    def kernel(spectra, last, twist, second, out, stack, spread, matrix):
+    def kernel(spectra, last, twist, second, out, turned, stack, spread, matrix):
         place = spot(plan)[0]
         rows = plan.rows
         for part in range(2):
@@ -411,22 +426,31 @@
         middle = jnp.where(place == 0, stack[rows : rows + 1, :1], 0.0)
         spread[:1] = spread[:1] + middle * alternating(plan, 1)
         real, imag = spread[:rows], spread[rows:]
-        turned = jnp.concatenate([real * twist[0] + imag * twist[1], imag * twist[0] - real * twist[1]], axis=0)
-        matrix[...] = product((last[0], last[1]), split(turned))
-        for index in range(plan.quarters):
-            start = pl.multiple_of((place ^ index) * plan.chunk, 8)
-            for column in range(plan.cols):
-                out[index, pl.ds(column, plan.chunk, stride=plan.cols), :] = matrix[
-                    pl.ds(start, plan.chunk), column * LANES : (column + 1) * LANES
-                ]
-
-    shape = jax.ShapeDtypeStruct((plan.quarters, plan.chunk * plan.cols, LANES), jnp.float32)
+        high, low = split(
+            jnp.concatenate([real * twist[0] + imag * twist[1], imag * twist[0] - real * twist[1]], axis=0)
+        )
+        turned[0], turned[1] = high, low
+        into_slots(plan, place, 1, last, (high, low), out, matrix)
+
+    shape = (
+        jax.ShapeDtypeStruct((plan.quarters // 2, plan.chunk * plan.cols, LANES), jnp.float32),
+        jax.ShapeDtypeStruct((2, 2 * plan.rows, plan.side), jnp.bfloat16),
+    )
     scratch = [
         pltpu.VMEM((2 * plan.rows, plan.half), jnp.float32),
         pltpu.VMEM((2 * plan.rows, plan.side), jnp.float32),
-        pltpu.VMEM((plan.n1s, plan.side), jnp.float32),
+        pltpu.VMEM((plan.n1s // 2, plan.side), jnp.float32),
     ]
     return call(kernel, shape, ["vmem"] * 4, scratch)
+
+
+def finish(plan):
+    def kernel(last, turned, out, matrix):
+        into_slots(plan, spot(plan)[0], 0, last, (turned[0], turned[1]), out, matrix)
+
+    shape = jax.ShapeDtypeStruct((plan.quarters // 2, plan.chunk * plan.cols, LANES), jnp.float32)
+    scratch = [pltpu.VMEM((plan.n1s // 2, plan.side), jnp.float32)]
+    return call(kernel, shape, ["vmem"] * 2, scratch)
 
 
 def swapped(value, bit):
@@ -443,7 +467,7 @@
 
     limbs = divisor.reshape(plan.chunk * plan.cols, LANES)
     spectra = reciprocal_spectra.reshape(2 * rounds, freq_rows, plane)
-    first, twist, second, near, held, facing, rim = prepare(plan)(*map(far, constants + [limbs, spectra]))
+    first, twist, second, near, facing, rim = prepare(plan)(*map(far, constants + [limbs, spectra]))
     bundled, rim = bundle(plan)(near, rim)
     pieces = {0: limbs}
     bit = quarters // 2
@@ -457,7 +481,7 @@
     rides = quarters <= 4
     if not rides:
         rim = lax.ppermute(rim, "acc", [(source, -source % quarters) for source in range(quarters)])
-    last, own, edge = resident(plan)(first, held, rim)
+    last, own, edge = resident(plan)(first, far(spectra), rim)
 
     own_spectrum = forward(plan)(*[pieces[index] for index in range(quarters)], first, twist, second)
     own = blend(plan, rides)(own, facing, edge, rim)
@@ -467,10 +491,11 @@
     every = lax.all_to_all(own_spectrum, ("blk", "tail"), 0, 0, tiled=True)
     sums = combine(plan)(every, own)
     back = lax.all_to_all(sums, ("blk", "tail"), 0, 0, tiled=True)
-    slots = backward(plan)(back, last, twist, second)
-
-    held = {index: slots[index] for index in range(quarters)}
-    bit = 1
+    odd, turned = backward(plan)(back, last, twist, second)
+    arrived = swapped(odd, 1)
+    even = finish(plan)(last, turned)
+    held = {2 * slot: even[slot] + arrived[slot] for slot in range(quarters // 2)}
+    bit = 2
     while bit < quarters:
         sent = sorted(index for index in held if index & bit)
         arrived = swapped(jnp.stack([held[index] for index in sent]), bit)

time: 46.9 us -> 46.8 us (level)
  waiting for transfers between devices: 15.8 us -> 14.4 us
  Pallas kernels: 6.28 us -> 7.46 us
    pallas_call x2 -> x3, Pallas kernels: 1.38 us -> 2.79 us  [the longest x1 1.56 us: per_device(): last, own, edge = resident(plan)(first, far(spectra), rim)]
    ppermute x6, waiting for transfers between devices: 12.9 us -> 11.6 us  [swapped(): lax.ppermute(value, 'acc', [(source, source ^ bit) for source in range(co...]
  transfers between devices with their start and end apart: 7 -> 7, of which waited for: 7 -> 6; matrix products, arithmetic and copies ran while one was open for 0% -> 0% of each run, Pallas kernels for 7% -> 10%
where the time goes in v4:
time: 46.8 us; the launch traced here: 46.4 us
  waiting for transfers between devices  14.4 us (31%)
  blocking collectives  12.2 us (26%)
  starting transfers between devices  11.6 us (25%)
  Pallas kernels  7.46 us (16%)
  other arithmetic  0.69 us (1%)
    all_to_all x1, blocking collectives, per_device(): back = lax.all_to_all(sums, ('blk', 'tail'), 0, 0, tiled=True)  12.2 us
    ppermute x6, waiting for transfers between devices, swapped(): lax.ppermute(value, 'acc', [(source, source ^ bit) for source in range(co...  11.6 us
    all_to_all x1, starting transfers between devices, per_device(): every = lax.all_to_all(own_spectrum, ('blk', 'tail'), 0, 0, tiled=True)  6.1 us
    ppermute x6, starting transfers between devices, swapped(): lax.ppermute(value, 'acc', [(source, source ^ bit) for source in range(co...  5.45 us
    all_to_all x1, waiting for transfers between devices, per_device(): every = lax.all_to_all(own_spectrum, ('blk', 'tail'), 0, 0, tiled=True)  2.87 us
    pallas_call x1, Pallas kernels, per_device(): prepare(plan)(*map(far, constants + [limbs, spectra]))  1.97 us
    pallas_call x1, Pallas kernels, per_device(): forward(plan)  1.69 us
    pallas_call x1, Pallas kernels, per_device(): last, own, edge = resident(plan)(first, far(spectra), rim)  1.56 us
  transfers between devices with their start and end apart: 7, of which 6 were waited for; matrix products, arithmetic and copies ran while one was open for 0% of the time, Pallas kernels for 10%

profile of v4, /device:TPU:0, one launch (start us, length us, event | category | flops | bytes accessed | tf_op | source)
XLA Modules:
  0.0 46.4 jit_solution(3994759436432059590)
XLA Ops:
  0.0 3.0 %collective-permute-start.1 = (f32[256,128]{1,0:T(8,128)}, f32[256,128]{1,0:T(8,128)S(1)}, u32[]{:S(2)}, u32[]{:S(2)}) collective-permute-start(f32[256,128]{1,0:T(8,128)} %bitcast.5), channel_id=1, source_target_pairs={{0,4},{2,6},{4,0},{6,2},{1,5},{3,7},{5,1},{7,3},{8,12},{10,14},{12... | collective-permute-start | bytes 393224 | tf_op jit(solution)/shard_map/ppermute | solution.py:458
  3.0 2.0 %shard_map.73 = (bf16[2,256,256]{2,1,0:T(8,128)(2,1)S(1)}, f32[2,128,512]{2,1,0:T(8,128)S(1)}, bf16[2,512,512]{2,1,0:T(8,128)(2,1)S(1)}, f32[256,128]{1,0:T(8,12...) custom-call(f32[2,128,256]{2,1,0:T(8,128)} %constant.10.clone.refs_0_, ...), custom_call_target="tpu_custom_call" | custom-call | flops 1000000 | bytes 1000000 | tf_op jit(solution)/shard_map/pallas_call | solution.py:470
  4.9 0.2 shard_map.74
  5.1 0.1 collective-permute-start
  5.2 1.5 %collective-permute-done.1.refs_2_ = f32[256,128]{1,0:T(8,128)S(1)} collective-permute-done((f32[256,128]{1,0:T(8,128)}, f32[256,128]{1,0:T(8,128)S(1)}, u32[]{:S(2)}, u32[]{:S(2)}) %collective-permute-start.1) | collective-permute-done | bytes 131104 | tf_op jit(solution)/shard_map/ppermute | solution.py:458
  6.7 0.0 collective-permute-start.2
  6.7 0.0 collective-permute-done.refs_1_.other
  6.7 1.3 %collective-permute-done.2.refs_3_ = f32[256,128]{1,0:T(8,128)S(1)} collective-permute-done((f32[256,128]{1,0:T(8,128)S(1)}, f32[256,128]{1,0:T(8,128)S(1)}, u32[]{:S(2)}, u32[]{:S(2)}) %collective-permute-start.2) | collective-permute-done | bytes 131104 | tf_op jit(solution)/shard_map/ppermute | solution.py:458
  8.0 1.7 %shard_map.76 = f32[8,64,128]{2,1,0:T(8,128)} custom-call(f32[256,128]{1,0:T(8,128)S(1)} %get-tuple-element.19.near.refs_0_, f32[272,128]{1,0:T(8,128)S(1)} %collective-permute-done.refs_1_.other, f32[256,128]{1,0:T(8,128)S(1)} %collective-permute-done.1.refs_2_, f32[256,128]{1,0:T(8,128)S(1)} %collective-permute-done.2.refs_3_, ...), custom_call_target="tpu_custom_call" | custom-call | flops 1000000 | bytes 1000000 | tf_op jit(solution)/shard_map/pallas_call | solution.py:486
  9.7 6.1 %all-to-all-start = ((f32[8,64,128]{2,1,0:T(8,128)}), f32[8,64,128]{2,1,0:T(8,128)S(1)}, u32[]{:S(2)}, u32[]{:S(2)}) async-start(f32[8,64,128]{2,1,0:T(8,128)} %shard_map.76), calls=%async_computation | async-start | bytes 524288 | tf_op jit(solution)/shard_map/all_to_all | solution.py:491
  15.8 0.5 %shard_map.77 = f32[8,16,256]{2,1,0:T(8,128)S(1)} custom-call(f32[8,8,16,128]{3,2,1,0:T(8,128)S(1)} %get-tuple-element.27.held, f32[272,128]{1,0:T(8,128)S(1)} %collective-permute-done.refs_1_.other), custom_call_target="tpu_custom_call" | custom-call | flops 1000000 | bytes 1000000 | tf_op jit(solution)/shard_map/pallas_call | solution.py:479
  16.3 1.0 %collective-permute-start.3 = (f32[8,16,256]{2,1,0:T(8,128)S(1)}, f32[8,16,256]{2,1,0:T(8,128)S(1)}, u32[]{:S(2)}, u32[]{:S(2)}) collective-permute-start(f32[8,16,256]{2,1,0:T(8,128)S(1)} %shard_map.77), channel_id=1, source_target_pairs={{0,6},{2,4},{4,2},{6,0},{1,7},{3,5},{5,3},{7,1},{8,14},{10,12},{12... | collective-permute-start | bytes 393224 | tf_op jit(solution)/shard_map/ppermute | solution.py:458
  17.4 1.6 %shard_map.75 = (bf16[2,256,256]{2,1,0:T(8,128)(2,1)S(1)}, f32[8,2,16,128]{3,2,1,0:T(8,128)S(1)}, f32[8,256]{1,0:T(8,128)S(1)}) custom-call(bf16[2,256,256]{2,1,0:T(8,128)(2,1)S(1)} %get-tuple-element.18.first.refs_4_, f32[8,16,4096]{2,1,0:T(8,128)} %bitcast.4, f32[8,256]{1,0:T(8,128)S(1)} %get-tuple-element.21.rim), custom_call_target="tpu_custom_call" | custom-call | flops 1000000 | bytes 1000000 | tf_op jit(solution)/shard_map/pallas_call | solution.py:484
  18.9 3.2 %collective-permute-done.3.arrived = f32[8,16,256]{2,1,0:T(8,128)S(1)} collective-permute-done((f32[8,16,256]{2,1,0:T(8,128)S(1)}, f32[8,16,256]{2,1,0:T(8,128)S(1)}, u32[]{:S(2)}, u32[]{:S(2)}) %collective-permute-start.3) | collective-permute-done | bytes 131104 | tf_op jit(solution)/shard_map/ppermute | solution.py:458
  22.2 2.9 %all-to-all-done.spectra = f32[8,64,128]{2,1,0:T(8,128)S(1)} async-done(((f32[8,64,128]{2,1,0:T(8,128)}), f32[8,64,128]{2,1,0:T(8,128)S(1)}, u32[]{:S(2)}, u32[]{:S(2)}) %all-to-all-start) | async-done | bytes 262176 | tf_op jit(solution)/shard_map/all_to_all | solution.py:491
  25.0 0.3 shard_map.79
  25.4 12.2 %all_to_all.10.spectra = f32[8,64,128]{2,1,0:T(8,128)S(1)} all-to-all(f32[8,64,128]{2,1,0:T(8,128)S(1)} %shard_map.79), channel_id=1, replica_groups=mesh['blk'=4,'acc'=4,'tail'=2] {'blk','tail'}, dimensions={0} | all-to-all | bytes 524288 | tf_op jit(solution)/shard_map/all_to_all | solution.py:493
  37.6 1.0 %shard_map.80 = (f32[2,256,128]{2,1,0:T(8,128)S(1)}, bf16[2,256,512]{2,1,0:T(8,128)(2,1)S(1)}) custom-call(f32[8,64,128]{2,1,0:T(8,128)S(1)} %all_to_all.10.spectra, bf16[2,256,256]{2,1,0:T(8,128)(2,1)S(1)} %get-tuple-element.22.last, f32[2,128,512]{2,1,0:T(8,128)S(1)} %get-tuple-element.24.refs_5_.twist, ...), custom_call_target="tpu_custom_call" | custom-call | flops 1000000 | bytes 1000000 | tf_op jit(solution)/shard_map/pallas_call | solution.py:494
  38.5 0.1 collective-permute-start.4
  38.6 0.3 shard_map.81
  38.9 1.2 %collective-permute-done.4 = f32[2,256,128]{2,1,0:T(8,128)S(1)} collective-permute-done((f32[2,256,128]{2,1,0:T(8,128)S(1)}, f32[2,256,128]{2,1,0:T(8,128)S(1)}, u32[]{:S(2)}, u32[]{:S(2)}) %collective-permute-start.4) | collective-permute-done | bytes 262176 | tf_op jit(solution)/shard_map/ppermute | solution.py:458
  40.1 1.3 %collective-permute-start.5 = (f32[1,256,128]{2,1,0:T(8,128)S(1)}, f32[1,256,128]{2,1,0:T(8,128)S(1)}, u32[]{:S(2)}, u32[]{:S(2)}) collective-permute-start(f32[1,256,128]{2,1,0:T(8,128)S(1)} %slice_add_fusion), channel_id=1, source_target_pairs={{0,4},{2,6},{4,0},{6,2},{1,5},{3,7},{5,1},{7,3},{8,12},{10,14},{12... | collective-permute-start | bytes 393224 | tf_op jit(solution)/shard_map/ppermute | solution.py:458
  41.5 4.3 %collective-permute-done.5 = f32[1,256,128]{2,1,0:T(8,128)S(1)} collective-permute-done((f32[1,256,128]{2,1,0:T(8,128)S(1)}, f32[1,256,128]{2,1,0:T(8,128)S(1)}, u32[]{:S(2)}, u32[]{:S(2)}) %collective-permute-start.5) | collective-permute-done | bytes 131104 | tf_op jit(solution)/shard_map/ppermute | solution.py:458
  45.8 0.7 %fusion = f32[1,256,128]{2,1,0:T(8,128)} fusion(f32[1,256,128]{2,1,0:T(8,128)S(1)} %collective-permute-done.5, f32[2,256,128]{2,1,0:T(8,128)S(1)} %collective-permute-done.4, f32[2,256,128]{2,1,0:T(8,128)S(1)} %shard_map.81), kind=kLoop, calls=%fused_computation.2 | loop fusion | flops 65536 | bytes 524288 | tf_op jit(solution)/shard_map/add | solution.py:502
  (2 shorter events, 0.0 us)
Async XLA Ops:
  0.0 6.7 %collective-permute-start.1 = (f32[256,128]{1,0:T(8,128)}, f32[256,128]{1,0:T(8,128)S(1)}, u32[]{:S(2)}, u32[]{:S(2)}) collective-permute-start(f32[256,128]{1,0:T(8,128)} %bitcast.5), channel_id=1, source_target_pairs={{0,4},{2,6},{4,0},{6,2},{1,5},{3,7},{5,1},{7,3},{8,12},{10,14},{12... | collective-permute-start | bytes 393224 | tf_op jit(solution)/shard_map/ppermute | solution.py:458
  5.1 1.6 %collective-permute-start = (f32[272,128]{1,0:T(8,128)S(1)}, f32[272,128]{1,0:T(8,128)S(1)}, u32[]{:S(2)}, u32[]{:S(2)}) collective-permute-start(f32[272,128]{1,0:T(8,128)S(1)} %get-tuple-element.23), channel_id=1, source_target_pairs={{0,2},{2,0},{4,6},{6,4},{1,3},{3,1},{5,7},{7,5},{8,10},{10,8},{12,... | collective-permute-start | bytes 417800 | tf_op jit(solution)/shard_map/ppermute | solution.py:458
  6.7 1.3 %collective-permute-start.2 = (f32[256,128]{1,0:T(8,128)S(1)}, f32[256,128]{1,0:T(8,128)S(1)}, u32[]{:S(2)}, u32[]{:S(2)}) collective-permute-start(f32[256,128]{1,0:T(8,128)S(1)} %collective-permute-done.1.refs_2_), channel_id=1, source_target_pairs={{0,2},{2,0},{4,6},{6,4},{1,3},{3,1},{5,7},{7,5},{8,10},{10,8},{12,... | collective-permute-start | bytes 393224 | tf_op jit(solution)/shard_map/ppermute | solution.py:458
  9.7 15.3 %all-to-all-start = ((f32[8,64,128]{2,1,0:T(8,128)}), f32[8,64,128]{2,1,0:T(8,128)S(1)}, u32[]{:S(2)}, u32[]{:S(2)}) async-start(f32[8,64,128]{2,1,0:T(8,128)} %shard_map.76), calls=%async_computation | async-start | bytes 524288 | tf_op jit(solution)/shard_map/all_to_all | solution.py:491
  16.3 5.8 %collective-permute-start.3 = (f32[8,16,256]{2,1,0:T(8,128)S(1)}, f32[8,16,256]{2,1,0:T(8,128)S(1)}, u32[]{:S(2)}, u32[]{:S(2)}) collective-permute-start(f32[8,16,256]{2,1,0:T(8,128)S(1)} %shard_map.77), channel_id=1, source_target_pairs={{0,6},{2,4},{4,2},{6,0},{1,7},{3,5},{5,3},{7,1},{8,14},{10,12},{12... | collective-permute-start | bytes 393224 | tf_op jit(solution)/shard_map/ppermute | solution.py:458
  38.5 1.6 %collective-permute-start.4 = (f32[2,256,128]{2,1,0:T(8,128)S(1)}, f32[2,256,128]{2,1,0:T(8,128)S(1)}, u32[]{:S(2)}, u32[]{:S(2)}) collective-permute-start(f32[2,256,128]{2,1,0:T(8,128)S(1)} %get-tuple-element.30), channel_id=1, source_target_pairs={{0,2},{2,0},{4,6},{6,4},{1,3},{3,1},{5,7},{7,5},{8,10},{10,8},{12,... | collective-permute-start | bytes 786440 | tf_op jit(solution)/shard_map/ppermute | solution.py:458
  40.1 5.6 %collective-permute-start.5 = (f32[1,256,128]{2,1,0:T(8,128)S(1)}, f32[1,256,128]{2,1,0:T(8,128)S(1)}, u32[]{:S(2)}, u32[]{:S(2)}) collective-permute-start(f32[1,256,128]{2,1,0:T(8,128)S(1)} %slice_add_fusion), channel_id=1, source_target_pairs={{0,4},{2,6},{4,0},{6,2},{1,5},{3,7},{5,1},{7,3},{8,12},{10,14},{12... | collective-permute-start | bytes 393224 | tf_op jit(solution)/shard_map/ppermute | solution.py:458

commit v5 on v4

--- a/solution.py
+++ b/solution.py
@@ -397,18 +397,19 @@
     return call(kernel, shape, ["vmem"] * 2)
 
 
-def into_slots(plan, place, odd, last, turned, out, matrix):
-    where = [pl.ds(pl.multiple_of((place ^ (2 * slot + odd)) * plan.chunk, 16), plan.chunk) for slot in range(plan.quarters // 2)]
+def into_slots(plan, slots, last, turned, out, matrix):
+    place = spot(plan)[0]
+    where = [pl.ds(pl.multiple_of((place ^ slot) * plan.chunk, 16), plan.chunk) for slot in slots]
     rows = [jnp.concatenate([last[part, at, :] for at in where], axis=0) for part in range(2)]
     matrix[...] = product(rows, turned)
-    for slot in range(plan.quarters // 2):
+    for index in range(len(slots)):
         for column in range(plan.cols):
-            out[slot, pl.ds(column, plan.chunk, stride=plan.cols), :] = matrix[
-                slot * plan.chunk : (slot + 1) * plan.chunk, column * LANES : (column + 1) * LANES
+            out[index, pl.ds(column, plan.chunk, stride=plan.cols), :] = matrix[
+                index * plan.chunk : (index + 1) * plan.chunk, column * LANES : (column + 1) * LANES
             ]
 
 
-def backward(plan):
+def backward(plan, slots):
     def kernel(spectra, last, twist, second, out, turned, stack, spread, matrix):
         place = spot(plan)[0]
         rows = plan.rows
@@ -430,26 +431,26 @@
             jnp.concatenate([real * twist[0] + imag * twist[1], imag * twist[0] - real * twist[1]], axis=0)
         )
         turned[0], turned[1] = high, low
-        into_slots(plan, place, 1, last, (high, low), out, matrix)
+        into_slots(plan, slots, last, (high, low), out, matrix)
 
     shape = (
-        jax.ShapeDtypeStruct((plan.quarters // 2, plan.chunk * plan.cols, LANES), jnp.float32),
+        jax.ShapeDtypeStruct((len(slots), plan.chunk * plan.cols, LANES), jnp.float32),
         jax.ShapeDtypeStruct((2, 2 * plan.rows, plan.side), jnp.bfloat16),
     )
     scratch = [
         pltpu.VMEM((2 * plan.rows, plan.half), jnp.float32),
         pltpu.VMEM((2 * plan.rows, plan.side), jnp.float32),
-        pltpu.VMEM((plan.n1s // 2, plan.side), jnp.float32),
+        pltpu.VMEM((len(slots) * plan.chunk, plan.side), jnp.float32),
     ]
     return call(kernel, shape, ["vmem"] * 4, scratch)
 
 
-def finish(plan):
+def finish(plan, slots):
     def kernel(last, turned, out, matrix):
-        into_slots(plan, spot(plan)[0], 0, last, (turned[0], turned[1]), out, matrix)
-
-    shape = jax.ShapeDtypeStruct((plan.quarters // 2, plan.chunk * plan.cols, LANES), jnp.float32)
-    scratch = [pltpu.VMEM((plan.n1s // 2, plan.side), jnp.float32)]
+        into_slots(plan, slots, last, (turned[0], turned[1]), out, matrix)
+
+    shape = jax.ShapeDtypeStruct((len(slots), plan.chunk * plan.cols, LANES), jnp.float32)
+    scratch = [pltpu.VMEM((len(slots) * plan.chunk, plan.side), jnp.float32)]
     return call(kernel, shape, ["vmem"] * 2, scratch)
 
 
@@ -491,10 +492,17 @@
     every = lax.all_to_all(own_spectrum, ("blk", "tail"), 0, 0, tiled=True)
     sums = combine(plan)(every, own)
     back = lax.all_to_all(sums, ("blk", "tail"), 0, 0, tiled=True)
-    odd, turned = backward(plan)(back, last, twist, second)
-    arrived = swapped(odd, 1)
-    even = finish(plan)(last, turned)
-    held = {2 * slot: even[slot] + arrived[slot] for slot in range(quarters // 2)}
+    first_sent = [index for index in range(quarters) if index & 1 and (index & 2 or quarters == 2)]
+    others = [index for index in range(quarters) if index not in first_sent]
+    sent, turned = backward(plan, first_sent)(back, last, twist, second)
+    arrived = swapped(sent, 1)
+    rest = finish(plan, others)(last, turned)
+    slot = {index: rest[where] for where, index in enumerate(others)}
+    held = {index ^ 1: slot[index ^ 1] + arrived[where] for where, index in enumerate(first_sent)}
+    later = [index for index in others if index & 1]
+    if later:
+        arrived = swapped(jnp.stack([slot[index] for index in later]), 1)
+        held.update({index ^ 1: slot[index ^ 1] + arrived[where] for where, index in enumerate(later)})
     bit = 2
     while bit < quarters:
         sent = sorted(index for index in held if index & bit)

time: 46.8 us -> 46.9 us (level)
    ppermute x6 -> x7, starting transfers between devices: 5.45 us -> 5.61 us  [swapped(): lax.ppermute(value, 'acc', [(source, source ^ bit) for source in range(co...]
    ppermute x6 -> x7, waiting for transfers between devices: 11.6 us -> 11.5 us  [swapped(): lax.ppermute(value, 'acc', [(source, source ^ bit) for source in range(co...]
  transfers between devices with their start and end apart: 7 -> 8, of which waited for: 6 -> 6; matrix products, arithmetic and copies ran while one was open for 0% -> 0% of each run, Pallas kernels for 10% -> 10%
where the time goes in v5:
time: 46.9 us; the launch traced here: 46.6 us
  waiting for transfers between devices  14.4 us (31%)
  blocking collectives  12.2 us (26%)
  starting transfers between devices  11.7 us (25%)
  Pallas kernels  7.48 us (16%)
  other arithmetic  0.7 us (1%)
    all_to_all x1, blocking collectives, per_device(): back = lax.all_to_all(sums, ('blk', 'tail'), 0, 0, tiled=True)  12.2 us
    ppermute x7, waiting for transfers between devices, swapped(): lax.ppermute(value, 'acc', [(source, source ^ bit) for source in range(co...  11.5 us
    all_to_all x1, starting transfers between devices, per_device(): every = lax.all_to_all(own_spectrum, ('blk', 'tail'), 0, 0, tiled=True)  6.1 us
    ppermute x7, starting transfers between devices, swapped(): lax.ppermute(value, 'acc', [(source, source ^ bit) for source in range(co...  5.61 us
    all_to_all x1, waiting for transfers between devices, per_device(): every = lax.all_to_all(own_spectrum, ('blk', 'tail'), 0, 0, tiled=True)  2.87 us
    pallas_call x1, Pallas kernels, per_device(): prepare(plan)(*map(far, constants + [limbs, spectra]))  1.97 us
    pallas_call x1, Pallas kernels, per_device(): forward(plan)  1.68 us
    pallas_call x1, Pallas kernels, per_device(): last, own, edge = resident(plan)(first, far(spectra), rim)  1.56 us
  transfers between devices with their start and end apart: 8, of which 6 were waited for; matrix products, arithmetic and copies ran while one was open for 0% of the time, Pallas kernels for 10%

profile of v5, /device:TPU:0, one launch (start us, length us, event | category | flops | bytes accessed | tf_op | source)
XLA Modules:
  0.0 46.6 jit_solution(6336198861979065736)
XLA Ops:
  0.0 3.0 %collective-permute-start.1 = (f32[256,128]{1,0:T(8,128)}, f32[256,128]{1,0:T(8,128)S(1)}, u32[]{:S(2)}, u32[]{:S(2)}) collective-permute-start(f32[256,128]{1,0:T(8,128)} %bitcast.5), channel_id=1, source_target_pairs={{0,4},{2,6},{4,0},{6,2},{1,5},{3,7},{5,1},{7,3},{8,12},{10,14},{12... | collective-permute-start | bytes 393224 | tf_op jit(solution)/shard_map/ppermute | solution.py:459
  3.0 2.0 %shard_map.73 = (bf16[2,256,256]{2,1,0:T(8,128)(2,1)S(1)}, f32[2,128,512]{2,1,0:T(8,128)S(1)}, bf16[2,512,512]{2,1,0:T(8,128)(2,1)S(1)}, f32[256,128]{1,0:T(8,12...) custom-call(f32[2,128,256]{2,1,0:T(8,128)} %constant.10.clone.refs_0_, ...), custom_call_target="tpu_custom_call" | custom-call | flops 1000000 | bytes 1000000 | tf_op jit(solution)/shard_map/pallas_call | solution.py:471
  4.9 0.2 shard_map.74
  5.1 0.1 collective-permute-start
  5.2 1.5 %collective-permute-done.1.refs_2_ = f32[256,128]{1,0:T(8,128)S(1)} collective-permute-done((f32[256,128]{1,0:T(8,128)}, f32[256,128]{1,0:T(8,128)S(1)}, u32[]{:S(2)}, u32[]{:S(2)}) %collective-permute-start.1) | collective-permute-done | bytes 131104 | tf_op jit(solution)/shard_map/ppermute | solution.py:459
  6.7 0.0 collective-permute-start.2
  6.7 1.3 %collective-permute-done.2.refs_3_ = f32[256,128]{1,0:T(8,128)S(1)} collective-permute-done((f32[256,128]{1,0:T(8,128)S(1)}, f32[256,128]{1,0:T(8,128)S(1)}, u32[]{:S(2)}, u32[]{:S(2)}) %collective-permute-start.2) | collective-permute-done | bytes 131104 | tf_op jit(solution)/shard_map/ppermute | solution.py:459
  8.0 1.7 %shard_map.76 = f32[8,64,128]{2,1,0:T(8,128)} custom-call(f32[256,128]{1,0:T(8,128)S(1)} %get-tuple-element.19.near.refs_0_, f32[272,128]{1,0:T(8,128)S(1)} %collective-permute-done.refs_1_.other, f32[256,128]{1,0:T(8,128)S(1)} %collective-permute-done.1.refs_2_, f32[256,128]{1,0:T(8,128)S(1)} %collective-permute-done.2.refs_3_, ...), custom_call_target="tpu_custom_call" | custom-call | flops 1000000 | bytes 1000000 | tf_op jit(solution)/shard_map/pallas_call | solution.py:487
  9.7 6.1 %all-to-all-start = ((f32[8,64,128]{2,1,0:T(8,128)}), f32[8,64,128]{2,1,0:T(8,128)S(1)}, u32[]{:S(2)}, u32[]{:S(2)}) async-start(f32[8,64,128]{2,1,0:T(8,128)} %shard_map.76), calls=%async_computation | async-start | bytes 524288 | tf_op jit(solution)/shard_map/all_to_all | solution.py:492
  15.8 0.5 %shard_map.77 = f32[8,16,256]{2,1,0:T(8,128)S(1)} custom-call(f32[8,8,16,128]{3,2,1,0:T(8,128)S(1)} %get-tuple-element.27.held, f32[272,128]{1,0:T(8,128)S(1)} %collective-permute-done.refs_1_.other), custom_call_target="tpu_custom_call" | custom-call | flops 1000000 | bytes 1000000 | tf_op jit(solution)/shard_map/pallas_call | solution.py:480
  16.3 1.0 %collective-permute-start.3 = (f32[8,16,256]{2,1,0:T(8,128)S(1)}, f32[8,16,256]{2,1,0:T(8,128)S(1)}, u32[]{:S(2)}, u32[]{:S(2)}) collective-permute-start(f32[8,16,256]{2,1,0:T(8,128)S(1)} %shard_map.77), channel_id=1, source_target_pairs={{0,6},{2,4},{4,2},{6,0},{1,7},{3,5},{5,3},{7,1},{8,14},{10,12},{12... | collective-permute-start | bytes 393224 | tf_op jit(solution)/shard_map/ppermute | solution.py:459
  17.4 1.6 %shard_map.75 = (bf16[2,256,256]{2,1,0:T(8,128)(2,1)S(1)}, f32[8,2,16,128]{3,2,1,0:T(8,128)S(1)}, f32[8,256]{1,0:T(8,128)S(1)}) custom-call(bf16[2,256,256]{2,1,0:T(8,128)(2,1)S(1)} %get-tuple-element.18.first.refs_4_, f32[8,16,4096]{2,1,0:T(8,128)} %bitcast.4, f32[8,256]{1,0:T(8,128)S(1)} %get-tuple-element.21.rim), custom_call_target="tpu_custom_call" | custom-call | flops 1000000 | bytes 1000000 | tf_op jit(solution)/shard_map/pallas_call | solution.py:485
  18.9 3.2 %collective-permute-done.3.arrived = f32[8,16,256]{2,1,0:T(8,128)S(1)} collective-permute-done((f32[8,16,256]{2,1,0:T(8,128)S(1)}, f32[8,16,256]{2,1,0:T(8,128)S(1)}, u32[]{:S(2)}, u32[]{:S(2)}) %collective-permute-start.3) | collective-permute-done | bytes 131104 | tf_op jit(solution)/shard_map/ppermute | solution.py:459
  22.2 2.9 %all-to-all-done.spectra = f32[8,64,128]{2,1,0:T(8,128)S(1)} async-done(((f32[8,64,128]{2,1,0:T(8,128)}), f32[8,64,128]{2,1,0:T(8,128)S(1)}, u32[]{:S(2)}, u32[]{:S(2)}) %all-to-all-start) | async-done | bytes 262176 | tf_op jit(solution)/shard_map/all_to_all | solution.py:492
  25.0 0.3 shard_map.79
  25.3 12.2 %all_to_all.10.spectra = f32[8,64,128]{2,1,0:T(8,128)S(1)} all-to-all(f32[8,64,128]{2,1,0:T(8,128)S(1)} %shard_map.79), channel_id=1, replica_groups=mesh['blk'=4,'acc'=4,'tail'=2] {'blk','tail'}, dimensions={0} | all-to-all | bytes 524288 | tf_op jit(solution)/shard_map/all_to_all | solution.py:494
  37.5 0.9 %shard_map.80 = (f32[1,256,128]{2,1,0:T(8,128)S(1)}, bf16[2,256,512]{2,1,0:T(8,128)(2,1)S(1)}) custom-call(f32[8,64,128]{2,1,0:T(8,128)S(1)} %all_to_all.10.spectra, bf16[2,256,256]{2,1,0:T(8,128)(2,1)S(1)} %get-tuple-element.22.last, f32[2,128,512]{2,1,0:T(8,128)S(1)} %get-tuple-element.24.refs_5_.twist, ...), custom_call_target="tpu_custom_call" | custom-call | flops 1000000 | bytes 1000000 | tf_op jit(solution)/shard_map/pallas_call | solution.py:497
  38.5 0.1 collective-permute-start.5
  38.6 0.3 shard_map.81
  38.9 1.0 %collective-permute-done.5 = f32[1,256,128]{2,1,0:T(8,128)S(1)} collective-permute-done((f32[1,256,128]{2,1,0:T(8,128)S(1)}, f32[1,256,128]{2,1,0:T(8,128)S(1)}, u32[]{:S(2)}, u32[]{:S(2)}) %collective-permute-start.5) | collective-permute-done | bytes 131104 | tf_op jit(solution)/shard_map/ppermute | solution.py:459
  39.9 0.2 collective-permute-start.4
  40.1 1.3 %collective-permute-start.6 = (f32[1,256,128]{2,1,0:T(8,128)S(1)}, f32[1,256,128]{2,1,0:T(8,128)S(1)}, u32[]{:S(2)}, u32[]{:S(2)}) collective-permute-start(f32[1,256,128]{2,1,0:T(8,128)S(1)} %get-tuple-element.32), channel_id=1, source_target_pairs={{0,4},{2,6},{4,0},{6,2},{1,5},{3,7},{5,1},{7,3},{8,12},{10,14},{12... | collective-permute-start | bytes 393224 | tf_op jit(solution)/shard_map/ppermute | solution.py:459
  41.4 4.5 %collective-permute-done.6 = f32[1,256,128]{2,1,0:T(8,128)S(1)} collective-permute-done((f32[1,256,128]{2,1,0:T(8,128)S(1)}, f32[1,256,128]{2,1,0:T(8,128)S(1)}, u32[]{:S(2)}, u32[]{:S(2)}) %collective-permute-start.6) | collective-permute-done | bytes 131104 | tf_op jit(solution)/shard_map/ppermute | solution.py:459
  45.9 0.7 %fusion = f32[1,256,128]{2,1,0:T(8,128)} fusion(f32[1,256,128]{2,1,0:T(8,128)S(1)} %collective-permute-done.6, f32[1,256,128]{2,1,0:T(8,128)S(1)} %collective-permute-done.4, f32[3,256,128]{2,1,0:T(8,128)S(1)} %shard_map.81), kind=kLoop, calls=%fused_computation.2 | loop fusion | flops 65536 | bytes 524288 | tf_op jit(solution)/shard_map/add | solution.py:510
  (4 shorter events, 0.1 us)
Async XLA Ops:
  0.0 6.7 %collective-permute-start.1 = (f32[256,128]{1,0:T(8,128)}, f32[256,128]{1,0:T(8,128)S(1)}, u32[]{:S(2)}, u32[]{:S(2)}) collective-permute-start(f32[256,128]{1,0:T(8,128)} %bitcast.5), channel_id=1, source_target_pairs={{0,4},{2,6},{4,0},{6,2},{1,5},{3,7},{5,1},{7,3},{8,12},{10,14},{12... | collective-permute-start | bytes 393224 | tf_op jit(solution)/shard_map/ppermute | solution.py:459
  5.1 1.6 %collective-permute-start = (f32[272,128]{1,0:T(8,128)S(1)}, f32[272,128]{1,0:T(8,128)S(1)}, u32[]{:S(2)}, u32[]{:S(2)}) collective-permute-start(f32[272,128]{1,0:T(8,128)S(1)} %get-tuple-element.23), channel_id=1, source_target_pairs={{0,2},{2,0},{4,6},{6,4},{1,3},{3,1},{5,7},{7,5},{8,10},{10,8},{12,... | collective-permute-start | bytes 417800 | tf_op jit(solution)/shard_map/ppermute | solution.py:459
  6.7 1.3 %collective-permute-start.2 = (f32[256,128]{1,0:T(8,128)S(1)}, f32[256,128]{1,0:T(8,128)S(1)}, u32[]{:S(2)}, u32[]{:S(2)}) collective-permute-start(f32[256,128]{1,0:T(8,128)S(1)} %collective-permute-done.1.refs_2_), channel_id=1, source_target_pairs={{0,2},{2,0},{4,6},{6,4},{1,3},{3,1},{5,7},{7,5},{8,10},{10,8},{12,... | collective-permute-start | bytes 393224 | tf_op jit(solution)/shard_map/ppermute | solution.py:459
  9.7 15.3 %all-to-all-start = ((f32[8,64,128]{2,1,0:T(8,128)}), f32[8,64,128]{2,1,0:T(8,128)S(1)}, u32[]{:S(2)}, u32[]{:S(2)}) async-start(f32[8,64,128]{2,1,0:T(8,128)} %shard_map.76), calls=%async_computation | async-start | bytes 524288 | tf_op jit(solution)/shard_map/all_to_all | solution.py:492
  16.3 5.8 %collective-permute-start.3 = (f32[8,16,256]{2,1,0:T(8,128)S(1)}, f32[8,16,256]{2,1,0:T(8,128)S(1)}, u32[]{:S(2)}, u32[]{:S(2)}) collective-permute-start(f32[8,16,256]{2,1,0:T(8,128)S(1)} %shard_map.77), channel_id=1, source_target_pairs={{0,6},{2,4},{4,2},{6,0},{1,7},{3,5},{5,3},{7,1},{8,14},{10,12},{12... | collective-permute-start | bytes 393224 | tf_op jit(solution)/shard_map/ppermute | solution.py:459
  38.5 1.4 %collective-permute-start.5 = (f32[1,256,128]{2,1,0:T(8,128)S(1)}, f32[1,256,128]{2,1,0:T(8,128)S(1)}, u32[]{:S(2)}, u32[]{:S(2)}) collective-permute-start(f32[1,256,128]{2,1,0:T(8,128)S(1)} %get-tuple-element.30), channel_id=1, source_target_pairs={{0,2},{2,0},{4,6},{6,4},{1,3},{3,1},{5,7},{7,5},{8,10},{10,8},{12,... | collective-permute-start | bytes 393224 | tf_op jit(solution)/shard_map/ppermute | solution.py:459
  39.9 1.5 %collective-permute-start.4 = (f32[1,256,128]{2,1,0:T(8,128)S(1)}, f32[1,256,128]{2,1,0:T(8,128)S(1)}, u32[]{:S(2)}, u32[]{:S(2)}) collective-permute-start(f32[1,256,128]{2,1,0:T(8,128)S(1)} %get-tuple-element.31), channel_id=1, source_target_pairs={{0,2},{2,0},{4,6},{6,4},{1,3},{3,1},{5,7},{7,5},{8,10},{10,8},{12,... | collective-permute-start | bytes 393224 | tf_op jit(solution)/shard_map/ppermute | solution.py:459
  40.1 5.8 %collective-permute-start.6 = (f32[1,256,128]{2,1,0:T(8,128)S(1)}, f32[1,256,128]{2,1,0:T(8,128)S(1)}, u32[]{:S(2)}, u32[]{:S(2)}) collective-permute-start(f32[1,256,128]{2,1,0:T(8,128)S(1)} %get-tuple-element.32), channel_id=1, source_target_pairs={{0,4},{2,6},{4,0},{6,2},{1,5},{3,7},{5,1},{7,3},{8,12},{10,14},{12... | collective-permute-start | bytes 393224 | tf_op jit(solution)/shard_map/ppermute | solution.py:459

commit v6 on v5

--- a/solution.py
+++ b/solution.py
@@ -191,9 +191,9 @@
 
 def prepare(plan):
     def kernel(*refs):
-        first, twist, second, near, facing, rim = refs[7:13]
-        first_rows, first_part, twist_rows, twist_part = refs[13:17]
-        sems, facing_sems, rim_sems = refs[17:]
+        first, twist, second, near, facing, rim, tail = refs[7:14]
+        first_rows, first_part, twist_rows, twist_part = refs[14:18]
+        sems, facing_sems, rim_sems = refs[18:]
         place, m_lo, _ = spot(plan)
         targets = (first_rows, first_part, twist_rows, twist_part, second, near)
         copies = [
@@ -209,8 +209,13 @@
         part_cos = first_part[pl.ds(place, 1), 0, :]
         part_sin = first_part[pl.ds(place, 1), 1, :]
         rows = plan.rows
-        first[0, :rows], first[1, :rows] = split(first_rows[0] * part_cos - first_rows[1] * part_sin)
-        first[0, rows:], first[1, rows:] = split(first_rows[0] * part_sin + first_rows[1] * part_cos)
+        start = (place ^ (plan.quarters - 1)) * plan.chunk
+        real = first_rows[0] * part_cos - first_rows[1] * part_sin
+        imag = first_rows[0] * part_sin + first_rows[1] * part_cos
+        for part, value in enumerate((real, imag)):
+            some = slice(part * rows, (part + 1) * rows)
+            first[0, some], first[1, some] = split(value)
+            tail[0, some], tail[1, some] = split(pltpu.roll(value, plan.n1s - start, 1)[:, : plan.chunk])
         copies[2].wait()
         copies[3].wait()
         part_cos = twist_part[pl.ds(place, 1), 0, :]
@@ -228,6 +233,7 @@
         shape((plan.chunk * plan.cols, LANES), jnp.float32),
         held_shape(plan, plan.freq_rows),
         held_shape(plan, TILE),
+        shape((2, 2 * plan.rows, plan.chunk), jnp.bfloat16),
     )
     scratch = [
         pltpu.VMEM((2, plan.rows, plan.n1s), jnp.float32),
@@ -312,18 +318,34 @@
     return slice(start, start + plan.slice_rows)
 
 
-def forward(plan):
+def begin(plan):
     def kernel(*refs):
-        limbs = refs[: plan.quarters]
-        first, twist, second, out, matrix, turned, packed, sems = refs[plan.quarters :]
+        limbs = refs[: plan.quarters - 1]
+        first, out, matrix = refs[plan.quarters - 1 :]
         place = spot(plan)[0]
         for index in range(plan.quarters):
             start = pl.multiple_of((place ^ index) * plan.chunk, 8)
             for column in range(plan.cols):
-                matrix[pl.ds(start, plan.chunk), column * LANES : (column + 1) * LANES] = limbs[index][
-                    pl.ds(column, plan.chunk, stride=plan.cols), :
-                ]
-        value = product((first[0], first[1]), split(matrix[...]))
+                lanes = slice(column * LANES, (column + 1) * LANES)
+                if index < plan.quarters - 1:
+                    value = limbs[index][pl.ds(column, plan.chunk, stride=plan.cols), :]
+                else:
+                    value = jnp.zeros((plan.chunk, LANES), jnp.float32)
+                matrix[pl.ds(start, plan.chunk), lanes] = value
+        out[...] = product((first[0], first[1]), split(matrix[...]))
+
+    shape = jax.ShapeDtypeStruct((2 * plan.rows, plan.side), jnp.float32)
+    scratch = [pltpu.VMEM((plan.n1s, plan.side), jnp.float32)]
+    return call(kernel, shape, ["vmem"] * plan.quarters, scratch)
+
+
+def forward(plan):
+    def kernel(limbs, begun, tail, twist, second, out, matrix, turned, packed, sems):
+        place = spot(plan)[0]
+        for column in range(plan.cols):
+            rows = pl.ds(column, plan.chunk, stride=plan.cols)
+            matrix[:, column * LANES : (column + 1) * LANES] = limbs[rows, :]
+        value = begun[...] + product((tail[0], tail[1]), split(matrix[...]))
         rows = plan.rows
         real, imag = value[:rows], value[rows:]
         turned[:rows] = real * twist[0] - imag * twist[1]
@@ -358,12 +380,12 @@
 
     shape = jax.ShapeDtypeStruct((plan.groups, plan.packed, LANES), jnp.float32)
     scratch = [
-        pltpu.VMEM((plan.n1s, plan.side), jnp.float32),
+        pltpu.VMEM((plan.chunk, plan.side), jnp.float32),
         pltpu.VMEM((2 * plan.rows, plan.side), jnp.float32),
         pltpu.VMEM((plan.groups, plan.packed, LANES), jnp.float32),
         pltpu.SemaphoreType.DMA((PIECES,)),
     ]
-    return call(kernel, shape, ["vmem"] * (plan.quarters + 3), scratch, "hbm")
+    return call(kernel, shape, ["vmem"] * 5, scratch, "hbm")
 
 
 def combine(plan):
@@ -391,7 +413,7 @@
                     out[block, packed_rows(plan, part, column)] = sums[part * plan.half_cols + column]
             return carry
 
-        lax.fori_loop(0, plan.groups, one_block, 0)
+        lax.fori_loop(0, plan.groups, one_block, 0, unroll=4)
 
     shape = jax.ShapeDtypeStruct((plan.groups, plan.packed, LANES), jnp.float32)
     return call(kernel, shape, ["vmem"] * 2)
@@ -420,10 +442,12 @@
                     start = part * rows + group * plan.slice_rows
                     stack[start : start + plan.slice_rows, lanes] = spectra[group, packed_rows(plan, part, column)]
         value = split(stack[...])
-        by_cos = product(value, (second[0, :, : plan.half], second[1, :, : plan.half]), True)
-        by_sin = product(value, (second[0, :, plan.half :], second[1, :, plan.half :]), True)
-        spread[:rows] = by_cos[:rows] - by_sin[rows:]
-        spread[rows:] = by_cos[rows:] + by_sin[:rows]
+        high, low = value
+        paired = lambda half: jnp.concatenate(
+            [jnp.concatenate([half[:rows], -half[rows:]], axis=1), jnp.concatenate([half[rows:], half[:rows]], axis=1)],
+            axis=0,
+        )
+        spread[...] = product((paired(high), paired(low)), (second[0], second[1]), True)
         middle = jnp.where(place == 0, stack[rows : rows + 1, :1], 0.0)
         spread[:1] = spread[:1] + middle * alternating(plan, 1)
         real, imag = spread[:rows], spread[rows:]
@@ -468,7 +492,7 @@
 
     limbs = divisor.reshape(plan.chunk * plan.cols, LANES)
     spectra = reciprocal_spectra.reshape(2 * rounds, freq_rows, plane)
-    first, twist, second, near, facing, rim = prepare(plan)(*map(far, constants + [limbs, spectra]))
+    first, twist, second, near, facing, rim, tail = prepare(plan)(*map(far, constants + [limbs, spectra]))
     bundled, rim = bundle(plan)(near, rim)
     pieces = {0: limbs}
     bit = quarters // 2
@@ -484,7 +508,8 @@
         rim = lax.ppermute(rim, "acc", [(source, -source % quarters) for source in range(quarters)])
     last, own, edge = resident(plan)(first, far(spectra), rim)
 
-    own_spectrum = forward(plan)(*[pieces[index] for index in range(quarters)], first, twist, second)
+    begun = begin(plan)(*[pieces[index] for index in range(quarters - 1)], first)
+    own_spectrum = forward(plan)(pieces[quarters - 1], begun, tail, twist, second)
     own = blend(plan, rides)(own, facing, edge, rim)
     if plan.per > 1:
         first_row = lax.axis_index(("blk", "tail")) % plan.per * plan.slice_rows
@@ -502,7 +527,8 @@
     later = [index for index in others if index & 1]
     if later:
         arrived = swapped(jnp.stack([slot[index] for index in later]), 1)
-        held.update({index ^ 1: slot[index ^ 1] + arrived[where] for where, index in enumerate(later)})
+        sums = {index ^ 1: slot[index ^ 1] + arrived[where] for where, index in enumerate(later)}
+        held.update(lax.optimization_barrier(sums))
     bit = 2
     while bit < quarters:
         sent = sorted(index for index in held if index & bit)

time: 46.9 us -> 46.8 us (level)
    pallas_call x1 -> x2, Pallas kernels: 1.68 us -> 2.04 us  [the longest x1 1.61 us: per_device(): forward(plan)(pieces[quarters - 1], begun, tail, twist, second)]
  transfers between devices with their start and end apart: 8 -> 8, of which waited for: 6 -> 6; matrix products, arithmetic and copies ran while one was open for 0% -> 0% of each run, Pallas kernels for 10% -> 11%
where the time goes in v6:
time: 46.8 us; the launch traced here: 46.4 us
  waiting for transfers between devices  14 us (30%)
  blocking collectives  12.2 us (26%)
  starting transfers between devices  11.7 us (25%)
  Pallas kernels  7.77 us (17%)
  other arithmetic  0.71 us (2%)
    all_to_all x1, blocking collectives, per_device(): back = lax.all_to_all(sums, ('blk', 'tail'), 0, 0, tiled=True)  12.2 us
    ppermute x7, waiting for transfers between devices, swapped(): lax.ppermute(value, 'acc', [(source, source ^ bit) for source in range(co...  11.1 us
    all_to_all x1, starting transfers between devices, per_device(): every = lax.all_to_all(own_spectrum, ('blk', 'tail'), 0, 0, tiled=True)  6.09 us
    ppermute x7, starting transfers between devices, swapped(): lax.ppermute(value, 'acc', [(source, source ^ bit) for source in range(co...  5.62 us
    all_to_all x1, waiting for transfers between devices, per_device(): every = lax.all_to_all(own_spectrum, ('blk', 'tail'), 0, 0, tiled=True)  2.87 us
    pallas_call x1, Pallas kernels, per_device(): prepare(plan)(*map(far, constants + [limbs, spectra]))  1.97 us
    pallas_call x1, Pallas kernels, per_device(): forward(plan)(pieces[quarters - 1], begun, tail, twist, second)  1.61 us
    pallas_call x1, Pallas kernels, per_device(): last, own, edge = resident(plan)(first, far(spectra), rim)  1.56 us
  transfers between devices with their start and end apart: 8, of which 6 were waited for; matrix products, arithmetic and copies ran while one was open for 0% of the time, Pallas kernels for 11%

profile of v6, /device:TPU:0, one launch (start us, length us, event | category | flops | bytes accessed | tf_op | source)
XLA Modules:
  0.0 46.4 jit_solution(14058717177320727667)
XLA Ops:
  0.0 3.0 %collective-permute-start = (f32[256,128]{1,0:T(8,128)}, f32[256,128]{1,0:T(8,128)S(1)}, u32[]{:S(2)}, u32[]{:S(2)}) collective-permute-start(f32[256,128]{1,0:T(8,128)} %bitcast.9), channel_id=1, source_target_pairs={{0,4},{2,6},{4,0},{6,2},{1,5},{3,7},{5,1},{7,3},{8,12},{10,14},{12... | collective-permute-start | bytes 393224 | tf_op jit(solution)/shard_map/ppermute | solution.py:483
  3.0 2.0 %shard_map.73 = (bf16[2,256,256]{2,1,0:T(8,128)(2,1)S(1)}, f32[2,128,512]{2,1,0:T(8,128)S(1)}, bf16[2,512,512]{2,1,0:T(8,128)(2,1)S(1)}, f32[256,128]{1,0:T(8,12...) custom-call(f32[2,128,256]{2,1,0:T(8,128)} %constant.10.clone.refs_0_, ...), custom_call_target="tpu_custom_call" | custom-call | flops 1000000 | bytes 1000000 | tf_op jit(solution)/shard_map/pallas_call | solution.py:495
  4.9 0.2 shard_map.74
  5.1 0.1 collective-permute-start.2
  5.2 1.5 %collective-permute-done.refs_2_ = f32[256,128]{1,0:T(8,128)S(1)} collective-permute-done((f32[256,128]{1,0:T(8,128)}, f32[256,128]{1,0:T(8,128)S(1)}, u32[]{:S(2)}, u32[]{:S(2)}) %collective-permute-start) | collective-permute-done | bytes 131104 | tf_op jit(solution)/shard_map/ppermute | solution.py:483
  6.7 0.4 shard_map.76.begun
  7.1 0.9 %collective-permute-done.1.limbs = f32[256,128]{1,0:T(8,128)S(1)} collective-permute-done((f32[256,128]{1,0:T(8,128)S(1)}, f32[256,128]{1,0:T(8,128)S(1)}, u32[]{:S(2)}, u32[]{:S(2)}) %collective-permute-start.1) | collective-permute-done | bytes 131104 | tf_op jit(solution)/shard_map/ppermute | solution.py:483
  8.0 1.6 %shard_map.77 = f32[8,64,128]{2,1,0:T(8,128)} custom-call(f32[256,128]{1,0:T(8,128)S(1)} %collective-permute-done.1.limbs, f32[256,512]{1,0:T(8,128)S(1)} %shard_map.76.begun, bf16[2,256,64]{2,1,0:T(8,128)(2,1)S(1)} %get-tuple-element.25.tail, f32[2,128,512]{2,1,0:T(8,128)S(1)} %get-tuple-element.26.twist, bf16[2,512,512]{2,1,0:T(8,128)(2,1)S(1)} %get-tuple-element.27.second), custom_call_target="tpu_custom_call" | custom-call | flops 1000000 | bytes 1000000 | tf_op jit(solution)/shard_map/pallas_call | solution.py:512
  9.6 6.1 %all-to-all-start = ((f32[8,64,128]{2,1,0:T(8,128)}), f32[8,64,128]{2,1,0:T(8,128)S(1)}, u32[]{:S(2)}, u32[]{:S(2)}) async-start(f32[8,64,128]{2,1,0:T(8,128)} %shard_map.77), calls=%async_computation | async-start | bytes 524288 | tf_op jit(solution)/shard_map/all_to_all | solution.py:517
  15.7 0.5 %shard_map.78 = f32[8,16,256]{2,1,0:T(8,128)S(1)} custom-call(f32[8,8,16,128]{3,2,1,0:T(8,128)S(1)} %get-tuple-element.29.held, f32[272,128]{1,0:T(8,128)S(1)} %collective-permute-done.2.refs_1_.other), custom_call_target="tpu_custom_call" | custom-call | flops 1000000 | bytes 1000000 | tf_op jit(solution)/shard_map/pallas_call | solution.py:504
  16.2 1.0 %collective-permute-start.3 = (f32[8,16,256]{2,1,0:T(8,128)S(1)}, f32[8,16,256]{2,1,0:T(8,128)S(1)}, u32[]{:S(2)}, u32[]{:S(2)}) collective-permute-start(f32[8,16,256]{2,1,0:T(8,128)S(1)} %shard_map.78), channel_id=1, source_target_pairs={{0,6},{2,4},{4,2},{6,0},{1,7},{3,5},{5,3},{7,1},{8,14},{10,12},{12... | collective-permute-start | bytes 393224 | tf_op jit(solution)/shard_map/ppermute | solution.py:483
  17.3 1.6 %shard_map.75 = (bf16[2,256,256]{2,1,0:T(8,128)(2,1)S(1)}, f32[8,2,16,128]{3,2,1,0:T(8,128)S(1)}, f32[8,256]{1,0:T(8,128)S(1)}) custom-call(bf16[2,256,256]{2,1,0:T(8,128)(2,1)S(1)} %get-tuple-element.19.first.refs_3_, f32[8,16,4096]{2,1,0:T(8,128)} %bitcast.8, f32[8,256]{1,0:T(8,128)S(1)} %get-tuple-element.22.rim), custom_call_target="tpu_custom_call" | custom-call | flops 1000000 | bytes 1000000 | tf_op jit(solution)/shard_map/pallas_call | solution.py:509
  18.9 3.2 %collective-permute-done.3.arrived = f32[8,16,256]{2,1,0:T(8,128)S(1)} collective-permute-done((f32[8,16,256]{2,1,0:T(8,128)S(1)}, f32[8,16,256]{2,1,0:T(8,128)S(1)}, u32[]{:S(2)}, u32[]{:S(2)}) %collective-permute-start.3) | collective-permute-done | bytes 131104 | tf_op jit(solution)/shard_map/ppermute | solution.py:483
  22.1 2.9 %all-to-all-done.spectra = f32[8,64,128]{2,1,0:T(8,128)S(1)} async-done(((f32[8,64,128]{2,1,0:T(8,128)}), f32[8,64,128]{2,1,0:T(8,128)S(1)}, u32[]{:S(2)}, u32[]{:S(2)}) %all-to-all-start) | async-done | bytes 262176 | tf_op jit(solution)/shard_map/all_to_all | solution.py:517
  25.0 0.2 shard_map.80
  25.2 12.2 %all_to_all.10.spectra = f32[8,64,128]{2,1,0:T(8,128)S(1)} all-to-all(f32[8,64,128]{2,1,0:T(8,128)S(1)} %shard_map.80), channel_id=1, replica_groups=mesh['blk'=4,'acc'=4,'tail'=2] {'blk','tail'}, dimensions={0} | all-to-all | bytes 524288 | tf_op jit(solution)/shard_map/all_to_all | solution.py:519
  37.4 0.9 %shard_map.81 = (f32[1,256,128]{2,1,0:T(8,128)S(1)}, bf16[2,256,512]{2,1,0:T(8,128)(2,1)S(1)}) custom-call(f32[8,64,128]{2,1,0:T(8,128)S(1)} %all_to_all.10.spectra, bf16[2,256,256]{2,1,0:T(8,128)(2,1)S(1)} %get-tuple-element.23.last, f32[2,128,512]{2,1,0:T(8,128)S(1)} %get-tuple-element.26.twist, bf16[2,512,512]{2,1,0:T(8,128)(2,1)S(1)} %get-tuple-element.27.second), custom_call_target="tpu_custom_call" | custom-call | flops 1000000 | bytes 1000000 | tf_op jit(solution)/shard_map/pallas_call | solution.py:522
  38.3 0.1 collective-permute-start.5
  38.4 0.3 shard_map.82
  38.7 1.0 %collective-permute-done.5 = f32[1,256,128]{2,1,0:T(8,128)S(1)} collective-permute-done((f32[1,256,128]{2,1,0:T(8,128)S(1)}, f32[1,256,128]{2,1,0:T(8,128)S(1)}, u32[]{:S(2)}, u32[]{:S(2)}) %collective-permute-start.5) | collective-permute-done | bytes 131104 | tf_op jit(solution)/shard_map/ppermute | solution.py:483
  39.8 0.2 collective-permute-start.4
  40.0 1.3 %collective-permute-start.6 = (f32[1,256,128]{2,1,0:T(8,128)S(1)}, f32[1,256,128]{2,1,0:T(8,128)S(1)}, u32[]{:S(2)}, u32[]{:S(2)}) collective-permute-start(f32[1,256,128]{2,1,0:T(8,128)S(1)} %get-tuple-element.33), channel_id=1, source_target_pairs={{0,4},{2,6},{4,0},{6,2},{1,5},{3,7},{5,1},{7,3},{8,12},{10,14},{12... | collective-permute-start | bytes 393224 | tf_op jit(solution)/shard_map/ppermute | solution.py:483
  41.3 4.5 %collective-permute-done.6 = f32[1,256,128]{2,1,0:T(8,128)S(1)} collective-permute-done((f32[1,256,128]{2,1,0:T(8,128)S(1)}, f32[1,256,128]{2,1,0:T(8,128)S(1)}, u32[]{:S(2)}, u32[]{:S(2)}) %collective-permute-start.6) | collective-permute-done | bytes 131104 | tf_op jit(solution)/shard_map/ppermute | solution.py:483
  45.8 0.7 %bitcast_add_fusion = f32[256,128]{1,0:T(8,128)} fusion(f32[256,128]{1,0:T(8,128)S(1)} %fusion, f32[1,256,128]{2,1,0:T(8,128)S(1)} %collective-permute-done.6), kind=kLoop, calls=%fused_computation.3 | loop fusion | flops 32768 | bytes 393216 | tf_op jit(solution)/shard_map/add | solution.py:536
  (6 shorter events, 0.1 us)
Async XLA Ops:
  0.0 6.7 %collective-permute-start = (f32[256,128]{1,0:T(8,128)}, f32[256,128]{1,0:T(8,128)S(1)}, u32[]{:S(2)}, u32[]{:S(2)}) collective-permute-start(f32[256,128]{1,0:T(8,128)} %bitcast.9), channel_id=1, source_target_pairs={{0,4},{2,6},{4,0},{6,2},{1,5},{3,7},{5,1},{7,3},{8,12},{10,14},{12... | collective-permute-start | bytes 393224 | tf_op jit(solution)/shard_map/ppermute | solution.py:483
  5.1 1.6 %collective-permute-start.2 = (f32[272,128]{1,0:T(8,128)S(1)}, f32[272,128]{1,0:T(8,128)S(1)}, u32[]{:S(2)}, u32[]{:S(2)}) collective-permute-start(f32[272,128]{1,0:T(8,128)S(1)} %get-tuple-element.24), channel_id=1, source_target_pairs={{0,2},{2,0},{4,6},{6,4},{1,3},{3,1},{5,7},{7,5},{8,10},{10,8},{12,... | collective-permute-start | bytes 417800 | tf_op jit(solution)/shard_map/ppermute | solution.py:483
  6.7 1.3 %collective-permute-start.1 = (f32[256,128]{1,0:T(8,128)S(1)}, f32[256,128]{1,0:T(8,128)S(1)}, u32[]{:S(2)}, u32[]{:S(2)}) collective-permute-start(f32[256,128]{1,0:T(8,128)S(1)} %collective-permute-done.refs_2_), channel_id=1, source_target_pairs={{0,2},{2,0},{4,6},{6,4},{1,3},{3,1},{5,7},{7,5},{8,10},{10,8},{12,... | collective-permute-start | bytes 393224 | tf_op jit(solution)/shard_map/ppermute | solution.py:483
  9.6 15.3 %all-to-all-start = ((f32[8,64,128]{2,1,0:T(8,128)}), f32[8,64,128]{2,1,0:T(8,128)S(1)}, u32[]{:S(2)}, u32[]{:S(2)}) async-start(f32[8,64,128]{2,1,0:T(8,128)} %shard_map.77), calls=%async_computation | async-start | bytes 524288 | tf_op jit(solution)/shard_map/all_to_all | solution.py:517
  16.2 5.8 %collective-permute-start.3 = (f32[8,16,256]{2,1,0:T(8,128)S(1)}, f32[8,16,256]{2,1,0:T(8,128)S(1)}, u32[]{:S(2)}, u32[]{:S(2)}) collective-permute-start(f32[8,16,256]{2,1,0:T(8,128)S(1)} %shard_map.78), channel_id=1, source_target_pairs={{0,6},{2,4},{4,2},{6,0},{1,7},{3,5},{5,3},{7,1},{8,14},{10,12},{12... | collective-permute-start | bytes 393224 | tf_op jit(solution)/shard_map/ppermute | solution.py:483
  38.3 1.4 %collective-permute-start.5 = (f32[1,256,128]{2,1,0:T(8,128)S(1)}, f32[1,256,128]{2,1,0:T(8,128)S(1)}, u32[]{:S(2)}, u32[]{:S(2)}) collective-permute-start(f32[1,256,128]{2,1,0:T(8,128)S(1)} %get-tuple-element.32), channel_id=1, source_target_pairs={{0,2},{2,0},{4,6},{6,4},{1,3},{3,1},{5,7},{7,5},{8,10},{10,8},{12,... | collective-permute-start | bytes 393224 | tf_op jit(solution)/shard_map/ppermute | solution.py:483
  39.8 1.5 %collective-permute-start.4 = (f32[1,256,128]{2,1,0:T(8,128)S(1)}, f32[1,256,128]{2,1,0:T(8,128)S(1)}, u32[]{:S(2)}, u32[]{:S(2)}) collective-permute-start(f32[1,256,128]{2,1,0:T(8,128)S(1)} %get-tuple-element.34), channel_id=1, source_target_pairs={{0,2},{2,0},{4,6},{6,4},{1,3},{3,1},{5,7},{7,5},{8,10},{10,8},{12,... | collective-permute-start | bytes 393224 | tf_op jit(solution)/shard_map/ppermute | solution.py:483
  40.0 5.8 %collective-permute-start.6 = (f32[1,256,128]{2,1,0:T(8,128)S(1)}, f32[1,256,128]{2,1,0:T(8,128)S(1)}, u32[]{:S(2)}, u32[]{:S(2)}) collective-permute-start(f32[1,256,128]{2,1,0:T(8,128)S(1)} %get-tuple-element.33), channel_id=1, source_target_pairs={{0,4},{2,6},{4,0},{6,2},{1,5},{3,7},{5,1},{7,3},{8,12},{10,14},{12... | collective-permute-start | bytes 393224 | tf_op jit(solution)/shard_map/ppermute | solution.py:483

commit v7 on v6

--- a/solution.py
+++ b/solution.py
@@ -413,7 +413,7 @@
                     out[block, packed_rows(plan, part, column)] = sums[part * plan.half_cols + column]
             return carry
 
-        lax.fori_loop(0, plan.groups, one_block, 0, unroll=4)
+        lax.fori_loop(0, plan.groups, one_block, 0, unroll=8)
 
     shape = jax.ShapeDtypeStruct((plan.groups, plan.packed, LANES), jnp.float32)
     return call(kernel, shape, ["vmem"] * 2)
@@ -442,12 +442,10 @@
                     start = part * rows + group * plan.slice_rows
                     stack[start : start + plan.slice_rows, lanes] = spectra[group, packed_rows(plan, part, column)]
         value = split(stack[...])
-        high, low = value
-        paired = lambda half: jnp.concatenate(
-            [jnp.concatenate([half[:rows], -half[rows:]], axis=1), jnp.concatenate([half[rows:], half[:rows]], axis=1)],
-            axis=0,
-        )
-        spread[...] = product((paired(high), paired(low)), (second[0], second[1]), True)
+        by_cos = product(value, (second[0, :, : plan.half], second[1, :, : plan.half]), True)
+        by_sin = product(value, (second[0, :, plan.half :], second[1, :, plan.half :]), True)
+        spread[:rows] = by_cos[:rows] - by_sin[rows:]
+        spread[rows:] = by_cos[rows:] + by_sin[:rows]
         middle = jnp.where(place == 0, stack[rows : rows + 1, :1], 0.0)
         spread[:1] = spread[:1] + middle * alternating(plan, 1)
         real, imag = spread[:rows], spread[rows:]

time: 46.8 us -> 46.8 us (level)
  no operation moved by 1% of the time
where the time goes in v7:
time: 46.8 us; the launch traced here: 46.4 us
  waiting for transfers between devices  13.9 us (30%)
  blocking collectives  12.2 us (26%)
  starting transfers between devices  11.7 us (25%)
  Pallas kernels  7.79 us (17%)
  other arithmetic  0.71 us (2%)
    all_to_all x1, blocking collectives, per_device(): back = lax.all_to_all(sums, ('blk', 'tail'), 0, 0, tiled=True)  12.2 us
    ppermute x7, waiting for transfers between devices, swapped(): lax.ppermute(value, 'acc', [(source, source ^ bit) for source in range(co...  11.1 us
    all_to_all x1, starting transfers between devices, per_device(): every = lax.all_to_all(own_spectrum, ('blk', 'tail'), 0, 0, tiled=True)  6.09 us
    ppermute x7, starting transfers between devices, swapped(): lax.ppermute(value, 'acc', [(source, source ^ bit) for source in range(co...  5.62 us
    all_to_all x1, waiting for transfers between devices, per_device(): every = lax.all_to_all(own_spectrum, ('blk', 'tail'), 0, 0, tiled=True)  2.87 us
    pallas_call x1, Pallas kernels, per_device(): prepare(plan)(*map(far, constants + [limbs, spectra]))  1.97 us
    pallas_call x1, Pallas kernels, per_device(): forward(plan)(pieces[quarters - 1], begun, tail, twist, second)  1.61 us
    pallas_call x1, Pallas kernels, per_device(): last, own, edge = resident(plan)(first, far(spectra), rim)  1.56 us
  transfers between devices with their start and end apart: 8, of which 6 were waited for; matrix products, arithmetic and copies ran while one was open for 0% of the time, Pallas kernels for 11%

profile of v7, /device:TPU:0, one launch (start us, length us, event | category | flops | bytes accessed | tf_op | source)
XLA Modules:
  0.0 46.4 jit_solution(3135760206883406959)
XLA Ops:
  0.0 3.0 %collective-permute-start = (f32[256,128]{1,0:T(8,128)}, f32[256,128]{1,0:T(8,128)S(1)}, u32[]{:S(2)}, u32[]{:S(2)}) collective-permute-start(f32[256,128]{1,0:T(8,128)} %bitcast.9), channel_id=1, source_target_pairs={{0,4},{2,6},{4,0},{6,2},{1,5},{3,7},{5,1},{7,3},{8,12},{10,14},{12... | collective-permute-start | bytes 393224 | tf_op jit(solution)/shard_map/ppermute | solution.py:481
  3.0 2.0 %shard_map.73 = (bf16[2,256,256]{2,1,0:T(8,128)(2,1)S(1)}, f32[2,128,512]{2,1,0:T(8,128)S(1)}, bf16[2,512,512]{2,1,0:T(8,128)(2,1)S(1)}, f32[256,128]{1,0:T(8,12...) custom-call(f32[2,128,256]{2,1,0:T(8,128)} %constant.10.clone.refs_0_, ...), custom_call_target="tpu_custom_call" | custom-call | flops 1000000 | bytes 1000000 | tf_op jit(solution)/shard_map/pallas_call | solution.py:493
  4.9 0.2 shard_map.74
  5.1 0.1 collective-permute-start.2
  5.2 1.5 %collective-permute-done.refs_2_ = f32[256,128]{1,0:T(8,128)S(1)} collective-permute-done((f32[256,128]{1,0:T(8,128)}, f32[256,128]{1,0:T(8,128)S(1)}, u32[]{:S(2)}, u32[]{:S(2)}) %collective-permute-start) | collective-permute-done | bytes 131104 | tf_op jit(solution)/shard_map/ppermute | solution.py:481
  6.7 0.4 shard_map.76.begun
  7.1 0.9 %collective-permute-done.1.limbs = f32[256,128]{1,0:T(8,128)S(1)} collective-permute-done((f32[256,128]{1,0:T(8,128)S(1)}, f32[256,128]{1,0:T(8,128)S(1)}, u32[]{:S(2)}, u32[]{:S(2)}) %collective-permute-start.1) | collective-permute-done | bytes 131104 | tf_op jit(solution)/shard_map/ppermute | solution.py:481
  8.0 1.6 %shard_map.77 = f32[8,64,128]{2,1,0:T(8,128)} custom-call(f32[256,128]{1,0:T(8,128)S(1)} %collective-permute-done.1.limbs, f32[256,512]{1,0:T(8,128)S(1)} %shard_map.76.begun, bf16[2,256,64]{2,1,0:T(8,128)(2,1)S(1)} %get-tuple-element.25.tail, f32[2,128,512]{2,1,0:T(8,128)S(1)} %get-tuple-element.26.twist, bf16[2,512,512]{2,1,0:T(8,128)(2,1)S(1)} %get-tuple-element.27.second), custom_call_target="tpu_custom_call" | custom-call | flops 1000000 | bytes 1000000 | tf_op jit(solution)/shard_map/pallas_call | solution.py:510
  9.6 6.1 %all-to-all-start = ((f32[8,64,128]{2,1,0:T(8,128)}), f32[8,64,128]{2,1,0:T(8,128)S(1)}, u32[]{:S(2)}, u32[]{:S(2)}) async-start(f32[8,64,128]{2,1,0:T(8,128)} %shard_map.77), calls=%async_computation | async-start | bytes 524288 | tf_op jit(solution)/shard_map/all_to_all | solution.py:515
  15.7 0.5 %shard_map.78 = f32[8,16,256]{2,1,0:T(8,128)S(1)} custom-call(f32[8,8,16,128]{3,2,1,0:T(8,128)S(1)} %get-tuple-element.29.held, f32[272,128]{1,0:T(8,128)S(1)} %collective-permute-done.2.refs_1_.other), custom_call_target="tpu_custom_call" | custom-call | flops 1000000 | bytes 1000000 | tf_op jit(solution)/shard_map/pallas_call | solution.py:502
  16.2 1.0 %collective-permute-start.3 = (f32[8,16,256]{2,1,0:T(8,128)S(1)}, f32[8,16,256]{2,1,0:T(8,128)S(1)}, u32[]{:S(2)}, u32[]{:S(2)}) collective-permute-start(f32[8,16,256]{2,1,0:T(8,128)S(1)} %shard_map.78), channel_id=1, source_target_pairs={{0,6},{2,4},{4,2},{6,0},{1,7},{3,5},{5,3},{7,1},{8,14},{10,12},{12... | collective-permute-start | bytes 393224 | tf_op jit(solution)/shard_map/ppermute | solution.py:481
  17.3 1.6 %shard_map.75 = (bf16[2,256,256]{2,1,0:T(8,128)(2,1)S(1)}, f32[8,2,16,128]{3,2,1,0:T(8,128)S(1)}, f32[8,256]{1,0:T(8,128)S(1)}) custom-call(bf16[2,256,256]{2,1,0:T(8,128)(2,1)S(1)} %get-tuple-element.19.first.refs_3_, f32[8,16,4096]{2,1,0:T(8,128)} %bitcast.8, f32[8,256]{1,0:T(8,128)S(1)} %get-tuple-element.22.rim), custom_call_target="tpu_custom_call" | custom-call | flops 1000000 | bytes 1000000 | tf_op jit(solution)/shard_map/pallas_call | solution.py:507
  18.9 3.2 %collective-permute-done.3.arrived = f32[8,16,256]{2,1,0:T(8,128)S(1)} collective-permute-done((f32[8,16,256]{2,1,0:T(8,128)S(1)}, f32[8,16,256]{2,1,0:T(8,128)S(1)}, u32[]{:S(2)}, u32[]{:S(2)}) %collective-permute-start.3) | collective-permute-done | bytes 131104 | tf_op jit(solution)/shard_map/ppermute | solution.py:481
  22.1 2.9 %all-to-all-done.spectra = f32[8,64,128]{2,1,0:T(8,128)S(1)} async-done(((f32[8,64,128]{2,1,0:T(8,128)}), f32[8,64,128]{2,1,0:T(8,128)S(1)}, u32[]{:S(2)}, u32[]{:S(2)}) %all-to-all-start) | async-done | bytes 262176 | tf_op jit(solution)/shard_map/all_to_all | solution.py:515
  25.0 0.3 shard_map.80
  25.2 12.2 %all_to_all.10.spectra = f32[8,64,128]{2,1,0:T(8,128)S(1)} all-to-all(f32[8,64,128]{2,1,0:T(8,128)S(1)} %shard_map.80), channel_id=1, replica_groups=mesh['blk'=4,'acc'=4,'tail'=2] {'blk','tail'}, dimensions={0} | all-to-all | bytes 524288 | tf_op jit(solution)/shard_map/all_to_all | solution.py:517
  37.4 0.9 %shard_map.81 = (f32[1,256,128]{2,1,0:T(8,128)S(1)}, bf16[2,256,512]{2,1,0:T(8,128)(2,1)S(1)}) custom-call(f32[8,64,128]{2,1,0:T(8,128)S(1)} %all_to_all.10.spectra, bf16[2,256,256]{2,1,0:T(8,128)(2,1)S(1)} %get-tuple-element.23.last, f32[2,128,512]{2,1,0:T(8,128)S(1)} %get-tuple-element.26.twist, bf16[2,512,512]{2,1,0:T(8,128)(2,1)S(1)} %get-tuple-element.27.second), custom_call_target="tpu_custom_call" | custom-call | flops 1000000 | bytes 1000000 | tf_op jit(solution)/shard_map/pallas_call | solution.py:520
  38.3 0.1 collective-permute-start.5
  38.4 0.3 shard_map.82
  38.8 1.0 %collective-permute-done.5 = f32[1,256,128]{2,1,0:T(8,128)S(1)} collective-permute-done((f32[1,256,128]{2,1,0:T(8,128)S(1)}, f32[1,256,128]{2,1,0:T(8,128)S(1)}, u32[]{:S(2)}, u32[]{:S(2)}) %collective-permute-start.5) | collective-permute-done | bytes 131104 | tf_op jit(solution)/shard_map/ppermute | solution.py:481
  39.8 0.2 collective-permute-start.4
  40.0 1.3 %collective-permute-start.6 = (f32[1,256,128]{2,1,0:T(8,128)S(1)}, f32[1,256,128]{2,1,0:T(8,128)S(1)}, u32[]{:S(2)}, u32[]{:S(2)}) collective-permute-start(f32[1,256,128]{2,1,0:T(8,128)S(1)} %get-tuple-element.33), channel_id=1, source_target_pairs={{0,4},{2,6},{4,0},{6,2},{1,5},{3,7},{5,1},{7,3},{8,12},{10,14},{12... | collective-permute-start | bytes 393224 | tf_op jit(solution)/shard_map/ppermute | solution.py:481
  41.3 4.5 %collective-permute-done.6 = f32[1,256,128]{2,1,0:T(8,128)S(1)} collective-permute-done((f32[1,256,128]{2,1,0:T(8,128)S(1)}, f32[1,256,128]{2,1,0:T(8,128)S(1)}, u32[]{:S(2)}, u32[]{:S(2)}) %collective-permute-start.6) | collective-permute-done | bytes 131104 | tf_op jit(solution)/shard_map/ppermute | solution.py:481
  45.8 0.7 %bitcast_add_fusion = f32[256,128]{1,0:T(8,128)} fusion(f32[256,128]{1,0:T(8,128)S(1)} %fusion, f32[1,256,128]{2,1,0:T(8,128)S(1)} %collective-permute-done.6), kind=kLoop, calls=%fused_computation.3 | loop fusion | flops 32768 | bytes 393216 | tf_op jit(solution)/shard_map/add | solution.py:534
  (6 shorter events, 0.1 us)
Async XLA Ops:
  0.0 6.7 %collective-permute-start = (f32[256,128]{1,0:T(8,128)}, f32[256,128]{1,0:T(8,128)S(1)}, u32[]{:S(2)}, u32[]{:S(2)}) collective-permute-start(f32[256,128]{1,0:T(8,128)} %bitcast.9), channel_id=1, source_target_pairs={{0,4},{2,6},{4,0},{6,2},{1,5},{3,7},{5,1},{7,3},{8,12},{10,14},{12... | collective-permute-start | bytes 393224 | tf_op jit(solution)/shard_map/ppermute | solution.py:481
  5.1 1.6 %collective-permute-start.2 = (f32[272,128]{1,0:T(8,128)S(1)}, f32[272,128]{1,0:T(8,128)S(1)}, u32[]{:S(2)}, u32[]{:S(2)}) collective-permute-start(f32[272,128]{1,0:T(8,128)S(1)} %get-tuple-element.24), channel_id=1, source_target_pairs={{0,2},{2,0},{4,6},{6,4},{1,3},{3,1},{5,7},{7,5},{8,10},{10,8},{12,... | collective-permute-start | bytes 417800 | tf_op jit(solution)/shard_map/ppermute | solution.py:481
  6.7 1.3 %collective-permute-start.1 = (f32[256,128]{1,0:T(8,128)S(1)}, f32[256,128]{1,0:T(8,128)S(1)}, u32[]{:S(2)}, u32[]{:S(2)}) collective-permute-start(f32[256,128]{1,0:T(8,128)S(1)} %collective-permute-done.refs_2_), channel_id=1, source_target_pairs={{0,2},{2,0},{4,6},{6,4},{1,3},{3,1},{5,7},{7,5},{8,10},{10,8},{12,... | collective-permute-start | bytes 393224 | tf_op jit(solution)/shard_map/ppermute | solution.py:481
  9.6 15.3 %all-to-all-start = ((f32[8,64,128]{2,1,0:T(8,128)}), f32[8,64,128]{2,1,0:T(8,128)S(1)}, u32[]{:S(2)}, u32[]{:S(2)}) async-start(f32[8,64,128]{2,1,0:T(8,128)} %shard_map.77), calls=%async_computation | async-start | bytes 524288 | tf_op jit(solution)/shard_map/all_to_all | solution.py:515
  16.2 5.8 %collective-permute-start.3 = (f32[8,16,256]{2,1,0:T(8,128)S(1)}, f32[8,16,256]{2,1,0:T(8,128)S(1)}, u32[]{:S(2)}, u32[]{:S(2)}) collective-permute-start(f32[8,16,256]{2,1,0:T(8,128)S(1)} %shard_map.78), channel_id=1, source_target_pairs={{0,6},{2,4},{4,2},{6,0},{1,7},{3,5},{5,3},{7,1},{8,14},{10,12},{12... | collective-permute-start | bytes 393224 | tf_op jit(solution)/shard_map/ppermute | solution.py:481
  38.3 1.4 %collective-permute-start.5 = (f32[1,256,128]{2,1,0:T(8,128)S(1)}, f32[1,256,128]{2,1,0:T(8,128)S(1)}, u32[]{:S(2)}, u32[]{:S(2)}) collective-permute-start(f32[1,256,128]{2,1,0:T(8,128)S(1)} %get-tuple-element.32), channel_id=1, source_target_pairs={{0,2},{2,0},{4,6},{6,4},{1,3},{3,1},{5,7},{7,5},{8,10},{10,8},{12,... | collective-permute-start | bytes 393224 | tf_op jit(solution)/shard_map/ppermute | solution.py:481
  39.8 1.5 %collective-permute-start.4 = (f32[1,256,128]{2,1,0:T(8,128)S(1)}, f32[1,256,128]{2,1,0:T(8,128)S(1)}, u32[]{:S(2)}, u32[]{:S(2)}) collective-permute-start(f32[1,256,128]{2,1,0:T(8,128)S(1)} %get-tuple-element.34), channel_id=1, source_target_pairs={{0,2},{2,0},{4,6},{6,4},{1,3},{3,1},{5,7},{7,5},{8,10},{10,8},{12,... | collective-permute-start | bytes 393224 | tf_op jit(solution)/shard_map/ppermute | solution.py:481
  40.0 5.8 %collective-permute-start.6 = (f32[1,256,128]{2,1,0:T(8,128)S(1)}, f32[1,256,128]{2,1,0:T(8,128)S(1)}, u32[]{:S(2)}, u32[]{:S(2)}) collective-permute-start(f32[1,256,128]{2,1,0:T(8,128)S(1)} %get-tuple-element.33), channel_id=1, source_target_pairs={{0,4},{2,6},{4,0},{6,2},{1,5},{3,7},{5,1},{7,3},{8,12},{10,14},{12... | collective-permute-start | bytes 393224 | tf_op jit(solution)/shard_map/ppermute | solution.py:481
